TPU v7x, 32 devices: a whole 2x2x4 slice. The times are simulated.
32 devices in a mesh: expert: 16 (over z, y, x), context: 2 (over core).
Axes of the slice: x: 2, y: 2, z: 4, core: 2. Of those that a mesh axis runs over, the one named last changes fastest.
Arguments:
- tokens: bfloat16 [4096, 2048], P(('expert', 'context')), may hold values from -6 to 6
- routes: int32 [4096, 8], P(('expert', 'context')), may hold values from 0 to 31, all different within a row; in each aligned block of 128 rows (0 to 127, 128 to 255, ...) at most 40 rows name the same one
- documents: int32 [16, 256], P('expert'), may hold values from 0 to 3, never falling along the last dimension, each value on 1 to 128 neighbouring positions
- w_query: bfloat16 [2048, 4096], P(('expert', 'context')), may hold values from -0.125 to 0.125
- key_projection: bfloat16 [2048, 512], P(('expert', 'context')), may hold values from -0.125 to 0.125
- value_projection: bfloat16 [2048, 512], P(('expert', 'context')), may hold values from -0.125 to 0.125
- w_out: bfloat16 [4096, 2048], P(('expert', 'context')), may hold values from -0.75 to 0.75
- w_router: bfloat16 [2048, 32], P(('expert', 'context')), may hold values from -0.25 to 0.25
- gain_attn: bfloat16 [2048], P(('expert', 'context')), may hold values from 0.099609375 to 1.8984375
- gain_ffn: bfloat16 [2048], P(('expert', 'context')), may hold values from 0.099609375 to 1.8984375
- gain_query: bfloat16 [128], P(('expert', 'context')), may hold values from 0.099609375 to 1.8984375
- gain_key: bfloat16 [128], P(('expert', 'context')), may hold values from 0.099609375 to 1.8984375
- w_gate: bfloat16 [32, 2048, 768], P('expert', None, 'context'), may hold values from -0.125 to 0.125
- w_up: bfloat16 [32, 2048, 768], P('expert', None, 'context'), may hold values from -0.125 to 0.125
- w_down: bfloat16 [32, 768, 2048], P('expert', 'context'), may hold values from -0.875 to 0.875
- cotangent: bfloat16 [4096, 2048], P(('expert', 'context')), may hold values from -6 to 6
Outputs:
- block_out: bfloat16 [4096, 2048], P(('expert', 'context'))
- grad_tokens: float32 [4096, 2048], P(('expert', 'context'))
- grad_query: float32 [2048, 4096], P(('expert', 'context'))
- grad_key: float32 [2048, 512], P(('expert', 'context'))
- grad_value: float32 [2048, 512], P(('expert', 'context'))
- grad_out: float32 [4096, 2048], P(('expert', 'context'))
- grad_router: float32 [2048, 32], P(('expert', 'context'))
- grad_gain_attn: float32 [2048], P(('expert', 'context'))
- grad_gain_ffn: float32 [2048], P(('expert', 'context'))
- grad_gain_query: float32 [128], P(('expert', 'context'))
- grad_gain_key: float32 [128], P(('expert', 'context'))
- grad_gate: float32 [32, 2048, 768], P('expert', None, 'context')
- grad_up: float32 [32, 2048, 768], P('expert', None, 'context')
- grad_down: float32 [32, 768, 2048], P('expert', 'context')
Inputs may be any that keep to these rules, and one draw needn't show every extreme that they name: `routes`: each row names 8 different experts; among the 128 rows of one device no expert is named more than 40 times, a bound that some block reaches. `documents`: document numbers never fall along a sequence; each document holds at most 128 positions, and one exactly that many.
All inputs are finite; a program needn't handle non-finite values.
Results may differ from a plain program's by a relative error of at most 0.025.
Values may be sent and summed in bfloat16 or wider, within the bound.
A program may use at most 320 MiB of HBM per device.

v0:
```python
import math

import jax
import jax.numpy as jnp
from jax import lax
from jax.sharding import PartitionSpec as P

MODEL_WIDTH = 2048
QUERY_HEADS = 32
KEY_VALUE_HEADS = 4
HEAD_SIZE = 128
TOP = 8
EXP_DEV = 2
DEVICE_TOKENS = 128


epsilon = 1e-06
rope_base = 1000000.0


def norm_parts(values_in, gain_vec):
    inverse = lax.rsqrt(jnp.mean(values_in * values_in, axis=-1, keepdims=True) + epsilon)
    return (values_in * inverse * gain_vec, inverse)


def norm_back(values_in, inverse, gain_vec, grad_out):
    scaled = grad_out * gain_vec
    grad_in = inverse * (
        scaled
        - values_in * inverse * inverse * jnp.mean(scaled * values_in, axis=-1, keepdims=True)
    )
    return (grad_in, grad_out * values_in * inverse)


def rope_tables(positions):
    exponent = jnp.arange(HEAD_SIZE // 2).astype(jnp.float32) * (2.0 / HEAD_SIZE)
    frequency = jnp.exp(-math.log(rope_base) * exponent)
    angles = positions.astype(jnp.float32)[:, None] * frequency[None, :]
    return (jnp.cos(angles), jnp.sin(angles))


def apply_rotary(values_in, cosine_table, sine_table):
    half_width = values_in.shape[-1] // 2
    first_half = values_in[..., :half_width]
    second_half = values_in[..., half_width:]
    cos_wide = cosine_table[:, None, :]
    sin_wide = sine_table[:, None, :]
    return jnp.concatenate(
        [
            first_half * cos_wide - second_half * sin_wide,
            second_half * cos_wide + first_half * sin_wide,
        ],
        axis=-1,
    )


def apply_rotary_inverse(grad_out, cosine_table, sine_table):
    half_width = grad_out.shape[-1] // 2
    first_half = grad_out[..., :half_width]
    second_half = grad_out[..., half_width:]
    cos_wide = cosine_table[:, None, :]
    sin_wide = sine_table[:, None, :]
    return jnp.concatenate(
        [
            first_half * cos_wide + second_half * sin_wide,
            second_half * cos_wide - first_half * sin_wide,
        ],
        axis=-1,
    )


def local(
    tokens,
    routes,
    documents,
    w_query,
    key_projection,
    value_projection,
    w_out,
    w_router,
    gain_attn,
    gain_ffn,
    gain_query,
    gain_key,
    w_gate,
    w_up,
    w_down,
    cotangent,
):
    (
        query_weight,
        key_weight,
        value_weight,
        out_weight,
        router_weight,
        attn_gain,
        ffn_gain,
        query_gain,
        key_gain,
    ) = (
        lax.all_gather(w_query, ("expert", "context"), axis=0, tiled=True),
        lax.all_gather(key_projection, ("expert", "context"), axis=0, tiled=True),
        lax.all_gather(value_projection, ("expert", "context"), axis=0, tiled=True),
        lax.all_gather(w_out, ("expert", "context"), axis=0, tiled=True),
        lax.all_gather(w_router, ("expert", "context"), axis=0, tiled=True),
        lax.all_gather(gain_attn, ("expert", "context"), axis=0, tiled=True),
        lax.all_gather(gain_ffn, ("expert", "context"), axis=0, tiled=True),
        lax.all_gather(gain_query, ("expert", "context"), axis=0, tiled=True),
        lax.all_gather(gain_key, ("expert", "context"), axis=0, tiled=True),
    )
    attn_gain = attn_gain.astype(jnp.float32)
    ffn_gain = ffn_gain.astype(jnp.float32)
    query_gain = query_gain.astype(jnp.float32)
    key_gain = key_gain.astype(jnp.float32)
    experts_all = router_weight.shape[1]
    capacity = DEVICE_TOKENS * TOP * 5 // (4 * experts_all)
    sequence_length = DEVICE_TOKENS * lax.axis_size("context")
    query_group_width = QUERY_HEADS // KEY_VALUE_HEADS
    score_scale = HEAD_SIZE ** (-0.5)
    offset = lax.axis_index("context") * DEVICE_TOKENS
    places = offset + jnp.arange(DEVICE_TOKENS, dtype=jnp.int32)
    cosine_table, sine_table = rope_tables(places)
    inputs = tokens.astype(jnp.float32)
    normed_attn, inverse_attn = norm_parts(inputs, attn_gain)
    first_in = normed_attn.astype(jnp.bfloat16)
    query_raw = jnp.dot(first_in, query_weight, preferred_element_type=jnp.float32).reshape(
        DEVICE_TOKENS, QUERY_HEADS, HEAD_SIZE
    )
    unnormed_key = jnp.dot(first_in, key_weight, preferred_element_type=jnp.float32).reshape(
        DEVICE_TOKENS, KEY_VALUE_HEADS, HEAD_SIZE
    )
    value_low = jnp.dot(first_in, value_weight, preferred_element_type=jnp.float32).astype(
        jnp.bfloat16
    )
    query_normed, query_inverse = norm_parts(query_raw, query_gain)
    query_rows = (
        apply_rotary(query_normed, cosine_table, sine_table)
        .astype(jnp.bfloat16)
        .reshape(DEVICE_TOKENS, KEY_VALUE_HEADS, query_group_width, HEAD_SIZE)
    )
    normalized_key, key_inverse = norm_parts(unnormed_key, key_gain)
    local_keys = (
        apply_rotary(normalized_key, cosine_table, sine_table)
        .astype(jnp.bfloat16)
        .reshape(DEVICE_TOKENS, KEY_VALUE_HEADS * HEAD_SIZE)
    )
    gathered_keys, gathered_values = (
        lax.all_gather(local_keys, "context", axis=0, tiled=True),
        lax.all_gather(value_low, "context", axis=0, tiled=True),
    )
    key_per_head = gathered_keys.reshape(sequence_length, KEY_VALUE_HEADS, HEAD_SIZE)
    value_per_head = gathered_values.reshape(sequence_length, KEY_VALUE_HEADS, HEAD_SIZE)
    doc_keys = documents[0]
    doc_queries = lax.dynamic_slice_in_dim(doc_keys, offset, DEVICE_TOKENS)
    allowed = (places[:, None] >= jnp.arange(sequence_length, dtype=jnp.int32)[None, :]) & (
        doc_queries[:, None] == doc_keys[None, :]
    )

    def score_block():
        raw_scores = (
            jnp.einsum(
                "qhrd,khd->hrqk", query_rows, key_per_head, preferred_element_type=jnp.float32
            )
            * score_scale
        )
        return jnp.where(allowed, raw_scores, -1e30)

    scores = score_block()
    highest_score = jnp.max(scores, axis=-1, keepdims=True)
    log_total = highest_score + jnp.log(
        jnp.sum(jnp.exp(scores - highest_score), axis=-1, keepdims=True)
    )
    weights = jnp.exp(scores - log_total).astype(jnp.bfloat16)
    attended = (
        jnp.einsum("hrqk,khd->qhrd", weights, value_per_head, preferred_element_type=jnp.float32)
        .reshape(DEVICE_TOKENS, QUERY_HEADS * HEAD_SIZE)
        .astype(jnp.bfloat16)
    )
    middle = inputs + jnp.dot(attended, out_weight, preferred_element_type=jnp.float32)
    normed_ffn, inverse_ffn = norm_parts(middle, ffn_gain)
    second_in = normed_ffn.astype(jnp.bfloat16)
    logits = jnp.dot(second_in, router_weight, preferred_element_type=jnp.float32)
    expert_ids = jnp.arange(experts_all, dtype=jnp.int32)
    picked = routes[:, :, None] == expert_ids[None, None, :]
    chosen_logits = jnp.sum(jnp.where(picked, logits[:, None, :], 0.0), axis=-1)
    route_weights = jax.nn.softmax(chosen_logits, axis=-1)
    flat_routes = routes.reshape(-1)
    route_marks = (flat_routes[:, None] == expert_ids[None, :]).astype(jnp.int32)
    route_ranks = jnp.sum((jnp.cumsum(route_marks, axis=0) - 1) * route_marks, axis=1)
    targets = flat_routes * capacity + route_ranks
    pair_count = DEVICE_TOKENS * TOP
    sources = (
        jnp.full((experts_all * capacity,), pair_count, jnp.int32)
        .at[targets]
        .set(jnp.arange(pair_count, dtype=jnp.int32))
    )
    filled = sources < pair_count
    source_pairs = jnp.where(filled, sources, 0)
    source_tokens = source_pairs // TOP
    outgoing = jnp.where(filled[:, None], second_in[source_tokens], jnp.zeros((), jnp.bfloat16))
    incoming = lax.all_to_all(outgoing, "expert", split_axis=0, concat_axis=0, tiled=True)
    rows_in = lax.all_gather(incoming, "context", axis=0, tiled=True).reshape(
        -1, EXP_DEV, capacity, MODEL_WIDTH
    )
    gate_use, up_use, down_use = (w_gate, w_up, w_down)
    gate_value = jnp.einsum("secd,edf->secf", rows_in, gate_use, preferred_element_type=jnp.float32)
    up_value = jnp.einsum("secd,edf->secf", rows_in, up_use, preferred_element_type=jnp.float32)
    sigmoid_gate = jax.nn.sigmoid(gate_value)
    activation = (gate_value * sigmoid_gate * up_value).astype(jnp.bfloat16)
    partial_out = jnp.einsum(
        "secf,efd->secd", activation, down_use, preferred_element_type=jnp.float32
    ).reshape(-1, MODEL_WIDTH)
    expert_rows = lax.psum_scatter(
        partial_out.astype(jnp.bfloat16), "context", scatter_dimension=0, tiled=True
    )
    returned = lax.all_to_all(expert_rows, "expert", split_axis=0, concat_axis=0, tiled=True)
    route_out = returned[targets].reshape(DEVICE_TOKENS, TOP, MODEL_WIDTH)
    result = middle + jnp.sum(route_weights[:, :, None] * route_out, axis=1)
    block_out = result.astype(jnp.bfloat16)
    grad_result = cotangent.astype(jnp.float32)
    grad_route_weights = jnp.sum(grad_result[:, None, :] * route_out, axis=-1)
    grad_chosen = route_weights * (
        grad_route_weights - jnp.sum(route_weights * grad_route_weights, axis=-1, keepdims=True)
    )
    grad_logits = jnp.sum(jnp.where(picked, grad_chosen[:, :, None], 0.0), axis=1).astype(
        jnp.bfloat16
    )
    router_grad = jnp.dot(second_in.T, grad_logits, preferred_element_type=jnp.float32)
    grad_second = jnp.dot(grad_logits, router_weight.T, preferred_element_type=jnp.float32)
    pair_weights = route_weights.reshape(-1)[source_pairs]
    grad_outgoing = jnp.where(
        filled[:, None], pair_weights[:, None] * grad_result[source_tokens], 0.0
    ).astype(jnp.bfloat16)
    grad_incoming = lax.all_to_all(grad_outgoing, "expert", split_axis=0, concat_axis=0, tiled=True)
    grad_rows = lax.all_gather(grad_incoming, "context", axis=0, tiled=True).reshape(
        -1, EXP_DEV, capacity, MODEL_WIDTH
    )
    grad_act = jnp.einsum("secd,efd->secf", grad_rows, down_use, preferred_element_type=jnp.float32)
    grad_gate_v = (
        grad_act * up_value * sigmoid_gate * (1.0 + gate_value * (1.0 - sigmoid_gate))
    ).astype(jnp.bfloat16)
    grad_up_v = (grad_act * gate_value * sigmoid_gate).astype(jnp.bfloat16)
    down_grad = jnp.einsum(
        "secf,secd->efd", activation, grad_rows, preferred_element_type=jnp.float32
    )
    gate_grad = jnp.einsum(
        "secd,secf->edf", rows_in, grad_gate_v, preferred_element_type=jnp.float32
    )
    up_grad = jnp.einsum("secd,secf->edf", rows_in, grad_up_v, preferred_element_type=jnp.float32)
    grad_rows_in = jnp.einsum(
        "secf,edf->secd", grad_gate_v, gate_use, preferred_element_type=jnp.float32
    )
    grad_rows_in = (
        grad_rows_in
        + jnp.einsum("secf,edf->secd", grad_up_v, up_use, preferred_element_type=jnp.float32)
    ).reshape(-1, MODEL_WIDTH)
    grad_expert_rows = lax.psum_scatter(
        grad_rows_in.astype(jnp.bfloat16), "context", scatter_dimension=0, tiled=True
    )
    grad_returned = lax.all_to_all(
        grad_expert_rows, "expert", split_axis=0, concat_axis=0, tiled=True
    )
    grad_second = grad_second + jnp.sum(
        grad_returned[targets].reshape(DEVICE_TOKENS, TOP, MODEL_WIDTH).astype(jnp.float32), axis=1
    )
    grad_middle_norm, ffn_terms = norm_back(middle, inverse_ffn, ffn_gain, grad_second)
    ffn_gain_grad = jnp.sum(ffn_terms, axis=0)
    grad_middle = grad_result + grad_middle_norm
    grad_attn = grad_middle.astype(jnp.bfloat16)
    out_grad = jnp.dot(attended.T, grad_attn, preferred_element_type=jnp.float32)
    grad_attended = (
        jnp.dot(grad_attn, out_weight.T, preferred_element_type=jnp.float32)
        .astype(jnp.bfloat16)
        .reshape(DEVICE_TOKENS, KEY_VALUE_HEADS, query_group_width, HEAD_SIZE)
    )
    probabilities = jnp.exp(score_block() - log_total)
    grad_probs = jnp.einsum(
        "qhrd,khd->hrqk", grad_attended, value_per_head, preferred_element_type=jnp.float32
    )
    grad_scores = (
        probabilities * (grad_probs - jnp.sum(probabilities * grad_probs, axis=-1, keepdims=True))
    ).astype(jnp.bfloat16)
    grad_queries = (
        jnp.einsum("hrqk,khd->qhrd", grad_scores, key_per_head, preferred_element_type=jnp.float32)
        * score_scale
    )
    key_gradients = (
        jnp.einsum("hrqk,qhrd->khd", grad_scores, query_rows, preferred_element_type=jnp.float32)
        * score_scale
    )
    value_gradients = jnp.einsum(
        "hrqk,qhrd->khd",
        probabilities.astype(jnp.bfloat16),
        grad_attended,
        preferred_element_type=jnp.float32,
    )
    local_key_gradient, values_grad_own = (
        lax.psum_scatter(
            key_gradients.reshape(sequence_length, KEY_VALUE_HEADS * HEAD_SIZE).astype(
                jnp.bfloat16
            ),
            "context",
            scatter_dimension=0,
            tiled=True,
        ).astype(jnp.float32),
        lax.psum_scatter(
            value_gradients.reshape(sequence_length, KEY_VALUE_HEADS * HEAD_SIZE).astype(
                jnp.bfloat16
            ),
            "context",
            scatter_dimension=0,
            tiled=True,
        ).astype(jnp.float32),
    )
    grad_query_raw, query_terms = norm_back(
        query_raw,
        query_inverse,
        query_gain,
        apply_rotary_inverse(
            grad_queries.reshape(DEVICE_TOKENS, QUERY_HEADS, HEAD_SIZE), cosine_table, sine_table
        ),
    )
    query_gain_grad = jnp.sum(query_terms, axis=(0, 1))
    key_gradient_unnormed, key_terms = norm_back(
        unnormed_key,
        key_inverse,
        key_gain,
        apply_rotary_inverse(
            local_key_gradient.reshape(DEVICE_TOKENS, KEY_VALUE_HEADS, HEAD_SIZE),
            cosine_table,
            sine_table,
        ),
    )
    key_gain_grad = jnp.sum(key_terms, axis=(0, 1))
    grad_query_low = grad_query_raw.reshape(DEVICE_TOKENS, QUERY_HEADS * HEAD_SIZE).astype(
        jnp.bfloat16
    )
    key_gradient_narrow = key_gradient_unnormed.reshape(
        DEVICE_TOKENS, KEY_VALUE_HEADS * HEAD_SIZE
    ).astype(jnp.bfloat16)
    grad_value_low = values_grad_own.astype(jnp.bfloat16)
    grad_first = jnp.dot(grad_query_low, query_weight.T, preferred_element_type=jnp.float32)
    grad_first = grad_first + jnp.dot(
        key_gradient_narrow, key_weight.T, preferred_element_type=jnp.float32
    )
    grad_first = grad_first + jnp.dot(
        grad_value_low, value_weight.T, preferred_element_type=jnp.float32
    )
    query_grad = jnp.dot(first_in.T, grad_query_low, preferred_element_type=jnp.float32)
    key_grad = jnp.dot(first_in.T, key_gradient_narrow, preferred_element_type=jnp.float32)
    value_grad = jnp.dot(first_in.T, grad_value_low, preferred_element_type=jnp.float32)
    grad_input_norm, attn_terms = norm_back(inputs, inverse_attn, attn_gain, grad_first)
    attn_gain_grad = jnp.sum(attn_terms, axis=0)
    grad_tokens = grad_middle + grad_input_norm
    (
        query_grad,
        key_grad,
        value_grad,
        out_grad,
        router_grad,
        attn_gain_grad,
        ffn_gain_grad,
        query_gain_grad,
        key_gain_grad,
    ) = (
        lax.psum_scatter(query_grad, ("expert", "context"), scatter_dimension=0, tiled=True),
        lax.psum_scatter(key_grad, ("expert", "context"), scatter_dimension=0, tiled=True),
        lax.psum_scatter(value_grad, ("expert", "context"), scatter_dimension=0, tiled=True),
        lax.psum_scatter(out_grad, ("expert", "context"), scatter_dimension=0, tiled=True),
        lax.psum_scatter(router_grad, ("expert", "context"), scatter_dimension=0, tiled=True),
        lax.psum_scatter(attn_gain_grad, ("expert", "context"), scatter_dimension=0, tiled=True),
        lax.psum_scatter(ffn_gain_grad, ("expert", "context"), scatter_dimension=0, tiled=True),
        lax.psum_scatter(query_gain_grad, ("expert", "context"), scatter_dimension=0, tiled=True),
        lax.psum_scatter(key_gain_grad, ("expert", "context"), scatter_dimension=0, tiled=True),
    )
    return (
        block_out,
        grad_tokens,
        query_grad,
        key_grad,
        value_grad,
        out_grad,
        router_grad,
        attn_gain_grad,
        ffn_gain_grad,
        query_gain_grad,
        key_gain_grad,
        gate_grad,
        up_grad,
        down_grad,
    )


def solution(mesh):
    return jax.shard_map(
        local,
        mesh=mesh,
        in_specs=(
            P(("expert", "context"), None),
            P(("expert", "context"), None),
            P("expert", None),
            P(("expert", "context"), None),
            P(("expert", "context"), None),
            P(("expert", "context"), None),
            P(("expert", "context"), None),
            P(("expert", "context"), None),
            P(("expert", "context")),
            P(("expert", "context")),
            P(("expert", "context")),
            P(("expert", "context")),
            P("expert", None, "context"),
            P("expert", None, "context"),
            P("expert", "context", None),
            P(("expert", "context"), None),
        ),
        out_specs=(
            P(("expert", "context"), None),
            P(("expert", "context"), None),
            P(("expert", "context"), None),
            P(("expert", "context"), None),
            P(("expert", "context"), None),
            P(("expert", "context"), None),
            P(("expert", "context"), None),
            P(("expert", "context")),
            P(("expert", "context")),
            P(("expert", "context")),
            P(("expert", "context")),
            P("expert", None, "context"),
            P("expert", None, "context"),
            P("expert", "context", None),
        ),
        check_vma=False,
    )
```

profile of v0, /device:TPU:13, one launch (start us, length us, event | category | flops | bytes accessed | tf_op | source)
XLA Modules:
  0.0 2238.3 jit_solution(7838859988790446009)
XLA Ops:
  14.4 39.7 %all-reduce.9 = (bf16[2048]{0:T(1024)(128)(2,1)S(1)}, bf16[128]{0:T(256)(128)(2,1)S(1)}, bf16[128]{0:T(256)(128)(2,1)S(1)}, bf16[2048]{0:T(1024)(128)(2,1)S(1)}) all-reduce(bf16[2048]{0:T(1024)(128)(2,1)S(1)} %dynamic-update-slice, bf16[128]{0:T(256)(128)(2,1)S(1)} %dynamic-update-slice.1, ...), channel_id=1, replica_groups=mesh['expert'=16,'context'=2] {'expert','context'}, use_global_device_ids=true, to_apply=%add | all-reduce | flops 4352 | bytes 17408
  56.0 9.0 reduce-window.6
  82.2 43.6 %all-gather.10.cloned.1.call-done = bf16[2048,512]{1,0:T(8,128)(2,1)} async-done(((bf16[64,512]{1,0:T(8,128)(2,1)}), bf16[2048,512]{1,0:T(8,128)(2,1)}) %all-gather.10.cloned.1.call-update) | async-done | bytes 2097168 | tf_op jit(solution)/shard_map/all_gather | solution.py:102
  138.1 104.0 %all-gather.12.cloned.1.call-done = bf16[2048,4096]{1,0:T(8,128)(2,1)} async-done(((bf16[64,4096]{1,0:T(8,128)(2,1)}), bf16[2048,4096]{1,0:T(8,128)(2,1)}) %all-gather.12.cloned.1.call-update) | async-done | bytes 16777232 | tf_op jit(solution)/shard_map/all_gather | solution.py:101
  242.0 8.4 fusion.95
  262.0 95.3 %all-gather.14.cloned.1.call-done = bf16[4096,2048]{1,0:T(8,128)(2,1)} async-done(((bf16[128,2048]{1,0:T(8,128)(2,1)}), bf16[4096,2048]{1,0:T(8,128)(2,1)}) %all-gather.14.cloned.1.call-update) | async-done | bytes 16777232 | tf_op jit(solution)/shard_map/all_gather | solution.py:104
  357.3 8.6 multiply_reduce_fusion.4
  367.9 11.9 gather_fusion
  379.8 5.3 broadcast_select_fusion
  385.1 5.6 all-to-all-start
  390.7 142.4 %all-gather = bf16[32,64,32]{1,2,0:T(8,128)(2,1)S(1)} all-gather(bf16[1,64,32]{1,2,0:T(8,128)(2,1)S(1)} %bitcast.301), channel_id=1, replica_groups=mesh['expert'=16,'context'=2] {'expert','context'}, dimensions={0}, use_global_device_ids=true | all-gather | bytes 135168 | tf_op jit(solution)/shard_map/all_gather | solution.py:105
  535.6 12.1 gather_fusion.3
  549.3 5.0 gather_fusion.2
  554.4 4.9 select_convert_fusion
  559.4 121.4 %all_to_all.42 = bf16[16,80,2048]{2,1,0:T(8,128)(2,1)} all-to-all(bf16[16,80,2048]{2,1,0:T(8,128)(2,1)S(1)} %select_convert_fusion), channel_id=1, replica_groups=mesh['expert'=16,'context'=2] {'expert'}, dimensions={0} | all-to-all | bytes 10485760 | tf_op jit(solution)/shard_map/all_to_all | solution.py:234
  680.9 10.7 fusion.5
  692.6 7.7 fusion.7
  704.3 12.3 fusion.18
  717.9 8.5 convert_bitcast_fusion
  726.4 10.1 copy.158
  738.1 16.5 fusion.30
  754.5 14.0 fusion
  768.5 10.1 copy.163
  778.6 6.4 all-to-all-start.1
  785.0 12.9 reduce-scatter.18.cloned.1.call-done
  797.9 105.0 %all-to-all-done.1 = bf16[16,80,2048]{2,1,0:T(8,128)(2,1)} async-done(((bf16[16,80,2048]{2,1,0:T(8,128)(2,1)}), bf16[16,80,2048]{2,1,0:T(8,128)(2,1)}, u32[]{:S(2)}, u32[]{:S(2)}) %all-to-all-start.1) | async-done | bytes 5242912 | tf_op jit(solution)/shard_map/all_to_all | solution.py:216
  903.0 6.4 all-to-all-start.3
  912.5 12.1 gather_fusion.1
  924.6 4.9 fusion.10
  929.6 96.4 %all-to-all-done.3 = bf16[16,80,2048]{2,1,0:T(8,128)(2,1)} async-done(((bf16[16,80,2048]{2,1,0:T(8,128)(2,1)}), bf16[16,80,2048]{2,1,0:T(8,128)(2,1)}, u32[]{:S(2)}, u32[]{:S(2)}) %all-to-all-start.3) | async-done | bytes 5242912 | tf_op jit(solution)/shard_map/all_to_all | solution.py:260
  1026.0 12.0 gather_fusion.4
  1037.9 5.1 convert_reduce_fusion
  1045.4 11.8 fusion.44
  1057.6 5.7 fusion.11
  1065.2 4.9 fusion.13
  1077.6 7.3 reduce-scatter.28.cloned.1.call-done
  1096.5 17.2 fusion.67
  1126.9 6.6 fusion.41
  1134.4 13.3 fusion.93
  1149.2 11.2 fusion.24
  1160.4 10.2 convolution_bitcast_fusion
  1170.7 7.9 convolution_bitcast_fusion.1
  1178.6 12.4 fusion.103
  1195.9 39.2 %all-reduce.8 = (f32[2048]{0:T(1024)S(1)}, f32[2048]{0:T(1024)S(1)}, f32[128]{0:T(128)S(1)}, f32[128]{0:T(128)S(1)}) all-reduce(f32[2048]{0:T(1024)S(1)} %get-tuple-element.18, f32[2048]{0:T(1024)S(1)} %copy-done.60, f32[128]{0:T(128)S(1)} %bitcast_reduce_fusion, ...), channel_id=11, replica_groups=mesh['expert'=16,'context'=2] {'expert','context'}, use_global_device_ids=true, to_apply=%region_33.34.clone | all-reduce | flops 4352 | bytes 34816
  1242.0 90.3 %reduce-scatter.24.cloned.1.call-done = f32[64,512]{1,0:T(8,128)} async-done(((f32[2048,512]{1,0:T(8,128)}), f32[64,512]{1,0:T(8,128)}) %reduce-scatter.24.cloned.1.call-update) | async-done | bytes 131088 | tf_op jit(solution)/shard_map/reduce_scatter | solution.py:368
  1332.3 141.5 %reduce-scatter.22.cloned.1.call-done = f32[64,512]{1,0:T(8,128)} async-done(((f32[2048,512]{1,0:T(8,128)}), f32[64,512]{1,0:T(8,128)}) %reduce-scatter.22.cloned.1.call-update) | async-done | bytes 131088 | tf_op jit(solution)/shard_map/reduce_scatter | solution.py:367
  1473.7 392.7 %reduce-scatter.26.cloned.1.call-done = f32[128,2048]{1,0:T(8,128)} async-done(((f32[4096,2048]{1,0:T(8,128)}), f32[128,2048]{1,0:T(8,128)}) %reduce-scatter.26.cloned.1.call-update) | async-done | bytes 1048592 | tf_op jit(solution)/shard_map/reduce_scatter | solution.py:369
  1866.5 364.9 %reduce-scatter.20.cloned.1.call-done = f32[64,4096]{1,0:T(8,128)} async-done(((f32[2048,4096]{1,0:T(8,128)}), f32[64,4096]{1,0:T(8,128)}) %reduce-scatter.20.cloned.1.call-update) | async-done | bytes 1048592 | tf_op jit(solution)/shard_map/reduce_scatter | solution.py:366
  (321 shorter events, 117.5 us)
Async XLA Ops:
  7.2 697.1 %copy-start = (bf16[2,384,2048]{2,1,0:T(8,128)(2,1)S(1)}, bf16[2,384,2048]{2,1,0:T(8,128)(2,1)}, u32[]{:S(2)}) copy-start(bf16[2,384,2048]{2,1,0:T(8,128)(2,1)} %param.30) | copy-start | bytes 9437188
  7.2 67.7 %all-gather.8.cloned.1.call-start = ((), (), s32[]{:S(2)}) async-start(), calls=%async_computation.13 | async-start | bytes 2162688 | tf_op jit(solution)/shard_map/all_gather | solution.py:103
  7.9 117.9 %all-gather.10.cloned.1.call-start = ((), (), s32[]{:S(2)}) async-start(), calls=%async_computation.14 | async-start | bytes 2162688 | tf_op jit(solution)/shard_map/all_gather | solution.py:102
  8.7 233.3 %all-gather.12.cloned.1.call-start = ((), (), s32[]{:S(2)}) async-start(), calls=%async_computation.15 | async-start | bytes 17301504 | tf_op jit(solution)/shard_map/all_gather | solution.py:101
  9.4 347.9 %all-gather.14.cloned.1.call-start = ((), (), s32[]{:S(2)}) async-start(), calls=%async_computation.16 | async-start | bytes 17301504 | tf_op jit(solution)/shard_map/all_gather | solution.py:104
  55.1 186.9 %copy-start.40 = (f32[2048]{0:T(1024)}, f32[2048]{0:T(1024)S(1)}, u32[]{:S(2)}) copy-start(f32[2048]{0:T(1024)S(1)} %convert_element_type.157) | copy-start | bytes 24580
  55.1 310.8 %copy-start.52 = (f32[2048]{0:T(1024)}, f32[2048]{0:T(1024)S(1)}, u32[]{:S(2)}) copy-start(f32[2048]{0:T(1024)S(1)} %convert_element_type.169) | copy-start | bytes 24580
  74.9 179.3 %copy-start.36 = (f32[128,64]{1,0:T(8,128)}, f32[128,64]{1,0:T(8,128)S(1)}, u32[]{:S(2)}) copy-start(f32[128,64]{1,0:T(8,128)S(1)} %get-tuple-element.55) | copy-start | bytes 98308
  74.9 179.3 %copy-start.38 = (f32[128,64]{1,0:T(8,128)}, f32[128,64]{1,0:T(8,128)S(1)}, u32[]{:S(2)}) copy-start(f32[128,64]{1,0:T(8,128)S(1)} %get-tuple-element.56) | copy-start | bytes 98308
  129.8 120.6 %copy-start.25 = (f32[128,4,128]{2,1,0:T(4,128)}, f32[128,4,128]{2,1,0:T(4,128)S(1)}, u32[]{:S(2)}) copy-start(f32[128,4,128]{2,1,0:T(4,128)S(1)} %reshape.408) | copy-start | bytes 786436
  357.3 10.5 copy-start.54
  365.9 13.9 copy-start.67
  367.8 11.9 copy-start.62
  385.1 150.5 %copy-start.55 = (s32[2048]{0:T(1024)S(1)}, s32[2048]{0:T(1024)}, u32[]{:S(2)}) copy-start(s32[2048]{0:T(1024)} %get-tuple-element.66) | copy-start | bytes 24580
  385.1 169.3 %all-to-all-start = ((bf16[16,80,2048]{2,1,0:T(8,128)(2,1)}), bf16[16,80,2048]{2,1,0:T(8,128)(2,1)}, u32[]{:S(2)}, u32[]{:S(2)}) async-start(bf16[16,80,2048]{2,1,0:T(8,128)(2,1)} %broadcast_select_fusion), calls=%async_computation | async-start | bytes 10485760 | tf_op jit(solution)/shard_map/all_to_all | solution.py:201
  390.7 290.2 %all-gather.16.cloned.1.call-start = ((), (), s32[]{:S(2)}) async-start(), calls=%async_computation.17 | async-start | bytes 15728640 | tf_op jit(solution)/shard_map/all_gather | solution.py:202
  535.6 13.4 copy-start.56
  535.6 13.7 copy-start.61
  554.4 149.9 %all-gather.18.cloned.1.call-start = ((), (), s32[]{:S(2)}) async-start(), calls=%async_computation.19 | async-start | bytes 15728640 | tf_op jit(solution)/shard_map/all_gather | solution.py:235
  680.8 97.8 %reduce-scatter.16.cloned.1.call-start = ((), (), s32[]{:S(2)}) async-start(), calls=%async_computation.18 | async-start | bytes 15728640 | tf_op jit(solution)/shard_map/reduce_scatter | solution.py:213
  680.9 10.7 copy-start.27
  680.9 11.7 copy-start.72
  736.6 61.4 %reduce-scatter.18.cloned.1.call-start = ((), (), s32[]{:S(2)}) async-start(), calls=%async_computation.20 | async-start | bytes 15728640 | tf_op jit(solution)/shard_map/reduce_scatter | solution.py:257
  778.6 124.4 %all-to-all-start.1 = ((bf16[16,80,2048]{2,1,0:T(8,128)(2,1)}), bf16[16,80,2048]{2,1,0:T(8,128)(2,1)}, u32[]{:S(2)}, u32[]{:S(2)}) async-start(bf16[16,80,2048]{2,1,0:T(8,128)(2,1)} %bitcast.284), calls=%async_computation.2 | async-start | bytes 10485760 | tf_op jit(solution)/shard_map/all_to_all | solution.py:216
  903.0 123.0 %all-to-all-start.3 = ((bf16[16,80,2048]{2,1,0:T(8,128)(2,1)}), bf16[16,80,2048]{2,1,0:T(8,128)(2,1)}, u32[]{:S(2)}, u32[]{:S(2)}) async-start(bf16[16,80,2048]{2,1,0:T(8,128)(2,1)} %bitcast.283), calls=%async_computation.5 | async-start | bytes 10485760 | tf_op jit(solution)/shard_map/all_to_all | solution.py:260
  909.4 164.3 %reduce-scatter.30.cloned.1.call-start = ((), (), s32[]{:S(2)}) async-start(), calls=%async_computation.26 | async-start | bytes 393216
  912.5 12.1 copy-start.2
  1045.4 11.8 copy-start.13
  1045.4 12.1 copy-start.32
  1045.4 12.1 copy-start.43
  1045.4 12.1 copy-start.51
  1064.7 20.2 reduce-scatter.28.cloned.1.call-start
  1072.2 165.3 %reduce-scatter.32.cloned.1.call-start = ((), (), s32[]{:S(2)}) async-start(), calls=%async_computation.27 | async-start | bytes 1081344
  1073.6 258.6 %reduce-scatter.24.cloned.1.call-start = ((), (), s32[]{:S(2)}) async-start(), calls=%async_computation.23 | async-start | bytes 4325376 | tf_op jit(solution)/shard_map/reduce_scatter | solution.py:368
  1077.5 12.0 copy-start.37
  1077.5 12.0 copy-start.39
  1077.5 13.1 copy-start.26
  1077.5 15.4 copy-start.30
  1077.6 16.1 copy-start.59
  1077.6 396.2 %reduce-scatter.22.cloned.1.call-start = ((), (), s32[]{:S(2)}) async-start(), calls=%async_computation.22 | async-start | bytes 4325376 | tf_op jit(solution)/shard_map/reduce_scatter | solution.py:367
  1096.4 770.0 %reduce-scatter.26.cloned.1.call-start = ((), (), s32[]{:S(2)}) async-start(), calls=%async_computation.24 | async-start | bytes 34603008 | tf_op jit(solution)/shard_map/reduce_scatter | solution.py:369
  1113.7 1117.6 %reduce-scatter.20.cloned.1.call-start = ((), (), s32[]{:S(2)}) async-start(), calls=%async_computation.21 | async-start | bytes 34603008 | tf_op jit(solution)/shard_map/reduce_scatter | solution.py:366
  1149.2 11.2 copy-start.35
  1149.2 21.4 slice-start
  1149.2 21.4 slice-start.1
  1178.6 12.5 copy-start.65
  1178.6 12.5 copy-start.45
  1191.1 1040.2 %copy-start.1 = (bf16[2,384,2048]{2,1,0:T(8,128)(2,1)S(1)}, bf16[2,384,2048]{2,1,0:T(8,128)(2,1)}, u32[]{:S(2)}) copy-start(bf16[2,384,2048]{2,1,0:T(8,128)(2,1)} %param.30) | copy-start | bytes 9437188
  (48 other events, 163.0 us)
Sparse Core Ops, SparseCore 0:
  10.9 56.8 all-gather.7
  70.7 55.0 all-gather.9
  128.7 113.3 all-gather.11
  244.7 112.5 all-gather.13
  554.5 24.1 all-gather.15
  680.9 23.3 all-gather.17
  736.7 19.1 reduce-scatter.15
  778.7 19.1 reduce-scatter.17
  1064.8 8.5 reduce-scatter.29
  1076.1 8.8 reduce-scatter.27
  1087.2 104.2 reduce-scatter.31
  1194.2 137.9 reduce-scatter.23
  1335.1 138.5 reduce-scatter.21
  1476.5 389.9 reduce-scatter.25
  1869.2 362.0 reduce-scatter.19
where the time goes:
time: 2250 us; the launch traced here: 2240 us
  waiting for transfers between devices  1460 us (65%)
  blocking collectives  351 us (16%)
  matrix products  202 us (9%)
  local copies, waits for them, and re-layouts  123 us (5%)
  other arithmetic  67.6 us (3%)
    reduce_scatter x1, waiting for transfers between devices, local(): lax.psum_scatter(out_grad, ('expert', 'context'), scatter_dimension=0, ti...  393 us
    reduce_scatter x1, waiting for transfers between devices, local(): lax.psum_scatter(query_grad, ('expert', 'context'), scatter_dimension=0,...  365 us
    all_gather x1, blocking collectives, local(): lax.all_gather(w_router, ('expert', 'context'), axis=0, tiled=True)  142 us
    reduce_scatter x1, waiting for transfers between devices, local(): lax.psum_scatter(key_grad, ('expert', 'context'), scatter_dimension=0, ti...  141 us
    all_to_all x1, blocking collectives, local(): lax.all_to_all(grad_outgoing, 'expert', split_axis=0, concat_axis=0, tile...  121 us
    all_to_all x1, waiting for transfers between devices, local(): lax.all_to_all(expert_rows, 'expert', split_axis=0, concat_axis=0, tiled=...  105 us
    all_gather x1, waiting for transfers between devices, local(): lax.all_gather(w_query, ('expert', 'context'), axis=0, tiled=True)  104 us
    all_to_all x1, waiting for transfers between devices, local(): lax.all_to_all(grad_expert_rows, 'expert', split_axis=0, concat_axis=0, t...  96.4 us
  transfers between devices with their start and end apart: 18, of which 12 were waited for; matrix products, arithmetic and copies ran while one was open for 13% of the time, Pallas kernels for 0%

commit v1 on v0

v1 whole, which is shorter than its diff:
```python
import functools
import math

import jax
import jax.numpy as jnp
from jax import lax
from jax.experimental import pallas as pl
from jax.experimental.pallas import tpu as pltpu
from jax.sharding import PartitionSpec as P

MESH_ID = pl.DeviceIdType.MESH
BF = jnp.bfloat16
F32 = jnp.float32


class Net:
    def __init__(self, n_expert):
        side = math.isqrt(n_expert // 4)
        self.dims = (4, side, side)
        self.chips = n_expert

    def enter(self):
        e = lax.axis_index("expert")
        _, A, B = self.dims
        self.e = e
        self.at = (e // (A * B), (e // B) % A, e % B)
        self.c = lax.axis_index("context")
        return self

    def chip(self, at):
        _, A, B = self.dims
        return (at[0] * A + at[1]) * B + at[2]

    def moved(self, axis, to):
        at = list(self.at)
        at[axis] = to
        return tuple(at)

    def near(self, axis):
        n, p = self.dims[axis], self.at[axis]
        if n == 2:
            return [(None, 1 - p)]
        return [(p < n - 1, p + 1), (p > 0, p - 1)]


def when(cond, fn):
    if cond is None:
        fn()
    else:
        pl.when(cond)(fn)


def rcopy(src, dst, ss, rs, dev):
    return pltpu.make_async_remote_copy(
        src_ref=src, dst_ref=dst, send_sem=ss, recv_sem=rs, device_id=dev, device_id_type=MESH_ID
    )


def greet(net, axes, partner=True):
    bar = pltpu.get_barrier_semaphore()
    count = 0
    for axis in axes:
        for cond, to in net.near(axis):
            dev = (net.chip(net.moved(axis, to)), net.c)
            when(cond, lambda dev=dev: pl.semaphore_signal(bar, inc=1, device_id=dev, device_id_type=MESH_ID))
            count = count + (1 if cond is None else jnp.where(cond, 1, 0))
    if partner:
        pl.semaphore_signal(bar, inc=1, device_id=(net.e, 1 - net.c), device_id_type=MESH_ID)
        count = count + 1
    pl.semaphore_wait(bar, count)


def greet_all(net):
    bar = pltpu.get_barrier_semaphore()
    total = net.chips * 2
    me = net.e * 2 + net.c

    def body(k, _):
        t = (me + k) % total
        pl.semaphore_signal(bar, inc=1, device_id=(t // 2, t % 2), device_id_type=MESH_ID)
        return 0

    lax.fori_loop(1, total, body, 0)
    pl.semaphore_wait(bar, total - 1)


def interleave(*gens):
    gens = list(gens)
    while gens:
        for g in list(gens):
            try:
                next(g)
            except StopIteration:
                gens.remove(g)


def ag_piece(net, order, block, rs, ss, done, partner=True):
    def send(cond, at, kind, dev):
        ch = net.chip(at)
        mk = lambda: rcopy(block(ch, net.c), block(ch, net.c), ss(ch, kind), rs(ch, net.c), dev)
        when(cond, lambda: mk().start())
        return lambda: when(cond, lambda: mk().wait_send())

    def spread(at, stage):
        outs = []
        for i in range(stage, len(order)):
            axis = order[i]
            for k, (cond, to) in enumerate(net.near(axis)):
                outs.append(send(cond, at, 2 * i + k, (net.chip(net.moved(axis, to)), net.c)))
        if partner:
            outs.append(send(None, at, 6, (net.e, 1 - net.c)))
        return outs

    done.extend(spread(net.at, 0))
    yield
    known = [(None, net.at)]

    for i, axis in enumerate(order):
        n, p = net.dims[axis], net.at[axis]
        fresh = []
        if n == 2:
            steps = [(None, 1 - p, None)]
        else:
            steps = []
            for k in range(1, n):
                steps.append((p - k >= 0, p - k, 0))
                steps.append((p + k <= n - 1, p + k, 1))
        for cond, o, way in steps:
            for kcond, kat in known:
                at = list(kat)
                at[axis] = o
                at = tuple(at)
                both = cond if kcond is None else (kcond if cond is None else jnp.logical_and(cond, kcond))

                def onward(at, way, i, axis):
                    outs = []
                    if way is not None:
                        cond2, to = net.near(axis)[way]
                        outs.append((cond2, 2 * i + way, (net.chip(net.moved(axis, to)), net.c)))
                    for j in range(i + 1, len(order)):
                        for k, (c2, to) in enumerate(net.near(order[j])):
                            outs.append((c2, 2 * j + k, (net.chip(net.moved(order[j], to)), net.c)))
                    if partner:
                        outs.append((None, 6, (net.e, 1 - net.c)))
                    return outs

                def arrive(at=at, way=way, i=i, axis=axis):
                    ch = net.chip(at)
                    rcopy(block(ch, net.c), block(ch, net.c), ss(ch, 0), rs(ch, net.c), (net.e, net.c)).wait_recv()
                    for c2, kind, dev in onward(at, way, i, axis):
                        send(c2, at, kind, dev)

                when(both, arrive)

                def drain(at=at, way=way, i=i, axis=axis, both=both):
                    def inner():
                        ch = net.chip(at)
                        for c2, kind, dev in onward(at, way, i, axis):
                            when(c2, lambda kind=kind, dev=dev: rcopy(
                                block(ch, net.c), block(ch, net.c), ss(ch, kind), rs(ch, net.c), dev).wait_send())
                    when(both, inner)

                done.append(drain)
                fresh.append((both, at))
                yield
        known = known + fresh
    if partner:
        for kcond, kat in known:
            def theirs(kat=kat):
                ch = net.chip(kat)
                rcopy(block(ch, 1 - net.c), block(ch, 1 - net.c), ss(ch, 0), rs(ch, 1 - net.c), (net.e, net.c)).wait_recv()
            done.append(lambda kcond=kcond, theirs=theirs: when(kcond, theirs))


def add_into(dst, src, rows):
    step = 16
    assert rows % step == 0

    def body(i, _):
        r = pl.ds(pl.multiple_of(i * step, step), step)
        dst[r, :] = (dst[r, :].astype(F32) + src[r, :].astype(F32)).astype(BF)
        return 0

    lax.fori_loop(0, rows // step, body, 0)


def rs_piece(net, order, mine, acc, bufs, key, rs, ss, rows, done, partner=True):
    def all_combos(axes_left):
        out = [()]
        for ax in axes_left:
            out = [o + (v,) for o in out for v in range(net.dims[ax])]
        return out

    def p_send(at):
        ch = net.chip(at)
        mk = lambda: rcopy(mine(ch, 1 - net.c), acc(ch), ss(0, ch), rs(0, ch), (net.e, 1 - net.c))
        mk().start()
        done.append(lambda: mk().wait_send())

    def p_recv(at):
        ch = net.chip(at)
        rcopy(acc(ch), acc(ch), ss(0, ch), rs(0, ch), (net.e, net.c)).wait_recv()
        add_into(acc(ch), mine(ch, net.c), rows)

    stages = []
    for i, axis in enumerate(order):
        left = order[i + 1:]
        combos = all_combos(left)
        stages.append((i, axis, left, combos))

    def targets_of(i, axis, left, combo, t):
        at = list(net.at)
        at[axis] = t
        for ax, v in zip(left, combo):
            at[ax] = v
        return tuple(at)

    for i, axis, left, combos in stages:
        n, p = net.dims[axis], net.at[axis]
        for combo in combos:
            for d in range(1, n):
                t = (p + d) % n
                p_send(targets_of(i, axis, left, combo, t))
        yield
    p_send(net.at)
    yield

    for i, axis, left, combos in stages:
        n, p = net.dims[axis], net.at[axis]
        nxt = lambda to, axis=axis: (net.chip(net.moved(axis, to)), net.c)

        def gather_prev(at):
            p_recv(at)
            for i2, axis2, left2, _ in stages[:i]:
                land(i2, axis2, left2, at)

        def land(i2, axis2, left2, at):
            n2, p2 = net.dims[axis2], net.at[axis2]
            ch = net.chip(at)

            def take(way):
                k = key(i2, way, at)
                rcopy(bufs(i2, k), bufs(i2, k), ss(i2 + 1, k), rs(i2 + 1, k), (net.e, net.c)).wait_recv()
                add_into(acc(ch), bufs(i2, k), rows)

            if n2 == 2:
                take(0)
            else:
                when(p2 > 0, lambda: take(0))
                when(p2 < n2 - 1, lambda: take(1))

        for combo in combos:
            if n == 2:
                at = targets_of(i, axis, left, combo, 1 - p)
                gather_prev(at)
                ch = net.chip(at)
                k = key(i, 0, at)
                mk = lambda ch=ch, k=k, i=i: rcopy(acc(ch), bufs(i, k), ss(i + 1, k), rs(i + 1, k), nxt(1 - p))
                mk().start()
                done.append(lambda mk=mk: mk().wait_send())
                yield
            else:
                for s in range(n - 1):
                    for way in (0, 1):
                        t = n - 1 - s if way == 0 else s
                        cond = (p < t) if way == 0 else (p > t)
                        to = p + 1 if way == 0 else p - 1
                        inner_cond = (p > 0) if way == 0 else (p < n - 1)
                        at = targets_of(i, axis, left, combo, t)
                        ch, k = net.chip(at), key(i, way, at)
                        mk = lambda ch=ch, k=k, i=i, to=to: rcopy(acc(ch), bufs(i, k), ss(i + 1, k), rs(i + 1, k), nxt(to))

                        def step(at=at, ch=ch, k=k, i=i, inner_cond=inner_cond, mk=mk):
                            gather_prev(at)

                            def relay():
                                rcopy(bufs(i, k), bufs(i, k), ss(i + 1, k), rs(i + 1, k), (net.e, net.c)).wait_recv()
                                add_into(acc(ch), bufs(i, k), rows)

                            pl.when(inner_cond)(relay)
                            mk().start()

                        pl.when(cond)(step)
                        done.append(lambda cond=cond, mk=mk: pl.when(cond)(lambda: mk().wait_send()))
                        yield
    at = net.at
    p_recv(at)
    for i2, axis2, left2, _ in stages:
        n2, p2 = net.dims[axis2], net.at[axis2]
        ch = net.chip(at)

        def take(way, i2=i2):
            k = key(i2, way, at)
            rcopy(bufs(i2, k), bufs(i2, k), ss(i2 + 1, k), rs(i2 + 1, k), (net.e, net.c)).wait_recv()
            add_into(acc(ch), bufs(i2, k), rows)

        if n2 == 2:
            take(0)
        else:
            when(p2 > 0, lambda: take(0))
            when(p2 < n2 - 1, lambda: take(1))
        yield


def rs_keys(net, order):
    def size(i):
        left = order[i + 1:]
        m = 1
        for ax in left:
            m *= net.dims[ax]
        n = net.dims[order[i]]
        return m if n == 2 else 2 * n * m

    def key(i, way, at):
        left = order[i + 1:]
        k = 0
        for ax in left:
            k = k * net.dims[ax] + at[ax]
        n = net.dims[order[i]]
        if n == 2:
            return k
        return (k * n + at[order[i]]) * 2 + way

    return key, [size(i) for i in range(len(order))]


def params(cid, vmem=None):
    return pltpu.CompilerParams(collective_id=cid, has_side_effects=True, vmem_limit_bytes=vmem)


ANY = pl.BlockSpec(memory_space=pl.ANY)
VM = pl.BlockSpec(memory_space=pltpu.VMEM)
DMA = pltpu.SemaphoreType.DMA

ORDER_A = (0, 1, 2)
ORDER_B = (0, 2, 1)


def all_gather_all(n_expert, x, cid):
    rows, cols = x.shape
    half = rows // 2

    def kernel(x_ref, o_ref, rsem, ssem, lsem):
        net = Net(n_expert).enter()
        cp = pltpu.make_async_copy(x_ref, o_ref.at[net.e, net.c], lsem)
        cp.start()
        greet(net, (0, 1, 2))
        cp.wait()
        done = []
        gens = []
        for i, order in enumerate((ORDER_A, ORDER_B)):
            gens.append(ag_piece(
                net, order,
                lambda ch, co, i=i: o_ref.at[ch, co, pl.ds(i * half, half)],
                lambda ch, co, i=i: rsem.at[i, ch, co],
                lambda ch, kind, i=i: ssem.at[i, ch, kind], done))
        interleave(*gens)
        for f in done:
            f()

    return pl.pallas_call(
        kernel, out_shape=jax.ShapeDtypeStruct((n_expert, 2, rows, cols), x.dtype),
        in_specs=[VM], out_specs=ANY,
        scratch_shapes=[DMA((2, n_expert, 2)), DMA((2, n_expert, 7)), DMA],
        compiler_params=params(cid), name="gather_all",
    )(x)


def reduce_scatter_all(n_expert, t, cid):
    _, _, rows, cols = t.shape
    half = rows // 2
    net0 = Net(n_expert)
    orders = ((2, 1, 0), (1, 2, 0))
    keys = [rs_keys(net0, o) for o in orders]
    sizes = keys[0][1]
    ns = max([n_expert] + sizes)

    def kernel(t_ref, o_ref, acc, b0, b1, b2, rsem, ssem):
        net = Net(n_expert).enter()
        greet(net, (0, 1, 2))
        done, gens = [], []
        bb = (b0, b1, b2)
        for i, order in enumerate(orders):
            key = keys[i][0]
            r = pl.ds(i * half, half)
            gens.append(rs_piece(
                net, order,
                lambda ch, co, r=r: t_ref.at[ch, co, r],
                lambda ch, r=r: acc.at[ch, r],
                lambda st, k, r=r: bb[st].at[k, r],
                key,
                lambda st, k, i=i: rsem.at[i, st, k],
                lambda st, k, i=i: ssem.at[i, st, k], half, done))
        interleave(*gens)
        o_ref[...] = acc[net.e]
        for f in done:
            f()

    return pl.pallas_call(
        kernel, out_shape=jax.ShapeDtypeStruct((rows, cols), BF),
        in_specs=[VM], out_specs=VM,
        scratch_shapes=[pltpu.VMEM((n_expert, rows, cols), BF)]
        + [pltpu.VMEM((s, rows, cols), BF) for s in sizes]
        + [DMA((2, 4, ns)), DMA((2, 4, ns))],
        compiler_params=params(cid, 60 << 20), name="reduce_all",
    )(t)


def local_copy(src, dst, sem, done):
    cp = lambda: pltpu.make_async_copy(src, dst, sem)
    cp().start()
    done.append(lambda: cp().wait())


def col_ag(net, src, dst, rs, ss, done):
    z, c = net.at[0], net.c
    n = net.dims[0]
    own = z // 2 == c
    s0 = z % 2

    def zdev(to):
        return (net.chip(net.moved(0, to)), c)

    def hop(cond, s, h, way, to, source=None):
        mk = lambda: rcopy(dst(s, h) if source is None else source, dst(s, h), ss(way, s, h), rs(s, h), zdev(to))
        when(cond, lambda: mk().start())
        return lambda: when(cond, lambda: mk().wait_send())

    def arrived(s, h):
        rcopy(dst(s, h), dst(s, h), ss(0, s, h), rs(s, h), (net.e, c)).wait_recv()

    across = lambda: rcopy(src, dst(s0, c), ss(2, 0, 0), rs(s0, c), (net.e, 1 - c))
    keep = lambda: pltpu.make_async_copy(src, dst(s0, c), ss(2, 0, 1))

    def begin():
        keep().start()
        hop(z < n - 1, s0, c, 0, z + 1, src)
        hop(z > 0, s0, c, 1, z - 1, src)

    pl.when(own)(begin)
    pl.when(jnp.logical_not(own))(lambda: across().start())
    yield

    def second():
        arrived(s0, 1 - c)
        hop(z < n - 1, s0, 1 - c, 0, z + 1)
        hop(z > 0, s0, 1 - c, 1, z - 1)

    pl.when(own)(second)
    yield

    def end():
        keep().wait()
        for h in (c, 1 - c):
            source = src if h is c else None
            when(z < n - 1, lambda h=h, source=source: rcopy(
                src if source is not None else dst(s0, h), dst(s0, h), ss(0, s0, h), rs(s0, h), zdev(z + 1)).wait_send())
            when(z > 0, lambda h=h, source=source: rcopy(
                src if source is not None else dst(s0, h), dst(s0, h), ss(1, s0, h), rs(s0, h), zdev(z - 1)).wait_send())

    done.append(lambda: pl.when(own)(end))
    done.append(lambda: pl.when(jnp.logical_not(own))(lambda: across().wait_send()))

    for k in range(1, n):
        for way in (0, 1):
            o = z - k if way == 0 else z + k
            inside = o >= 0 if way == 0 else o <= n - 1
            cond = jnp.logical_and(inside, o // 2 == c)
            more = z < n - 1 if way == 0 else z > 0
            to = z + 1 if way == 0 else z - 1

            def step(o=o, way=way, more=more, to=to):
                for h in (0, 1):
                    arrived(o % 2, h)
                    hop(more, o % 2, h, way, to)

            def finish(o=o, way=way, more=more, to=to):
                for h in (0, 1):
                    when(more, lambda h=h: rcopy(
                        dst(o % 2, h), dst(o % 2, h), ss(way, o % 2, h), rs(o % 2, h), zdev(to)).wait_send())

            pl.when(cond)(step)
            done.append(lambda cond=cond, finish=finish: pl.when(cond)(finish))
            yield


def col_rs(net, part, out, acc, buf, fin, rs, ss, rows, done):
    z, c = net.at[0], net.c
    n = net.dims[0]

    def zdev(to):
        return (net.chip(net.moved(0, to)), c)

    def msg(way, s, h, to):
        return rcopy(acc(way, s, h), buf(way, s, h), ss(way, s, h), rs(way, s, h), zdev(to))

    def arrived(way, s, h):
        rcopy(buf(way, s, h), buf(way, s, h), ss(way, s, h), rs(way, s, h), (net.e, c)).wait_recv()

    for k in range(n - 1):
        for way in (0, 1):
            t = n - 1 - k if way == 0 else k
            s = t % 2
            cond = jnp.logical_and(z < t if way == 0 else z > t, t // 2 == c)
            inner = z > 0 if way == 0 else z < n - 1
            to = z + 1 if way == 0 else z - 1
            for h in (0, 1):
                def step(way=way, s=s, h=h, inner=inner, to=to):
                    def relay():
                        arrived(way, s, h)
                        sum_to(acc(way, s, h), [part(s, h), buf(way, s, h)], rows)

                    pl.when(inner)(relay)
                    pl.when(jnp.logical_not(inner))(lambda: sum_to(acc(way, s, h), [part(s, h)], rows))
                    msg(way, s, h, to).start()

                pl.when(cond)(step)
                done.append(lambda cond=cond, way=way, s=s, h=h, to=to: pl.when(cond)(lambda: msg(way, s, h, to).wait_send()))
                yield

    own = z // 2 == c
    s0 = z % 2
    cross = lambda: rcopy(fin(0), fin(1), ss(2, 0, 0), rs(2, 0, 0), (net.e, 1 - c))

    def last(h, to_ref):
        low, high = z > 0, z < n - 1
        pl.when(low)(lambda: arrived(0, s0, h))
        pl.when(high)(lambda: arrived(1, s0, h))
        mid = jnp.logical_and(low, high)
        pl.when(mid)(lambda: sum_to(to_ref, [part(s0, h), buf(0, s0, h), buf(1, s0, h)], rows))
        pl.when(jnp.logical_not(low))(lambda: sum_to(to_ref, [part(s0, h), buf(1, s0, h)], rows))
        pl.when(jnp.logical_not(high))(lambda: sum_to(to_ref, [part(s0, h), buf(0, s0, h)], rows))

    def final():
        last(1 - c, fin(0))
        cross().start()
        last(c, out)

    pl.when(own)(final)
    done.append(lambda: pl.when(own)(lambda: cross().wait_send()))

    def take():
        cross().wait_recv()
        sum_to(out, [fin(1)], rows)

    yield
    pl.when(jnp.logical_not(own))(take)


def sum_to(dst, srcs, rows):
    step = 16

    def body(i, _):
        r = pl.ds(pl.multiple_of(i * step, step), step)
        v = srcs[0][r, :]
        if len(srcs) > 1:
            v = v.astype(F32)
            for s in srcs[1:]:
                v = v + s[r, :].astype(F32)
        dst[r, :] = v.astype(BF)
        return 0

    lax.fori_loop(0, rows // step, body, 0)


def to_all(net, src, dst, rs, ss, done):
    total = net.chips * 2
    me = net.e * 2 + net.c

    def put(k, _):
        t = (me + k) % total
        rcopy(src(t), dst(me), ss(k), rs(me), (t // 2, t % 2)).start()
        return 0

    lax.fori_loop(1, total, put, 0)
    yield

    def take(k, _):
        t = (me + k) % total
        rcopy(src(t), dst(me), ss(k), rs(me), (t // 2, t % 2)).wait_send()
        rcopy(dst(t), dst(t), ss(k), rs(t), (net.e, net.c)).wait_recv()
        return 0

    done.append(lambda: lax.fori_loop(1, total, take, 0))


def gather_start(n_expert, tokens, wqkv, w_out, aux, cot, cid):
    T, D = tokens.shape
    Z, R, C = wqkv.shape
    HR = w_out.shape[0]
    AR, AW = aux.shape
    plane = n_expert // Z
    nd = 2 * n_expert

    def kernel(t_ref, w_ref, o_ref, a_ref, g_ref, X, W, O, A, G,
               xr, xs, wr, ws, war, was, oar, oas, ar, as_, gr, gs, loc):
        net = Net(n_expert).enter()
        z, p, c = net.at[0], net.e % plane, net.c
        me = net.e * 2 + c
        done = []
        local_copy(w_ref.at[z], W.at[z, p, c], loc.at[0], [])
        local_copy(o_ref, O.at[p, c], loc.at[1], [])
        local_copy(a_ref, A.at[me], loc.at[2], done)
        local_copy(g_ref, G.at[net.e, c], loc.at[3], [])
        greet_all(net)

        def wgen():
            for k in range(1, Z):
                j = (z + k) % Z
                mk = lambda j=j, k=k: rcopy(w_ref.at[j], W.at[z, p, c], ws.at[k], wr.at[z], (j * plane + p, c))
                mk().start()
                done.append(lambda mk=mk: mk().wait_send())
            yield
            pltpu.make_async_copy(w_ref.at[z], W.at[z, p, c], loc.at[0]).wait()
            for k in range(1, Z):
                o = (z + k) % Z
                rcopy(W.at[o, p, c], W.at[o, p, c], ws.at[k], wr.at[o], (net.e, c)).wait_recv()
            gens = []
            for i, order in enumerate(((1, 2), (2, 1))):
                r = pl.ds(i * (Z // 2), Z // 2)
                gens.append(ag_piece(
                    net, order, lambda ch, co, r=r: W.at[r, ch % plane, co],
                    lambda ch, co, i=i: war.at[i, ch % plane, co], lambda ch, kind, i=i: was.at[i, ch % plane, kind], done))
            while gens:
                for g in list(gens):
                    try:
                        next(g)
                        yield
                    except StopIteration:
                        gens.remove(g)

        def ogen(i, order):
            if i == 0:
                pltpu.make_async_copy(o_ref, O.at[p, c], loc.at[1]).wait()
            r = pl.ds(i * (HR // 2), HR // 2)
            yield from ag_piece(
                net, order, lambda ch, co: O.at[ch % plane, co, r],
                lambda ch, co: oar.at[i, ch % plane, co], lambda ch, kind: oas.at[i, ch % plane, kind], done)

        def ggen(i, order):
            if i == 0:
                pltpu.make_async_copy(g_ref, G.at[net.e, c], loc.at[3]).wait()
            r = pl.ds(i * (T // 2), T // 2)
            yield from ag_piece(
                net, order, lambda ch, co: G.at[ch, co, r],
                lambda ch, co: gr.at[i, ch, co], lambda ch, kind: gs.at[i, ch, kind], done)

        interleave(
            wgen(),
            to_all(net, lambda t: a_ref, lambda s: A.at[s], lambda s: ar.at[s], lambda k: as_.at[k], done),
            col_ag(net, t_ref, lambda s, h: X.at[s, h], lambda s, h: xr.at[s, h], lambda w, s, h: xs.at[w, s, h], done),
            ogen(0, (1, 2)), ogen(1, (2, 1)), ggen(0, ORDER_A), ggen(1, ORDER_B))
        for f in done:
            f()

    S = jax.ShapeDtypeStruct
    return pl.pallas_call(
        kernel,
        out_shape=(S((2, 2, T, D), BF), S((Z, plane, 2, R, C), BF), S((plane, 2, HR, D), BF), S((nd, AR, AW), BF),
                   S((n_expert, 2, T, D), BF)),
        in_specs=[VM, VM, VM, VM, VM], out_specs=(ANY,) * 5,
        scratch_shapes=[DMA((2, 2)), DMA((3, 2, 2)), DMA((Z,)), DMA((Z,)), DMA((2, plane, 2)), DMA((2, plane, 7)),
                        DMA((2, plane, 2)), DMA((2, plane, 7)), DMA((nd,)), DMA((nd,)),
                        DMA((2, n_expert, 2)), DMA((2, n_expert, 7)), DMA((4,))],
        compiler_params=params(cid), name="gather_start",
    )(tokens, wqkv, w_out, aux, cot)


def column_sum(n_expert, part, cid):
    _, _, T, D = part.shape

    def kernel(p_ref, o_ref, acc, buf, fin, rsem, ssem):
        net = Net(n_expert).enter()
        greet(net, (0,))
        done = []
        interleave(col_rs(
            net, lambda s, h: p_ref.at[s, h], o_ref, lambda w, s, h: acc.at[w, s, h], lambda w, s, h: buf.at[w, s, h],
            lambda i: fin.at[i], lambda w, s, h: rsem.at[w, s, h], lambda w, s, h: ssem.at[w, s, h], T, done))
        for f in done:
            f()

    return pl.pallas_call(
        kernel, out_shape=jax.ShapeDtypeStruct((T, D), BF), in_specs=[VM], out_specs=VM,
        scratch_shapes=[pltpu.VMEM((2, 2, 2, T, D), BF), pltpu.VMEM((2, 2, 2, T, D), BF), pltpu.VMEM((2, T, D), BF),
                        DMA((3, 2, 2)), DMA((3, 2, 2))],
        compiler_params=params(cid, 40 << 20), name="column_sum",
    )(part)


def column_gather(n_expert, x, cid):
    T, D = x.shape

    def kernel(x_ref, X, rsem, ssem):
        net = Net(n_expert).enter()
        greet(net, (0,))
        done = []
        interleave(col_ag(net, x_ref, lambda s, h: X.at[s, h], lambda s, h: rsem.at[s, h], lambda w, s, h: ssem.at[w, s, h], done))
        for f in done:
            f()

    return pl.pallas_call(
        kernel, out_shape=jax.ShapeDtypeStruct((2, 2, T, D), BF), in_specs=[VM], out_specs=ANY,
        scratch_shapes=[DMA((2, 2)), DMA((3, 2, 2))],
        compiler_params=params(cid), name="column_gather",
    )(x)


def gather_all(n_expert, x, aux, cid):
    rows, cols = x.shape
    half = rows // 2
    nd = 2 * n_expert

    def kernel(x_ref, a_ref, o_ref, A, rsem, ssem, ar, as_, lsem):
        net = Net(n_expert).enter()
        me = net.e * 2 + net.c
        done = []
        local_copy(x_ref, o_ref.at[net.e, net.c], lsem.at[0], [])
        local_copy(a_ref, A.at[me], lsem.at[1], done)
        greet_all(net)
        pltpu.make_async_copy(x_ref, o_ref.at[net.e, net.c], lsem.at[0]).wait()
        gens = [to_all(net, lambda t: a_ref, lambda s: A.at[s], lambda s: ar.at[s], lambda k: as_.at[k], done)]
        for i, order in enumerate((ORDER_A, ORDER_B)):
            gens.append(ag_piece(
                net, order,
                lambda ch, co, i=i: o_ref.at[ch, co, pl.ds(i * half, half)],
                lambda ch, co, i=i: rsem.at[i, ch, co],
                lambda ch, kind, i=i: ssem.at[i, ch, kind], done))
        interleave(*gens)
        for f in done:
            f()

    return pl.pallas_call(
        kernel,
        out_shape=(jax.ShapeDtypeStruct((n_expert, 2, rows, cols), x.dtype), jax.ShapeDtypeStruct((nd,) + aux.shape, aux.dtype)),
        in_specs=[VM, VM], out_specs=(ANY, ANY),
        scratch_shapes=[DMA((2, n_expert, 2)), DMA((2, n_expert, 7)), DMA((nd,)), DMA((nd,)), DMA((2,))],
        compiler_params=params(cid), name="gather_all",
    )(x, aux)


def exchange(n_expert, x, cid):
    nd = 2 * n_expert

    def kernel(x_ref, o_ref, ar, as_, lsem):
        net = Net(n_expert).enter()
        me = net.e * 2 + net.c
        done = []
        local_copy(x_ref.at[me], o_ref.at[me], lsem.at[0], done)
        greet_all(net)
        interleave(to_all(net, lambda t: x_ref.at[t], lambda s: o_ref.at[s], lambda s: ar.at[s], lambda k: as_.at[k], done))
        for f in done:
            f()

    return pl.pallas_call(
        kernel, out_shape=jax.ShapeDtypeStruct(x.shape, x.dtype), in_specs=[VM], out_specs=VM,
        scratch_shapes=[DMA((nd,)), DMA((nd,)), DMA((2,))],
        compiler_params=params(cid), name="exchange",
    )(x)


def reduce_end(n_expert, part, dw, do, small, cid):
    _, _, T, D = part.shape
    Z, plane, _, R, C = dw.shape
    HR = do.shape[2]
    nd = 2 * n_expert
    net0 = Net(n_expert)
    orders = ((2, 1), (1, 2))
    keys = [rs_keys(net0, o) for o in orders]
    sizes = keys[0][1]
    ns = max([plane] + sizes)
    hr = HR // 2

    def kernel(p_ref, dw_ref, do_ref, s_ref, x_out, w_out, o_out, s_out,
               acc, buf, fin, wacc, wb0, wb1, oacc, ob0, ob1, wsh,
               xr, xs, wr, ws, our, ous, sr, s_s, zr, zs, loc):
        net = Net(n_expert).enter()
        z, p, c = net.at[0], net.e % plane, net.c
        me = net.e * 2 + c
        done = []
        local_copy(s_ref.at[me], s_out.at[me], loc.at[0], done)
        greet_all(net)

        def wgen(q):
            i = q // (Z // 2)
            key = keys[i][0]
            bb = (wb0, wb1)
            yield from rs_piece(
                net, orders[i], lambda ch, co: dw_ref.at[q, ch % plane, co], lambda ch: wacc.at[q, ch % plane],
                lambda st, k: bb[st].at[q, k], key, lambda st, k: wr.at[q, st, k if st else k % plane],
                lambda st, k: ws.at[q, st, k if st else k % plane], R, done)
            mk = lambda: rcopy(wacc.at[q, p], wsh.at[z], zs.at[q], zr.at[z], (q * plane + p, c))
            pl.when(z != q)(lambda: mk().start())
            done.append(lambda: pl.when(z != q)(lambda: mk().wait_send()))
            pl.when(z == q)(lambda: sum_to(w_out.at[q], [wacc.at[q, p]], R))

        def ogen(i):
            key = keys[i][0]
            bb = (ob0, ob1)
            r = pl.ds(i * hr, hr)
            yield from rs_piece(
                net, orders[i], lambda ch, co: do_ref.at[ch % plane, co, r], lambda ch: oacc.at[ch % plane, r],
                lambda st, k: bb[st].at[k, r], key, lambda st, k: our.at[i, st, k if st else k % plane],
                lambda st, k: ous.at[i, st, k if st else k % plane], hr, done)

        interleave(
            to_all(net, lambda t: s_ref.at[t], lambda s: s_out.at[s], lambda s: sr.at[s], lambda k: s_s.at[k], done),
            *[wgen(q) for q in range(Z)],
            col_rs(net, lambda s, h: p_ref.at[s, h], x_out, lambda w, s, h: acc.at[w, s, h], lambda w, s, h: buf.at[w, s, h],
                   lambda i: fin.at[i], lambda w, s, h: xr.at[w, s, h], lambda w, s, h: xs.at[w, s, h], T, done),
            ogen(0), ogen(1))
        o_out[...] = oacc[p]
        for k in range(1, Z):
            o = (z + k) % Z
            rcopy(wsh.at[o], wsh.at[o], zs.at[0], zr.at[o], (net.e, c)).wait_recv()
            sum_to(w_out.at[o], [wsh.at[o]], R)
        for f in done:
            f()

    S = jax.ShapeDtypeStruct
    V = pltpu.VMEM
    return pl.pallas_call(
        kernel, out_shape=(S((T, D), BF), S((Z, R, C), BF), S((HR, D), BF), S(small.shape, small.dtype)),
        in_specs=[VM] * 4, out_specs=(VM,) * 4,
        scratch_shapes=[V((2, 2, 2, T, D), BF), V((2, 2, 2, T, D), BF), V((2, T, D), BF),
                        V((Z, plane, R, C), BF), V((Z, sizes[0], R, C), BF), V((Z, sizes[1], R, C), BF),
                        V((plane, HR, D), BF), V((sizes[0], HR, D), BF), V((sizes[1], HR, D), BF), V((Z, R, C), BF),
                        DMA((3, 2, 2)), DMA((3, 2, 2)), DMA((Z, 3, ns)), DMA((Z, 3, ns)), DMA((2, 3, ns)), DMA((2, 3, ns)),
                        DMA((nd,)), DMA((nd,)), DMA((Z,)), DMA((Z,)), DMA((1,))],
        compiler_params=params(cid, 60 << 20), name="reduce_end",
    )(part, dw, do, small)


MODEL_WIDTH = 2048
QUERY_HEADS = 32
KEY_VALUE_HEADS = 4
HEAD_SIZE = 128
GROUP = QUERY_HEADS // KEY_VALUE_HEADS
TOP = 8
EXP_DEV = 2

epsilon = 1e-06
rope_base = 1000000.0


def norm_parts(values_in, gain_vec):
    inverse = lax.rsqrt(jnp.mean(values_in * values_in, axis=-1, keepdims=True) + epsilon)
    return (values_in * inverse * gain_vec, inverse)


def norm_back(values_in, inverse, gain_vec, grad_out):
    scaled = grad_out * gain_vec
    grad_in = inverse * (
        scaled
        - values_in * inverse * inverse * jnp.mean(scaled * values_in, axis=-1, keepdims=True)
    )
    return (grad_in, grad_out * values_in * inverse)


def rope_tables(positions):
    exponent = jnp.arange(HEAD_SIZE // 2).astype(F32) * (2.0 / HEAD_SIZE)
    frequency = jnp.exp(-math.log(rope_base) * exponent)
    angles = positions.astype(F32)[:, None] * frequency[None, :]
    return (jnp.cos(angles), jnp.sin(angles))


def rotate(v, cos, sin):
    half = v.shape[-1] // 2
    a, b = v[..., :half], v[..., half:]
    return jnp.concatenate([a * cos - b * sin, b * cos + a * sin], axis=-1)


def rotate_back(v, cos, sin):
    half = v.shape[-1] // 2
    a, b = v[..., :half], v[..., half:]
    return jnp.concatenate([a * cos + b * sin, b * cos - a * sin], axis=-1)


def mm(a, b):
    return jnp.dot(a, b, preferred_element_type=F32)


def ein(spec, *args):
    return jnp.einsum(spec, *args, preferred_element_type=F32)


def local(
    n_expert, tokens, routes, documents, w_query, key_projection, value_projection, w_out, w_router,
    gain_attn, gain_ffn, gain_query, gain_key, w_gate, w_up, w_down, cotangent,
):
    Z = KEY_VALUE_HEADS
    plane = n_expert // Z
    nd = 2 * n_expert
    T, D = tokens.shape
    R, HR, E = w_query.shape[0], w_out.shape[0], w_router.shape[1]
    Q = gain_query.shape[0]
    KV = HEAD_SIZE
    GQ = GROUP * HEAD_SIZE
    e, c = lax.axis_index("expert"), lax.axis_index("context")
    z, p = e // plane, e % plane
    capacity = T * TOP * 5 // (4 * E)
    score_scale = HEAD_SIZE ** (-0.5)

    wqkv = jnp.concatenate(
        [w_query.reshape(R, Z, GQ), key_projection.reshape(R, Z, KV), value_projection.reshape(R, Z, KV)], axis=-1
    ).transpose(1, 0, 2)
    width = -(-(E + 4) // 128) * 128
    pad = lambda v: jnp.pad(v, (0, R - v.shape[0]))[:, None]
    head = jnp.concatenate(
        [w_router, gain_attn[:, None], gain_ffn[:, None], pad(gain_query), pad(gain_key), jnp.zeros((R, width - E - 4), BF)], axis=1
    )
    docs_own = lax.dynamic_slice_in_dim(documents[0], c * T, T).astype(BF)[None]
    docs_own = jnp.pad(docs_own, ((0, 15), (0, width - T)))
    aux = jnp.concatenate([head, docs_own], axis=0)
    X, W, O, A, G = gather_start(n_expert, tokens, wqkv, w_out, aux, cotangent, 0)
    W = W.reshape(D, GQ + 2 * KV)
    O = O.reshape(GQ, D)
    table = A[:, :R].reshape(D, width)
    router_weight = table[:, :E]
    attn_gain = table[:, E].astype(F32)
    ffn_gain = table[:, E + 1].astype(F32)
    query_gain = A[:, :Q, E + 2].reshape(HEAD_SIZE).astype(F32)
    key_gain = A[:, :Q, E + 3].reshape(HEAD_SIZE).astype(F32)
    docs = A[:, R, :T].reshape(Z, plane, 2 * T)
    docs = lax.dynamic_slice(docs, (2 * c, p, 0), (2, 1, 2 * T)).reshape(2, 2 * T)

    L = 2 * T
    x = X.reshape(2 * L, D).astype(F32)
    normed, inverse_attn = norm_parts(x, attn_gain)
    first_in = normed.astype(BF)
    raw = mm(first_in, W)
    query_raw = raw[:, :GQ].reshape(2, L, GROUP, HEAD_SIZE)
    key_raw = raw[:, GQ:GQ + KV].reshape(2, L, HEAD_SIZE)
    value = raw[:, GQ + KV:].reshape(2, L, HEAD_SIZE).astype(BF)
    cos, sin = rope_tables(jnp.arange(L, dtype=jnp.int32))
    qcos, qsin = cos[:, None, :], sin[:, None, :]
    query_normed, query_inverse = norm_parts(query_raw, query_gain)
    queries = rotate(query_normed, qcos, qsin).astype(BF)
    key_normed, key_inverse = norm_parts(key_raw, key_gain)
    keys = rotate(key_normed, cos, sin).astype(BF)
    places = jnp.arange(L, dtype=jnp.int32)
    allowed = (places[:, None] >= places[None, :])[None] & (docs[:, :, None] == docs[:, None, :])
    scores = ein("sqhd,skd->shqk", queries, keys) * score_scale
    scores = jnp.where(allowed[:, None], scores, -1e30)
    top = jnp.max(scores, axis=-1, keepdims=True)
    ex = jnp.exp(scores - top)
    probs = ex / jnp.sum(ex, axis=-1, keepdims=True)
    probs_low = probs.astype(BF)
    attended = ein("shqk,skd->sqhd", probs_low, value).reshape(2 * L, GQ).astype(BF)
    part = mm(attended, O).astype(BF).reshape(2, 2, T, D)
    middle = tokens.astype(F32) + column_sum(n_expert, part, 1).astype(F32)

    normed_ffn, inverse_ffn = norm_parts(middle, ffn_gain)
    second_in = normed_ffn.astype(BF)
    logits = mm(second_in, router_weight)
    ids = jnp.arange(E, dtype=jnp.int32)
    chosen = jnp.any(routes[:, :, None] == ids[None, None, :], axis=1)
    masked = jnp.where(chosen, logits, -jnp.inf)
    best = jnp.max(masked, axis=-1, keepdims=True)
    ew = jnp.where(chosen, jnp.exp(logits - best), 0.0)
    weights = ew / jnp.sum(ew, axis=-1, keepdims=True)
    marked = jnp.where(chosen, weights, -1.0).T
    N, M = gather_all(n_expert, second_in, marked, 2)

    mine = lax.dynamic_slice(M, (0, EXP_DEV * e, 0), (nd, EXP_DEV, T))
    here = mine >= 0.0
    rank = jnp.cumsum(here.astype(jnp.int32), axis=-1) - 1
    slots = jnp.arange(capacity, dtype=jnp.int32)
    pick = here[:, :, None, :] & (rank[:, :, None, :] == slots[None, None, :, None])
    slot_weight = jnp.sum(jnp.where(pick, mine[:, :, None, :], 0.0), axis=-1).transpose(1, 0, 2)[..., None]
    pick = pick.astype(BF)
    N = N.reshape(nd, T, D)
    G = G.reshape(nd, T, D)
    rows = ein("sect,std->escd", pick, N).astype(BF)
    g_rows = ein("sect,std->escd", pick, G)
    flat = lambda v: v.reshape(EXP_DEV, nd * capacity, v.shape[-1])
    deep = lambda v: v.reshape(EXP_DEV, nd, capacity, v.shape[-1])
    rows = flat(rows)
    grad_rows = flat((slot_weight * g_rows).astype(BF))
    gate_value = ein("emd,edf->emf", rows, w_gate)
    up_value = ein("emd,edf->emf", rows, w_up)
    sig = jax.nn.sigmoid(gate_value)
    act = (gate_value * sig * up_value).astype(BF)
    expert_part = deep(ein("emf,efd->emd", act, w_down))
    dots = jnp.sum(g_rows * expert_part, axis=-1)
    out_part = ein("sect,escd->std", pick, (slot_weight * expert_part).astype(BF)).astype(BF)
    dots = ein("sect,esc->set", pick.astype(F32), dots)
    grad_act = ein("emd,efd->emf", grad_rows, w_down)
    grad_gate_v = (grad_act * up_value * sig * (1.0 + gate_value * (1.0 - sig))).astype(BF)
    grad_up_v = (grad_act * gate_value * sig).astype(BF)
    down_grad = ein("emf,emd->efd", act, grad_rows)
    gate_grad = ein("emd,emf->edf", rows, grad_gate_v)
    up_grad = ein("emd,emf->edf", rows, grad_up_v)
    back_rows = ein("emf,edf->emd", grad_gate_v, w_gate) + ein("emf,edf->emd", grad_up_v, w_up)
    back_part = ein("sect,escd->std", pick, deep(back_rows.astype(BF))).astype(BF)

    dots_out = jnp.pad(dots, ((0, 0), (0, 8 - EXP_DEV), (0, 0)))
    dots_in = exchange(n_expert, dots_out, 3)
    parts = max(1, n_expert // 16)

    def summed(v, cid):
        v = v.reshape(n_expert, 2, T, D)
        W_ = D // parts
        return jnp.concatenate(
            [reduce_scatter_all(n_expert, v[..., i * W_:(i + 1) * W_], cid + 2 * i) for i in range(parts)], axis=1).astype(F32)

    back_sum = summed(back_part, 8)
    out_sum = summed(out_part, 9)

    block_out = (middle + out_sum).astype(BF)
    grad_result = cotangent.astype(F32)
    grad_weights = jnp.sum(dots_in[:, :EXP_DEV].reshape(n_expert, 2, EXP_DEV, T), axis=1).reshape(E, T).T
    grad_chosen = weights * (grad_weights - jnp.sum(weights * grad_weights, axis=-1, keepdims=True))
    grad_logits = jnp.where(chosen, grad_chosen, 0.0).astype(BF)
    router_grad = mm(second_in.T, grad_logits)
    grad_second = mm(grad_logits, router_weight.T) + back_sum
    grad_middle_norm, ffn_terms = norm_back(middle, inverse_ffn, ffn_gain, grad_second)
    ffn_gain_grad = jnp.sum(ffn_terms, axis=0)
    grad_middle = grad_result + grad_middle_norm

    GA = column_gather(n_expert, grad_middle.astype(BF), 6).reshape(2 * L, D)
    out_grad = mm(attended.T, GA)
    grad_attended = ein("td,fd->tf", GA, O).astype(BF).reshape(2, L, GROUP, HEAD_SIZE)
    grad_probs = ein("sqhd,skd->shqk", grad_attended, value)
    grad_scores = (probs * (grad_probs - jnp.sum(probs * grad_probs, axis=-1, keepdims=True))).astype(BF)
    grad_queries = ein("shqk,skd->sqhd", grad_scores, keys) * score_scale
    grad_keys = ein("shqk,sqhd->skd", grad_scores, queries) * score_scale
    grad_values = ein("shqk,sqhd->skd", probs_low, grad_attended)
    grad_query_raw, query_terms = norm_back(query_raw, query_inverse, query_gain, rotate_back(grad_queries, qcos, qsin))
    grad_key_raw, key_terms = norm_back(key_raw, key_inverse, key_gain, rotate_back(grad_keys, cos, sin))
    grad_raw = jnp.concatenate(
        [grad_query_raw.reshape(2 * L, GQ).astype(BF), grad_key_raw.reshape(2 * L, KV).astype(BF),
         grad_values.reshape(2 * L, KV).astype(BF)], axis=-1)
    query_gain_grad = jnp.sum(query_terms, axis=(0, 1, 2))
    key_gain_grad = jnp.sum(key_terms, axis=(0, 1))
    grad_first = ein("tf,df->td", grad_raw, W)
    raw_grad = mm(first_in.T, grad_raw)
    attn_gain_grad = jnp.sum(grad_first * x * inverse_attn, axis=0)

    small = jnp.concatenate([
        router_grad.reshape(nd, R * E), attn_gain_grad.reshape(nd, R), ffn_gain_grad.reshape(nd, R),
        query_gain_grad.reshape(nd, Q), key_gain_grad.reshape(nd, Q)], axis=1)
    n_small = small.shape[1]
    small = jnp.pad(small, ((0, 0), (0, -n_small % 1024))).reshape(nd, -1, 128)
    grad_first_sum, raw_sum, out_sum2, small_in = reduce_end(
        n_expert, grad_first.astype(BF).reshape(2, 2, T, D), raw_grad.astype(BF).reshape(Z, plane, 2, R, GQ + 2 * KV),
        out_grad.astype(BF).reshape(plane, 2, HR, D), small, 7)
    small_sum = jnp.sum(small_in, axis=0).reshape(-1)
    router_grad = small_sum[:R * E].reshape(R, E)
    attn_gain_grad = small_sum[R * E:R * E + R]
    ffn_gain_grad = small_sum[R * E + R:R * E + 2 * R]
    query_gain_grad = small_sum[R * E + 2 * R:R * E + 2 * R + Q]
    key_gain_grad = small_sum[R * E + 2 * R + Q:n_small]
    raw_sum = raw_sum.astype(F32)
    query_grad = raw_sum[:, :, :GQ].transpose(1, 0, 2).reshape(R, QUERY_HEADS * HEAD_SIZE)
    key_grad = raw_sum[:, :, GQ:GQ + KV].transpose(1, 0, 2).reshape(R, Z * KV)
    value_grad = raw_sum[:, :, GQ + KV:].transpose(1, 0, 2).reshape(R, Z * KV)

    own = tokens.astype(F32)
    inverse_own = lax.rsqrt(jnp.mean(own * own, axis=-1, keepdims=True) + epsilon)
    grad_in, _ = norm_back(own, inverse_own, attn_gain, grad_first_sum.astype(F32))
    grad_tokens = grad_middle + grad_in
    return (
        block_out, grad_tokens, query_grad, key_grad, value_grad, out_sum2.astype(F32), router_grad,
        attn_gain_grad, ffn_gain_grad, query_gain_grad, key_gain_grad, gate_grad, up_grad, down_grad,
    )


def solution(mesh):
    row = P(("expert", "context"), None)
    vec = P(("expert", "context"))
    hidden = P("expert", None, "context")
    return jax.shard_map(
        functools.partial(local, mesh.shape["expert"]),
        mesh=mesh,
        in_specs=(row, row, P("expert", None), row, row, row, row, row, vec, vec, vec, vec, hidden, hidden,
                  P("expert", "context", None), row),
        out_specs=(row, row, row, row, row, row, row, vec, vec, vec, vec, hidden, hidden, P("expert", "context", None)),
        check_vma=False,
    )
```

time: 2250 us -> 961 us (0.43)
  waiting for transfers between devices: 1460 us -> 0 us
  Pallas kernels: 0 us -> 642 us
  blocking collectives: 351 us -> 0 us
  local copies, waits for them, and re-layouts: 123 us -> 64.1 us
    reduce_scatter x6 -> x0, waiting for transfers between devices: 1000 us -> none  [the longest x1 393 us: local(): lax.psum_scatter(out_grad, ('expert', 'context'), scatter_dimension=0, ti...]
    pallas_call x0 -> x8, Pallas kernels: none -> 642 us  [the longest x2 250 us: reduce_scatter_all(): pl.pallas_call(kernel, out_shape=jax.ShapeDtypeStruct((rows, cols), BF),...]
    all_gather x6 -> x0, waiting for transfers between devices: 247 us -> none  [the longest x1 104 us: local(): lax.all_gather(w_query, ('expert', 'context'), axis=0, tiled=True)]
    all_to_all x3 -> x0, waiting for transfers between devices: 201 us -> none  [the longest x1 105 us: local(): lax.all_to_all(expert_rows, 'expert', split_axis=0, concat_axis=0, tiled=...]
    all_gather x3 -> x0, blocking collectives: 150 us -> none  [the longest x1 142 us: local(): lax.all_gather(w_router, ('expert', 'context'), axis=0, tiled=True)]
    all_to_all x1 -> x0, blocking collectives: 121 us -> none  [local(): lax.all_to_all(grad_outgoing, 'expert', split_axis=0, concat_axis=0, tile...]
    unnamed x2 -> x0, blocking collectives: 78.9 us -> none
    gather x5 -> x0, local copies, waits for them, and re-layouts: 53 us -> none  [the longest x1 12.1 us: local(): grad_result[source_tokens]]
  transfers between devices with their start and end apart: 18 -> 0, of which waited for: 12 -> 0; matrix products, arithmetic and copies ran while one was open for 13% -> 0% of each run, Pallas kernels for 0% -> 0%
where the time goes in v1:
time: 961 us; the launch traced here: 949 us
  Pallas kernels  642 us (67%)
  matrix products  197 us (20%)
  local copies, waits for them, and re-layouts  64.1 us (7%)
  other arithmetic  45.1 us (5%)
    pallas_call x2, Pallas kernels, reduce_scatter_all(): pl.pallas_call(kernel, out_shape=jax.ShapeDtypeStruct((rows, cols), BF),...  250 us
    dot_general x21, matrix products, ein(): return jnp.einsum(spec, *args, preferred_element_type=F32)  167 us
    pallas_call x1, Pallas kernels, gather_start(): pl.pallas_call(kernel, out_shape=(S((2, 2, T, D), BF), S((Z, plane, 2, R,...  127 us
    pallas_call x1, Pallas kernels, gather_all(): pl.pallas_call(kernel, out_shape=(jax.ShapeDtypeStruct((n_expert, 2, rows...  82.8 us
    pallas_call x1, Pallas kernels, reduce_end(): pl.pallas_call(kernel, out_shape=(S((T, D), BF), S((Z, R, C), BF), S((HR,...  82.4 us
    pallas_call x1, Pallas kernels, column_sum(): pl.pallas_call(kernel, out_shape=jax.ShapeDtypeStruct((T, D), BF), in_spe...  46.8 us
    pallas_call x1, Pallas kernels, column_gather(): pl.pallas_call(kernel, out_shape=jax.ShapeDtypeStruct((2, 2, T, D), BF),...  40.7 us
    dot_general x7, matrix products, mm(): return jnp.dot(a, b, preferred_element_type=F32)  24.3 us

profile of v1, /device:TPU:13, one launch (start us, length us, event | category | flops | bytes accessed | tf_op | source)
XLA Modules:
  0.0 949.4 jit_solution(15242276772733403955)
XLA Ops:
  11.1 126.7 %gather_start.1 = (bf16[2,2,128,2048]{3,2,1,0:T(8,128)(2,1)}, bf16[4,4,2,64,1280]{4,3,2,1,0:T(8,128)(2,1)}, bf16[4,2,128,2048]{3,2,1,0:T(8,128)(2,1)}, bf16[32,8...) custom-call(bf16[128,2048]{1,0:T(8,128)(2,1)} %t_ref.1, bf16[4,64,1280]{2,1,0:T(8,128)(2,1)} %maximum_bitcast_fusion.w_ref, ...), custom_call_target="tpu_custom_call" | custom-call | tf_op jit(solution)/shard_map/gather_start/pallas_call | solution.py:657
  137.8 2.1 fusion.5
  142.0 1.9 slice.83
  145.5 2.9 slice_convert_fusion
  148.3 2.1 copy.341
  150.5 1.6 copy.340
  152.1 2.1 fusion.7
  154.2 5.4 fusion.87
  164.4 1.8 slice_bitcast_fusion
  169.3 1.7 copy.239
  172.6 3.0 mul.698.clone
  176.9 2.1 subtract_convert_fusion
  179.0 5.6 fusion.86
  184.6 3.7 fusion.26
  188.3 2.8 copy.243
  191.1 4.8 convolution_convert_fusion.2
  196.0 46.8 %column_sum.1 = bf16[128,2048]{1,0:T(8,128)(2,1)S(1)} custom-call(bf16[2,2,128,2048]{3,2,1,0:T(8,128)(2,1)S(1)} %bitcast.257), custom_call_target="tpu_custom_call" | custom-call | tf_op jit(solution)/shard_map/column_sum/pallas_call | solution.py:682
  245.3 82.8 %gather_all.1 = (bf16[16,2,128,2048]{3,2,1,0:T(8,128)(2,1)}, f32[32,32,128]{2,1,0:T(8,128)}) custom-call(bf16[128,2048]{1,0:T(8,128)(2,1)} %copy-done.18, f32[32,128]{1,0:T(8,128)} %fusion.73.a_ref), custom_call_target="tpu_custom_call" | custom-call | tf_op jit(solution)/shard_map/gather_all/pallas_call | solution.py:732
  330.2 9.6 %convert_bitcast_fusion = bf16[2,32,40,2048]{3,2,0,1:T(8,128)(2,1)} fusion(bf16[32,128,2048,1]{2,1,3,0:T(8,128)(2,1)} %bitcast.265, s32[32,2,128]{2,1,0:T(2,128)S(1)} %copy.247, pred[32,2,128]{2,1,0:T(4,128)(4,1)S(1)} %get-tuple-element.116), kind=kOutput, calls=%fused_computation.10 | convolution fusion | flops 1348075520 | bytes 27303936 | tf_op jit(solution)/shard_map/sect,std->escd/dot_general | solution.py:883
  339.8 10.1 %copy.248 = bf16[2,32,40,2048]{3,2,1,0:T(8,128)(2,1)} copy(bf16[2,32,40,2048]{3,2,0,1:T(8,128)(2,1)} %convert_bitcast_fusion) | data formatting | bytes 20971520 | tf_op jit(solution)/shard_map/convert_element_type | solution.py:973
  350.0 9.4 fusion.88
  359.4 7.9 multiply_convert_fusion.4
  367.3 10.1 %fusion.89 = f32[2,1280,2048]{2,1,0:T(8,128)} fusion(bf16[2,1280,384]{2,1,0:T(8,128)(2,1)S(1)} %get-tuple-element.153, bf16[2,384,2048]{2,1,0:T(8,128)(2,1)S(1)} %copy-done), kind=kOutput, calls=%fused_computation.199 | convolution fusion | flops 4026531840 | bytes 26083328 | tf_op jit(solution)/shard_map/emf,efd->emd/dot_general | solution.py:883
  377.4 18.3 %fusion.2 = (bf16[2,32,40,2048]{3,2,0,1:T(8,128)(2,1)}, f32[2,32,40]{2,0,1:T(2,128)S(1)}) fusion(f32[2,32,40]{2,0,1:T(2,128)S(1)} %bitcast.299, f32[2,32,40,2048]{3,2,1,0:T(8,128)} %bitcast.258, bf16[32,128,2048,1]{2,1,3,0:T(8,128)(2,1)} %bitcast.266, s32[32,2,128]{2,1,0:T(2,128)S(1)} %copy.247, pred[32,2,128]{2,1,0:T(4,128)(4,1)S(1)} %get-tuple-element.116), kind=kOutput, calls=%fused_computation.6 | convolution fusion | flops 1363801600 | bytes 48295936 | tf_op jit(solution)/shard_map/sect,std->escd/dot_general | solution.py:883
  395.6 12.7 %bitcast_convert_fusion.1 = bf16[32,128,2048]{2,1,0:T(8,128)(2,1)} fusion(f32[2,32,40,2048]{3,2,1,0:T(8,128)} %bitcast.259, f32[2,32,40]{2,0,1:T(2,128)S(1)} %bitcast.300, s32[32,2,128]{2,1,0:T(2,128)S(1)} %copy.247, pred[32,2,128]{2,1,0:T(4,128)(4,1)S(1)} %get-tuple-element.116), kind=kOutput, calls=%fused_computation.2 | convolution fusion | flops 1361707008 | bytes 37799936 | tf_op jit(solution)/shard_map/sect,escd->std/dot_general | solution.py:883
  408.4 124.8 %reduce_all.2 = bf16[128,2048]{1,0:T(8,128)(2,1)} custom-call(bf16[16,2,128,2048]{3,2,1,0:T(8,128)(2,1)} %bitcast.260), custom_call_target="tpu_custom_call" | custom-call | tf_op jit(solution)/shard_map/reduce_all/pallas_call | solution.py:399
  533.2 10.2 %copy.251 = bf16[2,32,40,2048]{3,2,1,0:T(8,128)(2,1)} copy(bf16[2,32,40,2048]{3,2,0,1:T(8,128)(2,1)} %get-tuple-element.118) | data formatting | bytes 20971520 | tf_op jit(solution)/shard_map/convert_element_type | solution.py:978
  543.3 13.2 %multiply_convert_fusion.2 = (bf16[2,1280,384]{2,1,0:T(8,128)(2,1)}, bf16[2,1280,384]{2,1,0:T(8,128)(2,1)}) fusion(f32[2,1280,384]{2,1,0:T(8,128)} %copy-done.71, f32[2,1280,384]{2,1,0:T(8,128)} %get-tuple-element.154, bf16[2,1280,2048]{2,1,0:T(8,128)(2,1)} %bitcast.263, bf16[2,384,2048]{2,1,0:T(8,128)(2,1)S(1)} %copy-done), kind=kOutput, calls=%fused_computation.31 | convolution fusion | flops 4039311360 | bytes 25427968 | tf_op jit(solution)/shard_map/emd,efd->emf/dot_general | solution.py:883
  556.6 6.4 fusion.94
  564.0 12.6 %exchange.1 = f32[32,8,128]{2,1,0:T(8,128)} custom-call(f32[32,8,128]{2,1,0:T(8,128)} %pad.22.x_ref), custom_call_target="tpu_custom_call" | custom-call | tf_op jit(solution)/shard_map/exchange/pallas_call | solution.py:754
  579.1 10.8 %fusion.93 = f32[2,2048,384]{2,1,0:T(8,128)} fusion(bf16[2,1280,2048]{2,1,0:T(8,128)(2,1)} %bitcast.271, bf16[2,1280,384]{2,1,0:T(8,128)(2,1)} %get-tuple-element.120), kind=kOutput, calls=%fused_computation.203 | convolution fusion | flops 4026531840 | bytes 18743296 | tf_op jit(solution)/shard_map/emd,emf->edf/dot_general | solution.py:883
  589.9 10.6 %fusion.92 = f32[2,2048,384]{2,1,0:T(8,128)} fusion(bf16[2,1280,2048]{2,1,0:T(8,128)(2,1)} %bitcast.272, bf16[2,1280,384]{2,1,0:T(8,128)(2,1)S(1)} %copy-done.22), kind=kOutput, calls=%fused_computation.202 | convolution fusion | flops 4026531840 | bytes 18743296 | tf_op jit(solution)/shard_map/emd,emf->edf/dot_general | solution.py:883
  600.5 9.9 %fusion.90 = f32[2,1280,2048]{2,1,0:T(8,128)} fusion(bf16[2,1280,384]{2,1,0:T(8,128)(2,1)S(1)} %copy-done.22, bf16[2,2048,384]{2,1,0:T(8,128)(2,1)S(1)} %copy-done.35), kind=kOutput, calls=%fused_computation.200 | convolution fusion | flops 4026531840 | bytes 26083328 | tf_op jit(solution)/shard_map/emf,edf->emd/dot_general | solution.py:883
  610.4 13.7 %add_convert_fusion = bf16[2,1280,2048]{2,1,0:T(8,128)(2,1)} fusion(f32[2,1280,2048]{2,1,0:T(8,128)} %fusion.90, bf16[2,1280,384]{2,1,0:T(8,128)(2,1)} %get-tuple-element.120, bf16[2,2048,384]{2,1,0:T(8,128)(2,1)} %param.29), kind=kOutput, calls=%fused_computation.7 | convolution fusion | flops 4037017600 | bytes 36569088 | tf_op jit(solution)/shard_map/emf,edf->emd/dot_general | solution.py:883
  624.2 10.6 %bitcast_convert_fusion = bf16[32,128,2048]{2,1,0:T(8,128)(2,1)} fusion(bf16[2,32,40,2048]{3,2,1,0:T(8,128)(2,1)} %bitcast.262, s32[32,2,128]{2,1,0:T(2,128)S(1)} %copy.247, pred[32,2,128]{2,1,0:T(4,128)(4,1)S(1)} %get-tuple-element.116), kind=kOutput, calls=%fused_computation.1 | convolution fusion | flops 1351221248 | bytes 27303936 | tf_op jit(solution)/shard_map/sect,escd->std/dot_general | solution.py:883
  634.8 124.9 %reduce_all.3 = bf16[128,2048]{1,0:T(8,128)(2,1)} custom-call(bf16[16,2,128,2048]{3,2,1,0:T(8,128)(2,1)} %bitcast.261), custom_call_target="tpu_custom_call" | custom-call | tf_op jit(solution)/shard_map/reduce_all/pallas_call | solution.py:399
  759.7 1.8 multiply_reduce_fusion.2
  764.1 40.7 %column_gather.1 = bf16[2,2,128,2048]{3,2,1,0:T(8,128)(2,1)} custom-call(bf16[128,2048]{1,0:T(8,128)(2,1)} %fusion.82.x_ref), custom_call_target="tpu_custom_call" | custom-call | tf_op jit(solution)/shard_map/column_gather/pallas_call | solution.py:701
  804.8 5.3 fusion.25
  812.3 4.4 convolution_convert_fusion.1
  820.4 2.4 multiply_bitcast_fusion
  826.2 3.1 multiply_add_fusion
  829.3 1.9 multiply_reduce_fusion
  835.3 1.8 fusion.21
  837.1 8.3 fusion.11
  848.0 7.2 convolution_convert_fusion
  855.2 82.4 %reduce_end.1 = (bf16[128,2048]{1,0:T(8,128)(2,1)}, bf16[4,64,1280]{2,1,0:T(8,128)(2,1)}, bf16[128,2048]{1,0:T(8,128)(2,1)}, f32[32,24,128]{2,1,0:T(8,128)}) custom-call(bf16[2,2,128,2048]{3,2,1,0:T(8,128)(2,1)} %bitcast.290, bf16[4,4,2,64,1280]{4,3,2,1,0:T(8,128)(2,1)} %bitcast.280, bf16[4,2,128,2048]{3,2,1,0:T(8,128)(2,1)} %bitcast.281, ...), custom_call_target="tpu_custom_call" | custom-call | tf_op jit(solution)/shard_map/reduce_end/pallas_call | solution.py:821
  939.0 3.1 fusion.42
  (242 shorter events, 59.4 us)
Async XLA Ops:
  0.6 366.6 %copy-start = (bf16[2,384,2048]{2,1,0:T(8,128)(2,1)S(1)}, bf16[2,384,2048]{2,1,0:T(8,128)(2,1)}, u32[]{:S(2)}) copy-start(bf16[2,384,2048]{2,1,0:T(8,128)(2,1)} %param.30) | copy-start | bytes 9437188
  9.0 167.8 %copy-start.30 = (f32[256,64]{1,0:T(8,128)}, f32[256,64]{1,0:T(8,128)S(1)}, u32[]{:S(2)}) copy-start(f32[256,64]{1,0:T(8,128)S(1)} %get-tuple-element.147) | copy-start | bytes 196612
  9.0 167.8 %copy-start.32 = (f32[256,64]{1,0:T(8,128)}, f32[256,64]{1,0:T(8,128)S(1)}, u32[]{:S(2)}) copy-start(f32[256,64]{1,0:T(8,128)S(1)} %get-tuple-element.148) | copy-start | bytes 196612
  139.9 12.2 %copy-start.62 = (f32[2,2,128]{2,1,0:T(2,128)}, f32[2,2,128]{2,1,0:T(2,128)S(1)}, u32[]{:S(2)}) copy-start(f32[2,2,128]{2,1,0:T(2,128)S(1)} %add_rsqrt_fusion.2) | copy-start | bytes 6148
  144.0 8.1 copy-start.60
  144.1 17.8 %copy-start.58 = (f32[128]{0:T(128)}, f32[128]{0:T(128)S(1)}, u32[]{:S(2)}) copy-start(f32[128]{0:T(128)S(1)} %reshape.475) | copy-start | bytes 1540
  152.1 7.6 copy-start.49
  164.4 14.6 %copy-start.42 = (bf16[2,256,64]{2,1,0:T(8,128)(2,1)}, bf16[2,256,64]{2,1,0:T(8,128)(2,1)S(1)}, u32[]{:S(2)}) copy-start(bf16[2,256,64]{2,1,0:T(8,128)(2,1)S(1)} %get-tuple-element.141) | copy-start | bytes 196612
  172.5 3.0 copy-start.6
  179.0 5.6 copy-start.51
  184.6 3.7 copy-start.55
  195.9 46.8 %copy-start.10 = (bf16[128,2048]{1,0:T(8,128)(2,1)S(1)}, bf16[128,2048]{1,0:T(8,128)(2,1)}, u32[]{:S(2)}) copy-start(bf16[128,2048]{1,0:T(8,128)(2,1)} %t_ref.1) | copy-start | bytes 1572868
  195.9 47.6 %copy-start.47 = (f32[2048,1]{0,1:T(1,128)S(1)}, f32[2048,1]{0,1:T(1,128)}, u32[]{:S(2)}) copy-start(f32[2048,1]{0,1:T(1,128)} %copy.341) | copy-start | bytes 24580
  195.9 47.8 %copy-start.15 = (bf16[32,64,128]{2,1,0:T(8,128)(2,1)S(1)}, bf16[32,64,128]{2,1,0:T(8,128)(2,1)}, u32[]{:S(2)}) copy-start(bf16[32,64,128]{2,1,0:T(8,128)(2,1)} %slice.83) | copy-start | bytes 1572868
  196.0 47.8 %copy-start.46 = (pred[128,32]{0,1:T(8,128)(4,1)S(1)}, pred[128,32]{0,1:T(8,128)(4,1)}, u32[]{:S(2)}) copy-start(pred[128,32]{0,1:T(8,128)(4,1)} %fusion.69) | copy-start | bytes 12292
  350.0 9.4 copy-start.12
  350.0 9.4 copy-start.34
  359.3 7.9 copy-start.71
  367.3 10.1 %copy-start.8 = (bf16[2,1280,384]{2,1,0:T(8,128)(2,1)}, bf16[2,1280,384]{2,1,0:T(8,128)(2,1)S(1)}, u32[]{:S(2)}) copy-start(bf16[2,1280,384]{2,1,0:T(8,128)(2,1)S(1)} %get-tuple-element.153) | copy-start | bytes 5898244
  543.3 13.2 %copy-start.4 = (bf16[2,32,40,2048]{3,2,1,0:T(8,128)(2,1)S(1)}, bf16[2,32,40,2048]{3,2,1,0:T(8,128)(2,1)}, u32[]{:S(2)}) copy-start(bf16[2,32,40,2048]{3,2,1,0:T(8,128)(2,1)} %copy.251) | copy-start | bytes 31457284
  543.3 13.2 %copy-start.9 = (bf16[2,1280,384]{2,1,0:T(8,128)(2,1)S(1)}, bf16[2,1280,384]{2,1,0:T(8,128)(2,1)}, u32[]{:S(2)}) copy-start(bf16[2,1280,384]{2,1,0:T(8,128)(2,1)} %copy-done.8) | copy-start | bytes 5898244
  556.5 21.0 %copy-start.19 = (bf16[128,2048]{1,0:T(8,128)(2,1)S(1)}, bf16[128,2048]{1,0:T(8,128)(2,1)}, u32[]{:S(2)}) copy-start(bf16[128,2048]{1,0:T(8,128)(2,1)} %copy-done.18) | copy-start | bytes 1572868
  579.1 10.8 %copy-start.22 = (bf16[2,1280,384]{2,1,0:T(8,128)(2,1)S(1)}, bf16[2,1280,384]{2,1,0:T(8,128)(2,1)}, u32[]{:S(2)}) copy-start(bf16[2,1280,384]{2,1,0:T(8,128)(2,1)} %get-tuple-element.121) | copy-start | bytes 5898244
  589.9 10.6 %copy-start.35 = (bf16[2,2048,384]{2,1,0:T(8,128)(2,1)S(1)}, bf16[2,2048,384]{2,1,0:T(8,128)(2,1)}, u32[]{:S(2)}) copy-start(bf16[2,2048,384]{2,1,0:T(8,128)(2,1)} %param.28) | copy-start | bytes 9437188
  634.8 124.9 %copy-start.3 = (bf16[128,2048]{1,0:T(8,128)(2,1)S(1)}, bf16[128,2048]{1,0:T(8,128)(2,1)}, u32[]{:S(2)}) copy-start(bf16[128,2048]{1,0:T(8,128)(2,1)} %copy-done.2) | copy-start | bytes 1572868
  634.8 124.9 %copy-start.11 = (bf16[128,2048]{1,0:T(8,128)(2,1)S(1)}, bf16[128,2048]{1,0:T(8,128)(2,1)}, u32[]{:S(2)}) copy-start(bf16[128,2048]{1,0:T(8,128)(2,1)} %t_ref.1) | copy-start | bytes 1572868
  634.8 124.9 %copy-start.16 = (bf16[32,64,128]{2,1,0:T(8,128)(2,1)S(1)}, bf16[32,64,128]{2,1,0:T(8,128)(2,1)}, u32[]{:S(2)}) copy-start(bf16[32,64,128]{2,1,0:T(8,128)(2,1)} %slice.83) | copy-start | bytes 1572868
  634.8 125.0 %copy-start.48 = (f32[2048,1]{0,1:T(1,128)S(1)}, f32[2048,1]{0,1:T(1,128)}, u32[]{:S(2)}) copy-start(f32[2048,1]{0,1:T(1,128)} %copy.341) | copy-start | bytes 24580
  634.8 125.0 %copy-start.65 = (f32[128]{0:T(128)S(1)}, f32[128]{0:T(128)}, u32[]{:S(2)}) copy-start(f32[128]{0:T(128)} %copy-done.64) | copy-start | bytes 1540
  759.7 3.1 copy-start.23
  761.5 43.2 %copy-start.27 = (f32[128,2048]{1,0:T(8,128)}, f32[128,2048]{1,0:T(8,128)S(1)}, u32[]{:S(2)}) copy-start(f32[128,2048]{1,0:T(8,128)S(1)} %get-tuple-element.155) | copy-start | bytes 3145732
  761.6 43.2 %copy-start.67 = (f32[128]{0:T(128)}, f32[128]{0:T(128)S(1)}, u32[]{:S(2)}) copy-start(f32[128]{0:T(128)S(1)} %broadcast_multiply_fusion.3) | copy-start | bytes 1540
  804.8 5.6 copy-start.29
  804.8 5.6 copy-start.56
  812.3 4.4 copy-start.52
  826.2 3.1 copy-start.7
  826.2 3.1 copy-start.61
  837.1 8.3 copy-start.40
  837.1 9.2 copy-start.38
  855.2 83.8 %copy-start.24 = (bf16[128,2048]{1,0:T(8,128)(2,1)S(1)}, bf16[128,2048]{1,0:T(8,128)(2,1)}, u32[]{:S(2)}) copy-start(bf16[128,2048]{1,0:T(8,128)(2,1)} %g_ref.1) | copy-start | bytes 1572868
  855.2 83.8 %copy-start.28 = (f32[128,2048]{1,0:T(8,128)S(1)}, f32[128,2048]{1,0:T(8,128)}, u32[]{:S(2)}) copy-start(f32[128,2048]{1,0:T(8,128)} %copy-done.27) | copy-start | bytes 3145732
  855.2 83.8 %copy-start.36 = (bf16[128,2048]{1,0:T(8,128)(2,1)S(1)}, bf16[128,2048]{1,0:T(8,128)(2,1)}, u32[]{:S(2)}) copy-start(bf16[128,2048]{1,0:T(8,128)(2,1)} %reduce_all.2) | copy-start | bytes 1572868
  855.2 83.8 %copy-start.66 = (f32[128]{0:T(128)S(1)}, f32[128]{0:T(128)}, u32[]{:S(2)}) copy-start(f32[128]{0:T(128)} %copy-done.64) | copy-start | bytes 1540
  855.2 83.8 %copy-start.68 = (f32[128]{0:T(128)S(1)}, f32[128]{0:T(128)}, u32[]{:S(2)}) copy-start(f32[128]{0:T(128)} %copy-done.67) | copy-start | bytes 1540
  855.2 83.8 %copy-start.69 = (f32[128]{0:T(128)S(1)}, f32[128]{0:T(128)}, u32[]{:S(2)}) copy-start(f32[128]{0:T(128)} %add_rsqrt_fusion.3) | copy-start | bytes 1540
  939.0 3.1 copy-start.45
  945.3 2.6 copy-start.41
  945.3 3.6 copy-start.1
  (24 other events, 39.3 us)

commit v2 on v1

--- a/solution.py
+++ b/solution.py
@@ -592,8 +592,14 @@
     plane = n_expert // Z
     nd = 2 * n_expert
 
-    def kernel(t_ref, w_ref, o_ref, a_ref, g_ref, X, W, O, A, G,
-               xr, xs, wr, ws, war, was, oar, oas, ar, as_, gr, gs, loc):
+    with_g = cot is not None
+
+    def kernel(*refs):
+        k = 5 if with_g else 4
+        t_ref, w_ref, o_ref, a_ref = refs[:4]
+        g_ref, G = (refs[4], refs[2 * k - 1]) if with_g else (None, None)
+        X, W, O, A = refs[k:k + 4]
+        xr, xs, wr, ws, war, was, oar, oas, ar, as_, gr, gs, loc = refs[2 * k:]
         net = Net(n_expert).enter()
         z, p, c = net.at[0], net.e % plane, net.c
         me = net.e * 2 + c
@@ -601,7 +607,8 @@
         local_copy(w_ref.at[z], W.at[z, p, c], loc.at[0], [])
         local_copy(o_ref, O.at[p, c], loc.at[1], [])
         local_copy(a_ref, A.at[me], loc.at[2], done)
-        local_copy(g_ref, G.at[net.e, c], loc.at[3], [])
+        if with_g:
+            local_copy(g_ref, G.at[net.e, c], loc.at[3], [])
         greet_all(net)
 
         def wgen():
@@ -649,21 +656,21 @@
             wgen(),
             to_all(net, lambda t: a_ref, lambda s: A.at[s], lambda s: ar.at[s], lambda k: as_.at[k], done),
             col_ag(net, t_ref, lambda s, h: X.at[s, h], lambda s, h: xr.at[s, h], lambda w, s, h: xs.at[w, s, h], done),
-            ogen(0, (1, 2)), ogen(1, (2, 1)), ggen(0, ORDER_A), ggen(1, ORDER_B))
+            ogen(0, (1, 2)), ogen(1, (2, 1)), *([ggen(0, ORDER_A), ggen(1, ORDER_B)] if with_g else []))
         for f in done:
             f()
 
     S = jax.ShapeDtypeStruct
     return pl.pallas_call(
         kernel,
-        out_shape=(S((2, 2, T, D), BF), S((Z, plane, 2, R, C), BF), S((plane, 2, HR, D), BF), S((nd, AR, AW), BF),
-                   S((n_expert, 2, T, D), BF)),
-        in_specs=[VM, VM, VM, VM, VM], out_specs=(ANY,) * 5,
+        out_shape=(S((2, 2, T, D), BF), S((Z, plane, 2, R, C), BF), S((plane, 2, HR, D), BF), S((nd, AR, AW), BF))
+        + ((S((n_expert, 2, T, D), BF),) if with_g else ()),
+        in_specs=[VM] * (5 if with_g else 4), out_specs=(ANY,) * (5 if with_g else 4),
         scratch_shapes=[DMA((2, 2)), DMA((3, 2, 2)), DMA((Z,)), DMA((Z,)), DMA((2, plane, 2)), DMA((2, plane, 7)),
                         DMA((2, plane, 2)), DMA((2, plane, 7)), DMA((nd,)), DMA((nd,)),
                         DMA((2, n_expert, 2)), DMA((2, n_expert, 7)), DMA((4,))],
         compiler_params=params(cid), name="gather_start",
-    )(tokens, wqkv, w_out, aux, cot)
+    )(tokens, wqkv, w_out, aux, *((cot,) if with_g else ()))
 
 
 def column_sum(n_expert, part, cid):
@@ -830,6 +837,616 @@
     )(part, dw, do, small)
 
 
+def slot_plane(z, i):
+    near = jnp.where(z < 2, z, 3 - z)
+    t = jnp.where(jnp.logical_and(near == 1, i < 2), 1 - i, i)
+    return jnp.where(z < 2, t, 3 - t)
+
+
+class Gather22:
+    def __init__(self, net, N, T, rsem, ssem):
+        self.net, self.N, self.T, self.rsem, self.ssem = net, N, T, rsem, ssem
+        self.axes = ((1, 2), (2, 1))
+
+    def blk(self, piece, chip, core):
+        h = self.T // 2
+        return self.N.at[chip, pl.ds(pl.multiple_of(core * self.T + piece * h, h), h)]
+
+    def copy(self, piece, at, kind, dev):
+        n = self.net
+        ch = n.chip(at)
+        b = self.blk(piece, ch, n.c)
+        return rcopy(b, b, self.ssem.at[piece, ch, kind], self.rsem.at[piece, ch, n.c], dev)
+
+    def wait(self, piece, at, core):
+        n = self.net
+        ch = n.chip(at)
+        b = self.blk(piece, ch, core)
+        rcopy(b, b, self.ssem.at[piece, ch, 0], self.rsem.at[piece, ch, core], (n.e, n.c)).wait_recv()
+
+    def dev(self, axis, to=None):
+        n = self.net
+        return (n.chip(n.moved(axis, 1 - n.at[axis] if to is None else to)), n.c)
+
+    def level(self, piece, zt, two, three):
+        n = self.net
+        at = [zt, n.at[1], n.at[2]]
+        u, v = self.axes[piece]
+        if two:
+            at[u] = 1 - at[u]
+        if three:
+            at[v] = 1 - at[v]
+        return tuple(at)
+
+    def outs(self, piece, zt, two, three):
+        u, v = self.axes[piece]
+        at = self.level(piece, zt, two, three)
+        r = []
+        if not two and not three:
+            r.append((2, self.dev(u)))
+        if not three:
+            r.append((3, self.dev(v)))
+        r.append((4, (self.net.e, 1 - self.net.c)))
+        return at, r
+
+    def push(self, piece, zt, two, three):
+        at, r = self.outs(piece, zt, two, three)
+        for kind, dev in r:
+            self.copy(piece, at, kind, dev).start()
+
+    def begin(self):
+        z = self.net.at[0]
+        for piece in (0, 1):
+            pl.when(z < 3)(lambda piece=piece: self.copy(piece, self.net.at, 0, self.dev(0, z + 1)).start())
+            pl.when(z > 0)(lambda piece=piece: self.copy(piece, self.net.at, 1, self.dev(0, z - 1)).start())
+            self.push(piece, z, False, False)
+
+    def onward(self, zt):
+        z = self.net.at[0]
+        to = jnp.where(zt < z, z + 1, z - 1)
+        return to, jnp.logical_and(to >= 0, to <= 3)
+
+    def from_z(self, zt):
+        to, more = self.onward(zt)
+        for piece in (0, 1):
+            at = self.level(piece, zt, False, False)
+            self.wait(piece, at, self.net.c)
+            pl.when(more)(lambda piece=piece, at=at: self.copy(piece, at, 0, self.dev(0, to)).start())
+            self.push(piece, zt, False, False)
+
+    def from_two(self, zt):
+        for piece in (0, 1):
+            self.wait(piece, self.level(piece, zt, True, False), self.net.c)
+            self.push(piece, zt, True, False)
+
+    def from_three(self, zt):
+        for two in (False, True):
+            for piece in (0, 1):
+                self.wait(piece, self.level(piece, zt, two, True), self.net.c)
+                self.push(piece, zt, two, True)
+
+    def from_partner(self, zt):
+        for piece in (0, 1):
+            for a in (0, 1):
+                for b in (0, 1):
+                    self.wait(piece, (zt, a, b), 1 - self.net.c)
+
+    def drain(self, i):
+        z = self.net.at[0]
+        zt = slot_plane(z, i)
+        to, more = self.onward(zt)
+        for piece in (0, 1):
+            def own(piece=piece):
+                pl.when(z < 3)(lambda: self.copy(piece, self.net.at, 0, self.dev(0, z + 1)).wait_send())
+                pl.when(z > 0)(lambda: self.copy(piece, self.net.at, 1, self.dev(0, z - 1)).wait_send())
+
+            pl.when(i == 0)(own)
+            at0 = self.level(piece, zt, False, False)
+            pl.when(jnp.logical_and(i > 0, more))(
+                lambda piece=piece, at0=at0: self.copy(piece, at0, 0, self.dev(0, to)).wait_send())
+            for two in (False, True):
+                for three in (False, True):
+                    at, r = self.outs(piece, zt, two, three)
+                    for kind, dev in r:
+                        self.copy(piece, at, kind, dev).wait_send()
+
+
+def add_rows(dst, srcs, rows):
+    step = 32
+
+    def body(i, _):
+        r = pl.ds(pl.multiple_of(i * step, step), step)
+        v = dst[r, :].astype(F32)
+        for s in srcs:
+            v = v + s[r, :].astype(F32)
+        dst[r, :] = v.astype(BF)
+        return 0
+
+    lax.fori_loop(0, rows // step, body, 0)
+
+
+class Reduce22:
+    def __init__(self, net, T, acc, buf1, buf2, zbuf, sems):
+        self.net, self.T = net, T
+        self.acc, self.buf1, self.buf2, self.zbuf = acc, buf1, buf2, zbuf
+        (self.r0, self.s0, self.r1, self.s1, self.r2, self.s2, self.r3, self.s3) = sems
+        self.first = (2, 1)
+        self.second = (1, 2)
+
+    @staticmethod
+    def scratch(T, D):
+        V = pltpu.VMEM
+        return [V((16, T, D), BF), V((4, 2, T, D), BF), V((4, T, D), BF), V((2, 4, T, D), BF),
+                DMA((16,)), DMA((16,)), DMA((2, 4, 2)), DMA((2, 4, 2)), DMA((2, 4)), DMA((2, 4)), DMA((2, 2, 4)), DMA((2, 2, 4))]
+
+    def half(self, piece):
+        h = self.T // 2
+        return pl.ds(piece * h, h)
+
+    def ring(self):
+        n = self.net
+        a, b = n.at[1], n.at[2]
+        return [(1 - a, 1 - b), (a, 1 - b), (1 - a, b), (a, b)]
+
+    def p_copy(self, Tb, zt, ab):
+        n = self.net
+        p = ab[0] * 2 + ab[1]
+        ch = zt * 4 + p
+        src = Tb.at[p, pl.ds(pl.multiple_of((1 - n.c) * self.T, self.T), self.T)]
+        return rcopy(src, self.acc.at[ch], self.s0.at[ch], self.r0.at[ch], (n.e, 1 - n.c))
+
+    def p_send(self, Tb, zt):
+        for ab in self.ring():
+            self.p_copy(Tb, zt, ab).start()
+
+    def p_wait_send(self, Tb, zt):
+        for ab in self.ring():
+            self.p_copy(Tb, zt, ab).wait_send()
+
+    def p_take(self, Tb, zt, ab):
+        n = self.net
+        p = ab[0] * 2 + ab[1]
+        self.p_copy(Tb, zt, ab).wait_recv()
+        add_rows(self.acc.at[zt * 4 + p], [Tb.at[p, pl.ds(pl.multiple_of(n.c * self.T, self.T), self.T)]], self.T)
+
+    def one(self, piece, zt, idx):
+        n = self.net
+        ax = self.first[piece]
+        at = [zt, n.at[1], n.at[2]]
+        at[ax] = 1 - at[ax]
+        at[self.second[piece]] = idx
+        src = self.acc.at[n.chip(at), self.half(piece)]
+        dst = self.buf1.at[zt, idx, self.half(piece)]
+        return rcopy(src, dst, self.s1.at[piece, zt, idx], self.r1.at[piece, zt, idx], (n.chip(n.moved(ax, 1 - n.at[ax])), n.c))
+
+    def two(self, piece, zt):
+        n = self.net
+        ax = self.second[piece]
+        at = [zt, n.at[1], n.at[2]]
+        at[ax] = 1 - at[ax]
+        src = self.acc.at[n.chip(at), self.half(piece)]
+        return rcopy(src, self.buf2.at[zt, self.half(piece)], self.s2.at[piece, zt], self.r2.at[piece, zt],
+                     (n.chip(n.moved(ax, 1 - n.at[ax])), n.c))
+
+    def three(self, piece, zt):
+        n = self.net
+        z = n.at[0]
+        up = zt > z
+        d = jnp.where(up, 0, 1)
+        to = jnp.where(up, z + 1, z - 1)
+        src = self.acc.at[n.chip((zt, n.at[1], n.at[2])), self.half(piece)]
+        return rcopy(src, self.zbuf.at[d, zt, self.half(piece)], self.s3.at[piece, d, zt], self.r3.at[piece, d, zt],
+                     (n.chip(n.moved(0, to)), n.c))
+
+    def stage0(self, Tb, zt):
+        n = self.net
+        order = self.ring()
+        self.p_take(Tb, zt, order[0])
+        self.one(0, zt, 1 - n.at[1]).start()
+        self.one(1, zt, 1 - n.at[2]).start()
+        self.p_take(Tb, zt, order[1])
+        self.one(0, zt, n.at[1]).start()
+        self.p_take(Tb, zt, order[2])
+        self.one(1, zt, n.at[2]).start()
+        self.p_take(Tb, zt, order[3])
+
+    def stage1(self, zt):
+        n = self.net
+        for part in (0, 1):
+            for piece in (0, 1):
+                own = n.at[self.second[piece]]
+                idx = 1 - own if part == 0 else own
+                at = [zt, n.at[1], n.at[2]]
+                at[self.second[piece]] = idx
+                self.one(piece, zt, idx).wait_recv()
+                add_rows(self.acc.at[n.chip(at), self.half(piece)], [self.buf1.at[zt, idx, self.half(piece)]], self.T // 2)
+                if part == 0:
+                    self.two(piece, zt).start()
+
+    def stage2(self, zt):
+        n = self.net
+        z = n.at[0]
+        feeds = jnp.where(zt > z, z > 0, z < 3)
+        for piece in (0, 1):
+            self.two(piece, zt).wait_recv()
+            add_rows(self.acc.at[n.chip((zt, n.at[1], n.at[2])), self.half(piece)], [self.buf2.at[zt, self.half(piece)]], self.T // 2)
+            pl.when(jnp.logical_and(zt != z, jnp.logical_not(feeds)))(lambda piece=piece: self.three(piece, zt).start())
+
+    def relay(self, zt):
+        n = self.net
+        z = n.at[0]
+        d = jnp.where(zt > z, 0, 1)
+        feeds = jnp.where(zt > z, z > 0, z < 3)
+
+        def go():
+            for piece in (0, 1):
+                self.three(piece, zt).wait_recv()
+                add_rows(self.acc.at[n.chip((zt, n.at[1], n.at[2])), self.half(piece)],
+                         [self.zbuf.at[d, zt, self.half(piece)]], self.T // 2)
+                self.three(piece, zt).start()
+
+        pl.when(jnp.logical_and(zt != z, feeds))(go)
+
+    def arrive(self, piece, d):
+        n = self.net
+        z = n.at[0]
+        dst = self.zbuf.at[d, z, self.half(piece)]
+        rcopy(dst, dst, self.s3.at[piece, d, z], self.r3.at[piece, d, z], (n.e, n.c)).wait_recv()
+        add_rows(self.acc.at[n.e, self.half(piece)], [dst], self.T // 2)
+
+    def last(self, out):
+        z = self.net.at[0]
+        for piece in (0, 1):
+            pl.when(z > 0)(lambda piece=piece: self.arrive(piece, 0))
+            pl.when(z < 3)(lambda piece=piece: self.arrive(piece, 1))
+        out[...] = self.acc[self.net.e]
+
+    def drain(self, zt):
+        n = self.net
+        for piece in (0, 1):
+            for idx in (0, 1):
+                self.one(piece, zt, idx).wait_send()
+            self.two(piece, zt).wait_send()
+            pl.when(zt != n.at[0])(lambda piece=piece: self.three(piece, zt).wait_send())
+
+
+NT = (((1,), (1,)), ((), ()))
+TN = (((0,), (0,)), ((), ()))
+
+
+def experts_fused(x, marked, G, w_gate, w_up, w_down, cap, cid):
+    T, D = x.shape
+    E = marked.shape[0]
+    X2, _, Fh = w_gate.shape
+    chips = G.shape[0]
+    nd = 2 * chips
+    S2 = 2 * cap
+    M = 4 * S2
+    CW = 512
+    PR = 64
+    SW = 1024
+
+    def kernel(x_ref, a_ref, g_ref, wg_ref, wu_ref, wd_ref, o_sum, o_part, o_dots, o_rows, o_grows, o_act, o_ggu, N,
+               A, wgu, wdn, Nst, Gst, H, pk, pkt, sw, rowsb, growsb, h1, h2, actw, ggu, yb, To, Tb, dsend,
+               acc, b1, b2, zb, r0, s0, r1, s1, r2, s2, r3, s3, ar, asd, xr, xs, dr, ds_, lsem):
+        net = Net(chips).enter()
+        z, c, e = net.at[0], net.c, net.e
+        me = e * 2 + c
+        copies = [(wg_ref.at[i], wgu.at[i, :, pl.ds(0, Fh)]) for i in range(2)]
+        copies += [(wu_ref.at[i], wgu.at[i, :, pl.ds(Fh, Fh)]) for i in range(2)]
+        copies += [(wd_ref, wdn)]
+        loads = [lambda s=s, d=d, i=i: pltpu.make_async_copy(s, d, lsem.at[i]) for i, (s, d) in enumerate(copies)]
+        own = lambda: pltpu.make_async_copy(x_ref, N.at[e, pl.ds(pl.multiple_of(c * T, T), T)], lsem.at[6])
+        own().start()
+        acopy = lambda: pltpu.make_async_copy(a_ref, A.at[me], lsem.at[7])
+        acopy().start()
+        greet_all(net)
+        own().wait()
+        acopy().wait()
+        ag = Gather22(net, N, T, xr, xs)
+        rs = Reduce22(net, T, acc, b1, b2, zb, (r0, s0, r1, s1, r2, s2, r3, s3))
+        done = []
+        ag.begin()
+        interleave(to_all(net, lambda t: a_ref, lambda s: A.at[s], lambda s: ar.at[s], lambda k: asd.at[k], done))
+        for f in loads:
+            f().start()
+        lane = lax.broadcasted_iota(jnp.int32, (256, 256), 1)
+        sub = lax.broadcasted_iota(jnp.int32, (256, 256), 0)
+        U = jnp.where(jnp.logical_and(sub < lane, sub // 128 == lane // 128), 1.0, 0.0).astype(BF)
+        eye = jnp.where(sub == lane, 1.0, 0.0).astype(BF)
+        place = ((lax.broadcasted_iota(jnp.int32, (8, 256), 1) // 128) * cap).astype(F32)
+        ag.from_z(slot_plane(z, 1))
+        ag.from_two(z)
+        for f in done:
+            f()
+        for f in loads:
+            f().wait()
+
+        saves = lambda i: [
+            (rowsb, o_rows.at[:, i], 8), (growsb, o_grows.at[:, i], 9), (actw, o_act.at[:, i], 10), (ggu, o_ggu.at[:, i], 11)]
+
+        def body(i, _):
+            zt = slot_plane(z, i)
+            zn = slot_plane(z, i + 1)
+            zp = slot_plane(z, i - 1)
+            pltpu.make_async_copy(g_ref.at[pl.ds(zt * 4, 4)], Gst, lsem.at[13]).start()
+            ag.from_three(zt)
+            ag.from_partner(zt)
+            cpn = pltpu.make_async_copy(N.at[pl.ds(zt * 4, 4)], Nst, lsem.at[12])
+            cpn.start()
+            for ch in range(4):
+                for ei in range(2):
+                    for co in range(2):
+                        H[2 * ch + ei:2 * ch + ei + 1, co * 128:(co + 1) * 128] = A[(zt * 4 + ch) * 2 + co, pl.ds(2 * e + ei, 1), :]
+            h = H[...]
+            here = jnp.where(h >= 0.0, 1.0, 0.0)
+            slot = jnp.dot(here.astype(BF), U, preferred_element_type=F32) + place
+            slot = jnp.where(here > 0.0, slot, -1.0)
+            row_id = lax.broadcasted_iota(jnp.int32, (S2, 256), 0).astype(F32)
+            for ch in range(4):
+                for ei in range(2):
+                    q = 2 * ch + ei
+                    hit = row_id == slot[q:q + 1, :]
+                    pk[ch, ei * S2:(ei + 1) * S2, :] = jnp.where(hit, 1.0, 0.0).astype(BF)
+                    wcol = jnp.sum(jnp.where(hit, h[q:q + 1, :], 0.0), axis=1, keepdims=True)
+                    sw[ei, ch * S2:(ch + 1) * S2, :] = jnp.broadcast_to(wcol, (S2, 128))
+                pkt[ch] = lax.dot_general(eye, pk[ch], NT, preferred_element_type=F32).astype(BF)
+
+            def before():
+                for src, dst, s in saves(i):
+                    pltpu.make_async_copy(src, dst, lsem.at[s]).wait()
+
+            pl.when(i > 0)(before)
+            cpn.wait()
+            pltpu.make_async_copy(g_ref.at[pl.ds(zt * 4, 4)], Gst, lsem.at[13]).wait()
+
+            def picks(k, _):
+                ch, j = k // 2, k % 2
+                cols = pl.ds(pl.multiple_of(j * (D // 2), D // 2), D // 2)
+                at = pl.ds(pl.multiple_of(ch * S2, S2), S2)
+                for st, dst in ((Nst, rowsb), (Gst, growsb)):
+                    r = jnp.dot(pk[ch], st[ch, :, cols], preferred_element_type=F32).astype(BF)
+                    dst[0, at, cols] = r[:S2]
+                    dst[1, at, cols] = r[S2:]
+                return 0
+
+            lax.fori_loop(0, 8, picks, 0)
+            pltpu.make_async_copy(rowsb, o_rows.at[:, i], lsem.at[8]).start()
+            pltpu.make_async_copy(growsb, o_grows.at[:, i], lsem.at[9]).start()
+            pl.when(i < 2)(lambda: ag.from_z(slot_plane(z, i + 2)))
+            pl.when(i > 0)(lambda: rs.stage1(zp))
+
+            for ei in range(2):
+                h1[...] = jnp.dot(rowsb[ei], wgu[ei], preferred_element_type=F32)
+                h2[...] = lax.dot_general(growsb[ei], wdn[ei], NT, preferred_element_type=F32)
+
+                def point(k, _):
+                    r = pl.ds(pl.multiple_of(k * PR, PR), PR)
+                    gate, up, ga = h1[r, :Fh], h1[r, Fh:], h2[r, :]
+                    w = sw[ei, r, 0:1]
+                    sig = 1.0 / (1.0 + jnp.exp(-gate))
+                    silu = gate * sig
+                    act = silu * up
+                    actw[ei, r, :] = (w * act).astype(BF)
+                    sw[ei, r, :] = jnp.broadcast_to(jnp.sum(act * ga, axis=1, keepdims=True), (PR, 128))
+                    gact = w * ga
+                    ggu[ei, r, :Fh] = (gact * up * (sig + silu * (1.0 - sig))).astype(BF)
+                    ggu[ei, r, Fh:] = (gact * silu).astype(BF)
+                    return 0
+
+                lax.fori_loop(0, M // PR, point, 0)
+                for ch in range(4):
+                    dcol = sw[ei, ch * S2:(ch + 1) * S2, 0:1]
+                    dd = jnp.sum(pk[ch, ei * S2:(ei + 1) * S2, :].astype(F32) * dcol, axis=0, keepdims=True)
+                    for co in range(2):
+                        dsend[(zt * 4 + ch) * 2 + co, ei:ei + 1, :] = dd[:, co * 128:(co + 1) * 128]
+                if ei == 0:
+                    pl.when(i < 3)(lambda: ag.from_two(zn))
+            pltpu.make_async_copy(actw, o_act.at[:, i], lsem.at[10]).start()
+            pltpu.make_async_copy(ggu, o_ggu.at[:, i], lsem.at[11]).start()
+            pl.when(i > 0)(lambda: rs.stage2(zp))
+
+            def back(j, _):
+                rws = pl.ds(pl.multiple_of(j * CW, CW), CW)
+                for ei in range(2):
+                    r = lax.dot_general(ggu[ei], wgu[ei, rws, :], NT, preferred_element_type=F32).astype(BF)
+                    for ch in range(4):
+                        yb[ch, ei * S2:(ei + 1) * S2, rws] = r[ch * S2:(ch + 1) * S2]
+                return 0
+
+            lax.fori_loop(0, D // CW, back, 0)
+            for ab in rs.ring():
+                ch = ab[0] * 2 + ab[1]
+
+                def spread_back(j, _, ch=ch):
+                    cols = pl.ds(pl.multiple_of(j * SW, SW), SW)
+                    Tb[ch, :, cols] = jnp.dot(pkt[ch], yb[ch, :, cols], preferred_element_type=F32).astype(BF)
+                    return 0
+
+                lax.fori_loop(0, D // SW, spread_back, 0)
+                rs.p_copy(Tb, zt, ab).start()
+
+            def down(j, _):
+                cols = pl.ds(pl.multiple_of(j * CW, CW), CW)
+                for ei in range(2):
+                    r = jnp.dot(actw[ei], wdn[ei, :, cols], preferred_element_type=F32).astype(BF)
+                    for ch in range(4):
+                        yb[ch, ei * S2:(ei + 1) * S2, cols] = r[ch * S2:(ch + 1) * S2]
+                return 0
+
+            lax.fori_loop(0, D // CW, down, 0)
+            rs.stage0(Tb, zt)
+            rs.p_wait_send(Tb, zt)
+            for ch in range(4):
+                cp = lambda ch=ch: pltpu.make_async_copy(To.at[ch % 2], o_part.at[zt * 4 + ch], lsem.at[14 + ch % 2])
+                if ch >= 2:
+                    cp().wait()
+
+                def spread(j, _, ch=ch):
+                    cols = pl.ds(pl.multiple_of(j * SW, SW), SW)
+                    To[ch % 2, :, cols] = jnp.dot(pkt[ch], yb[ch, :, cols], preferred_element_type=F32).astype(BF)
+                    return 0
+
+                lax.fori_loop(0, D // SW, spread, 0)
+                cp().start()
+            for ch in (2, 3):
+                pltpu.make_async_copy(To.at[ch % 2], o_part.at[zt * 4 + ch], lsem.at[14 + ch % 2]).wait()
+            return 0
+
+        lax.fori_loop(0, 4, body, 0)
+        z3 = slot_plane(z, 3)
+        last_done = []
+        own_dots = pltpu.make_async_copy(dsend.at[me], o_dots.at[me], lsem.at[5])
+        own_dots.start()
+        interleave(to_all(net, lambda t: dsend.at[t], lambda s: o_dots.at[s], lambda s: dr.at[s], lambda k: ds_.at[k], last_done))
+        rs.stage1(z3)
+        rs.relay(slot_plane(z, 2))
+        rs.stage2(z3)
+        rs.relay(z3)
+        rs.relay(slot_plane(z, 1))
+        rs.last(o_sum)
+        own_dots.wait()
+        for f in last_done:
+            f()
+        for src, dst, s in saves(3):
+            pltpu.make_async_copy(src, dst, lsem.at[s]).wait()
+
+        def finish(i, _):
+            ag.drain(i)
+            rs.drain(slot_plane(z, i))
+            return 0
+
+        lax.fori_loop(0, 4, finish, 0)
+
+    S = jax.ShapeDtypeStruct
+    V = pltpu.VMEM
+    return pl.pallas_call(
+        kernel,
+        out_shape=(S((T, D), BF), S((chips, 2 * T, D), BF), S((nd, 8, 128), F32), S((2, 4, M, D), BF), S((2, 4, M, D), BF),
+                   S((2, 4, M, Fh), BF), S((2, 4, M, 2 * Fh), BF), S((chips, 2 * T, D), BF)),
+        in_specs=[VM, VM, ANY, ANY, ANY, ANY], out_specs=(VM, ANY, VM, ANY, ANY, ANY, ANY, ANY),
+        scratch_shapes=[
+            V((nd, E, T), F32), V((2, D, 2 * Fh), BF), V((2, Fh, D), BF), V((4, 2 * T, D), BF), V((4, 2 * T, D), BF),
+            V((8, 2 * T), F32), V((4, 2 * S2, 2 * T), BF), V((4, 2 * T, 2 * S2), BF), V((2, M, 128), F32), V((2, M, D), BF), V((2, M, D), BF),
+            V((M, 2 * Fh), F32), V((M, Fh), F32), V((2, M, Fh), BF), V((2, M, 2 * Fh), BF), V((4, 2 * S2, D), BF),
+            V((2, 2 * T, D), BF), V((4, 2 * T, D), BF), V((nd, 8, 128), F32)]
+        + Reduce22.scratch(T, D)
+        + [DMA((nd,)), DMA((nd,)), DMA((2, chips, 2)), DMA((2, chips, 5)), DMA((nd,)), DMA((nd,)), DMA((16,))],
+        compiler_params=params(cid, 64 << 20), name="experts",
+    )(x, marked, G, w_gate, w_up, w_down)[:7]
+
+
+def column_sum_gather(n_expert, part, x, cid):
+    _, _, T, D = part.shape
+
+    def kernel(p_ref, x_ref, o_ref, N, acc, buf, fin, rsem, ssem, xr, xs, lsem):
+        net = Net(n_expert).enter()
+        z, e, c = net.at[0], net.e, net.c
+        own = lambda: pltpu.make_async_copy(x_ref, N.at[e, pl.ds(pl.multiple_of(c * T, T), T)], lsem)
+        own().start()
+        greet(net, (0, 1, 2))
+        own().wait()
+        ag = Gather22(net, N, T, xr, xs)
+        done = []
+
+        def gather():
+            ag.begin()
+            yield
+            for i in range(4):
+                if i < 3:
+                    ag.from_z(slot_plane(z, i + 1))
+                    yield
+                ag.from_two(slot_plane(z, i))
+                yield
+                if i:
+                    ag.from_three(slot_plane(z, i - 1))
+                    yield
+            ag.from_three(slot_plane(z, 3))
+            for i in range(4):
+                ag.from_partner(slot_plane(z, i))
+
+        interleave(
+            col_rs(net, lambda s, h: p_ref.at[s, h], o_ref, lambda w, s, h: acc.at[w, s, h], lambda w, s, h: buf.at[w, s, h],
+                   lambda i: fin.at[i], lambda w, s, h: rsem.at[w, s, h], lambda w, s, h: ssem.at[w, s, h], T, done),
+            gather())
+        for f in done:
+            f()
+
+        def finish(i, _):
+            ag.drain(i)
+            return 0
+
+        lax.fori_loop(0, 4, finish, 0)
+
+    S = jax.ShapeDtypeStruct
+    V = pltpu.VMEM
+    return pl.pallas_call(
+        kernel, out_shape=(S((T, D), BF), S((n_expert, 2 * T, D), BF)), in_specs=[VM, VM], out_specs=(VM, ANY),
+        scratch_shapes=[V((2, 2, 2, T, D), BF), V((2, 2, 2, T, D), BF), V((2, T, D), BF),
+                        DMA((3, 2, 2)), DMA((3, 2, 2)), DMA((2, n_expert, 2)), DMA((2, n_expert, 5)), DMA],
+        compiler_params=params(cid, 40 << 20), name="column_sum_gather",
+    )(part, x)
+
+
+def reduce_and_column(n_expert, part, x, cid):
+    T, D = x.shape
+
+    def kernel(p_ref, x_ref, o_ref, X, Tb, acc, b1, b2, zb, r0, s0, r1, s1, r2, s2, r3, s3, xr, xs, lsem):
+        net = Net(n_expert).enter()
+        z = net.at[0]
+        load = lambda i: pltpu.make_async_copy(p_ref.at[pl.ds(slot_plane(z, 3 - i) * 4, 4)], Tb.at[i % 2], lsem.at[i % 2])
+        load(0).start()
+        greet(net, (0, 1, 2))
+        rs = Reduce22(net, T, acc, b1, b2, zb, (r0, s0, r1, s1, r2, s2, r3, s3))
+        done = []
+        far = lambda i: slot_plane(z, 3 - i)
+
+        def reduce():
+            for i in range(4):
+                if i:
+                    rs.p_wait_send(Tb.at[(i - 1) % 2], far(i - 1))
+                if i < 3:
+                    load(i + 1).start()
+                load(i).wait()
+                rs.p_send(Tb.at[i % 2], far(i))
+                yield
+                rs.stage0(Tb.at[i % 2], far(i))
+                yield
+                if i:
+                    rs.stage1(far(i - 1))
+                    yield
+                if i > 1:
+                    rs.stage2(far(i - 2))
+                    yield
+            rs.p_wait_send(Tb.at[1], far(3))
+            rs.stage1(far(3))
+            rs.stage2(far(2))
+            yield
+            for i in (0, 1, 2):
+                rs.relay(far(i))
+            rs.stage2(far(3))
+            rs.last(o_ref)
+
+        interleave(
+            reduce(),
+            col_ag(net, x_ref, lambda s, h: X.at[s, h], lambda s, h: xr.at[s, h], lambda w, s, h: xs.at[w, s, h], done))
+        for f in done:
+            f()
+
+        def finish(i, _):
+            rs.drain(slot_plane(z, i))
+            return 0
+
+        lax.fori_loop(0, 4, finish, 0)
+
+    S = jax.ShapeDtypeStruct
+    return pl.pallas_call(
+        kernel, out_shape=(S((T, D), BF), S((2, 2, T, D), BF)), in_specs=[ANY, VM], out_specs=(VM, ANY),
+        scratch_shapes=[pltpu.VMEM((2, 4, 2 * T, D), BF)] + Reduce22.scratch(T, D) + [DMA((2, 2)), DMA((3, 2, 2)), DMA((2,))],
+        compiler_params=params(cid, 60 << 20), name="reduce_and_column",
+    )(part, x)
+
+
 MODEL_WIDTH = 2048
 QUERY_HEADS = 32
 KEY_VALUE_HEADS = 4
@@ -883,82 +1500,10 @@
     return jnp.einsum(spec, *args, preferred_element_type=F32)
 
 
-def local(
-    n_expert, tokens, routes, documents, w_query, key_projection, value_projection, w_out, w_router,
-    gain_attn, gain_ffn, gain_query, gain_key, w_gate, w_up, w_down, cotangent,
-):
-    Z = KEY_VALUE_HEADS
-    plane = n_expert // Z
+def experts_wide(n_expert, second_in, marked, G, w_gate, w_up, w_down, capacity):
+    T, D = second_in.shape
     nd = 2 * n_expert
-    T, D = tokens.shape
-    R, HR, E = w_query.shape[0], w_out.shape[0], w_router.shape[1]
-    Q = gain_query.shape[0]
-    KV = HEAD_SIZE
-    GQ = GROUP * HEAD_SIZE
-    e, c = lax.axis_index("expert"), lax.axis_index("context")
-    z, p = e // plane, e % plane
-    capacity = T * TOP * 5 // (4 * E)
-    score_scale = HEAD_SIZE ** (-0.5)
-
-    wqkv = jnp.concatenate(
-        [w_query.reshape(R, Z, GQ), key_projection.reshape(R, Z, KV), value_projection.reshape(R, Z, KV)], axis=-1
-    ).transpose(1, 0, 2)
-    width = -(-(E + 4) // 128) * 128
-    pad = lambda v: jnp.pad(v, (0, R - v.shape[0]))[:, None]
-    head = jnp.concatenate(
-        [w_router, gain_attn[:, None], gain_ffn[:, None], pad(gain_query), pad(gain_key), jnp.zeros((R, width - E - 4), BF)], axis=1
-    )
-    docs_own = lax.dynamic_slice_in_dim(documents[0], c * T, T).astype(BF)[None]
-    docs_own = jnp.pad(docs_own, ((0, 15), (0, width - T)))
-    aux = jnp.concatenate([head, docs_own], axis=0)
-    X, W, O, A, G = gather_start(n_expert, tokens, wqkv, w_out, aux, cotangent, 0)
-    W = W.reshape(D, GQ + 2 * KV)
-    O = O.reshape(GQ, D)
-    table = A[:, :R].reshape(D, width)
-    router_weight = table[:, :E]
-    attn_gain = table[:, E].astype(F32)
-    ffn_gain = table[:, E + 1].astype(F32)
-    query_gain = A[:, :Q, E + 2].reshape(HEAD_SIZE).astype(F32)
-    key_gain = A[:, :Q, E + 3].reshape(HEAD_SIZE).astype(F32)
-    docs = A[:, R, :T].reshape(Z, plane, 2 * T)
-    docs = lax.dynamic_slice(docs, (2 * c, p, 0), (2, 1, 2 * T)).reshape(2, 2 * T)
-
-    L = 2 * T
-    x = X.reshape(2 * L, D).astype(F32)
-    normed, inverse_attn = norm_parts(x, attn_gain)
-    first_in = normed.astype(BF)
-    raw = mm(first_in, W)
-    query_raw = raw[:, :GQ].reshape(2, L, GROUP, HEAD_SIZE)
-    key_raw = raw[:, GQ:GQ + KV].reshape(2, L, HEAD_SIZE)
-    value = raw[:, GQ + KV:].reshape(2, L, HEAD_SIZE).astype(BF)
-    cos, sin = rope_tables(jnp.arange(L, dtype=jnp.int32))
-    qcos, qsin = cos[:, None, :], sin[:, None, :]
-    query_normed, query_inverse = norm_parts(query_raw, query_gain)
-    queries = rotate(query_normed, qcos, qsin).astype(BF)
-    key_normed, key_inverse = norm_parts(key_raw, key_gain)
-    keys = rotate(key_normed, cos, sin).astype(BF)
-    places = jnp.arange(L, dtype=jnp.int32)
-    allowed = (places[:, None] >= places[None, :])[None] & (docs[:, :, None] == docs[:, None, :])
-    scores = ein("sqhd,skd->shqk", queries, keys) * score_scale
-    scores = jnp.where(allowed[:, None], scores, -1e30)
-    top = jnp.max(scores, axis=-1, keepdims=True)
-    ex = jnp.exp(scores - top)
-    probs = ex / jnp.sum(ex, axis=-1, keepdims=True)
-    probs_low = probs.astype(BF)
-    attended = ein("shqk,skd->sqhd", probs_low, value).reshape(2 * L, GQ).astype(BF)
-    part = mm(attended, O).astype(BF).reshape(2, 2, T, D)
-    middle = tokens.astype(F32) + column_sum(n_expert, part, 1).astype(F32)
-
-    normed_ffn, inverse_ffn = norm_parts(middle, ffn_gain)
-    second_in = normed_ffn.astype(BF)
-    logits = mm(second_in, router_weight)
-    ids = jnp.arange(E, dtype=jnp.int32)
-    chosen = jnp.any(routes[:, :, None] == ids[None, None, :], axis=1)
-    masked = jnp.where(chosen, logits, -jnp.inf)
-    best = jnp.max(masked, axis=-1, keepdims=True)
-    ew = jnp.where(chosen, jnp.exp(logits - best), 0.0)
-    weights = ew / jnp.sum(ew, axis=-1, keepdims=True)
-    marked = jnp.where(chosen, weights, -1.0).T
+    e = lax.axis_index("expert")
     N, M = gather_all(n_expert, second_in, marked, 2)
 
     mine = lax.dynamic_slice(M, (0, EXP_DEV * e, 0), (nd, EXP_DEV, T))
@@ -1006,7 +1551,104 @@
     back_sum = summed(back_part, 8)
     out_sum = summed(out_part, 9)
 
-    block_out = (middle + out_sum).astype(BF)
+    return back_sum, out_sum, dots_in, gate_grad, up_grad, down_grad
+
+
+def local(
+    n_expert, tokens, routes, documents, w_query, key_projection, value_projection, w_out, w_router,
+    gain_attn, gain_ffn, gain_query, gain_key, w_gate, w_up, w_down, cotangent,
+):
+    Z = KEY_VALUE_HEADS
+    plane = n_expert // Z
+    nd = 2 * n_expert
+    T, D = tokens.shape
+    R, HR, E = w_query.shape[0], w_out.shape[0], w_router.shape[1]
+    Q = gain_query.shape[0]
+    KV = HEAD_SIZE
+    GQ = GROUP * HEAD_SIZE
+    e, c = lax.axis_index("expert"), lax.axis_index("context")
+    z, p = e // plane, e % plane
+    capacity = T * TOP * 5 // (4 * E)
+    score_scale = HEAD_SIZE ** (-0.5)
+
+    wqkv = jnp.concatenate(
+        [w_query.reshape(R, Z, GQ), key_projection.reshape(R, Z, KV), value_projection.reshape(R, Z, KV)], axis=-1
+    ).transpose(1, 0, 2)
+    width = -(-(E + 4) // 128) * 128
+    pad = lambda v: jnp.pad(v, (0, R - v.shape[0]))[:, None]
+    head = jnp.concatenate(
+        [w_router, gain_attn[:, None], gain_ffn[:, None], pad(gain_query), pad(gain_key), jnp.zeros((R, width - E - 4), BF)], axis=1
+    )
+    docs_own = lax.dynamic_slice_in_dim(documents[0], c * T, T).astype(BF)[None]
+    docs_own = jnp.pad(docs_own, ((0, 15), (0, width - T)))
+    aux = jnp.concatenate([head, docs_own], axis=0)
+    small_plane = plane == 4
+    X, W, O, A, *G = gather_start(n_expert, tokens, wqkv, w_out, aux, None if small_plane else cotangent, 0)
+    W = W.reshape(D, GQ + 2 * KV)
+    O = O.reshape(GQ, D)
+    table = A[:, :R].reshape(D, width)
+    router_weight = table[:, :E]
+    attn_gain = table[:, E].astype(F32)
+    ffn_gain = table[:, E + 1].astype(F32)
+    query_gain = A[:, :Q, E + 2].reshape(HEAD_SIZE).astype(F32)
+    key_gain = A[:, :Q, E + 3].reshape(HEAD_SIZE).astype(F32)
+    docs = A[:, R, :T].reshape(Z, plane, 2 * T)
+    docs = lax.dynamic_slice(docs, (2 * c, p, 0), (2, 1, 2 * T)).reshape(2, 2 * T)
+
+    L = 2 * T
+    x = X.reshape(2 * L, D).astype(F32)
+    normed, inverse_attn = norm_parts(x, attn_gain)
+    first_in = normed.astype(BF)
+    raw = mm(first_in, W)
+    query_raw = raw[:, :GQ].reshape(2, L, GROUP, HEAD_SIZE)
+    key_raw = raw[:, GQ:GQ + KV].reshape(2, L, HEAD_SIZE)
+    value = raw[:, GQ + KV:].reshape(2, L, HEAD_SIZE).astype(BF)
+    cos, sin = rope_tables(jnp.arange(L, dtype=jnp.int32))
+    qcos, qsin = cos[:, None, :], sin[:, None, :]
+    query_normed, query_inverse = norm_parts(query_raw, query_gain)
+    queries = rotate(query_normed, qcos, qsin).astype(BF)
+    key_normed, key_inverse = norm_parts(key_raw, key_gain)
+    keys = rotate(key_normed, cos, sin).astype(BF)
+    places = jnp.arange(L, dtype=jnp.int32)
+    allowed = (places[:, None] >= places[None, :])[None] & (docs[:, :, None] == docs[:, None, :])
+    scores = ein("sqhd,skd->shqk", queries, keys) * score_scale
+    scores = jnp.where(allowed[:, None], scores, -1e30)
+    top = jnp.max(scores, axis=-1, keepdims=True)
+    ex = jnp.exp(scores - top)
+    probs = ex / jnp.sum(ex, axis=-1, keepdims=True)
+    probs_low = probs.astype(BF)
+    attended = ein("shqk,skd->sqhd", probs_low, value).reshape(2 * L, GQ).astype(BF)
+    part = mm(attended, O).astype(BF).reshape(2, 2, T, D)
+    if small_plane:
+        attn_sum, G = column_sum_gather(n_expert, part, cotangent, 1)
+    else:
+        attn_sum, G = column_sum(n_expert, part, 1), G[0]
+    middle = tokens.astype(F32) + attn_sum.astype(F32)
+
+    normed_ffn, inverse_ffn = norm_parts(middle, ffn_gain)
+    second_in = normed_ffn.astype(BF)
+    logits = mm(second_in, router_weight)
+    ids = jnp.arange(E, dtype=jnp.int32)
+    chosen = jnp.any(routes[:, :, None] == ids[None, None, :], axis=1)
+    masked = jnp.where(chosen, logits, -jnp.inf)
+    best = jnp.max(masked, axis=-1, keepdims=True)
+    ew = jnp.where(chosen, jnp.exp(logits - best), 0.0)
+    weights = ew / jnp.sum(ew, axis=-1, keepdims=True)
+    marked = jnp.where(chosen, weights, -1.0).T
+    if small_plane:
+        back_sum, out_part, dots_in, rows, g_rows, act_w, gate_up = experts_fused(
+            second_in, marked, G, w_gate, w_up, w_down, capacity, 3)
+        flat = lambda v: v.reshape(EXP_DEV, -1, v.shape[-1])
+        Fh = act_w.shape[-1]
+        rows = flat(rows)
+        down_grad = ein("emf,emd->efd", flat(act_w), flat(g_rows))
+        gate_grad = ein("emd,emf->edf", rows, flat(gate_up[..., :Fh]))
+        up_grad = ein("emd,emf->edf", rows, flat(gate_up[..., Fh:]))
+    else:
+        back_sum, out_sum, dots_in, gate_grad, up_grad, down_grad = experts_wide(
+            n_expert, second_in, marked, G, w_gate, w_up, w_down, capacity)
+    back_sum = back_sum.astype(F32)
+
     grad_result = cotangent.astype(F32)
     grad_weights = jnp.sum(dots_in[:, :EXP_DEV].reshape(n_expert, 2, EXP_DEV, T), axis=1).reshape(E, T).T
     grad_chosen = weights * (grad_weights - jnp.sum(weights * grad_weights, axis=-1, keepdims=True))
@@ -1017,7 +1659,12 @@
     ffn_gain_grad = jnp.sum(ffn_terms, axis=0)
     grad_middle = grad_result + grad_middle_norm
 
-    GA = column_gather(n_expert, grad_middle.astype(BF), 6).reshape(2 * L, D)
+    if small_plane:
+        out_sum, GA = reduce_and_column(n_expert, out_part, grad_middle.astype(BF), 6)
+    else:
+        GA = column_gather(n_expert, grad_middle.astype(BF), 6)
+    block_out = (middle + out_sum.astype(F32)).astype(BF)
+    GA = GA.reshape(2 * L, D)
     out_grad = mm(attended.T, GA)
     grad_attended = ein("td,fd->tf", GA, O).astype(BF).reshape(2, L, GROUP, HEAD_SIZE)
     grad_probs = ein("sqhd,skd->shqk", grad_attended, value)

time: 961 us -> 712 us (0.74)
  matrix products: 197 us -> 68.9 us
  Pallas kernels: 642 us -> 564 us
  local copies, waits for them, and re-layouts: 64.1 us -> 37.1 us
  other arithmetic: 45.1 us -> 30.2 us
    dot_general x21 -> x10, matrix products: 167 us -> 44 us  [ein(): return jnp.einsum(spec, *args, preferred_element_type=F32)]
    pallas_call x1, Pallas kernels: 127 us -> 74.5 us  [gather_start(): pl.pallas_call(kernel, out_shape=(S((2, 2, T, D), BF), S((Z, plane, 2, R,...]
    pallas_call x6 -> x3, Pallas kernels: 432 us -> 404 us  [the longest x1 224 us: experts_fused(): pl.pallas_call(kernel, out_shape=(S((T, D), BF), S((chips, 2 * T, D), BF)...]
    convert_element_type x3 -> x0, local copies, waits for them, and re-layouts: 20.3 us -> none  [the longest x1 10.2 us: local(): grad_rows = flat((slot_weight * g_rows).astype(BF))]
where the time goes in v2:
time: 712 us; the launch traced here: 703 us
  Pallas kernels  564 us (79%)
  matrix products  68.9 us (10%)
  local copies, waits for them, and re-layouts  37.1 us (5%)
  other arithmetic  30.2 us (4%)
    pallas_call x1, Pallas kernels, experts_fused(): pl.pallas_call(kernel, out_shape=(S((T, D), BF), S((chips, 2 * T, D), BF)...  224 us
    pallas_call x1, Pallas kernels, reduce_and_column(): pl.pallas_call(kernel, out_shape=(S((T, D), BF), S((2, 2, T, D), BF)), in...  93.3 us
    pallas_call x1, Pallas kernels, column_sum_gather(): pl.pallas_call(kernel, out_shape=(S((T, D), BF), S((n_expert, 2 * T, D),...  86.9 us
    pallas_call x1, Pallas kernels, reduce_end(): pl.pallas_call(kernel, out_shape=(S((T, D), BF), S((Z, R, C), BF), S((HR,...  85.5 us
    pallas_call x1, Pallas kernels, gather_start(): pl.pallas_call(kernel, out_shape=(S((2, 2, T, D), BF), S((Z, plane, 2, R,...  74.5 us
    dot_general x10, matrix products, ein(): return jnp.einsum(spec, *args, preferred_element_type=F32)  44 us
    dot_general x7, matrix products, mm(): return jnp.dot(a, b, preferred_element_type=F32)  20.8 us

profile of v2, /device:TPU:13, one launch (start us, length us, event | category | flops | bytes accessed | tf_op | source)
XLA Modules:
  0.0 702.5 jit_solution(6852236684022770596)
XLA Ops:
  5.9 0.9 copy_bitcast_fusion.3
  6.8 1.1 copy.298
  8.8 74.5 %gather_start.1 = (bf16[2,2,128,2048]{3,2,1,0:T(8,128)(2,1)}, bf16[4,4,2,64,1280]{4,3,2,1,0:T(8,128)(2,1)}, bf16[4,2,128,2048]{3,2,1,0:T(8,128)(2,1)}, bf16[32,80,128]{2,1,0:T(8,128)(2,1)}) custom-call(bf16[128,2048]{1,0:T(8,128)(2,1)} %refs_0_.1, bf16[4,64,1280]{2,1,0:T(8,128)(2,1)} %maximum_bitcast_fusion.refs_1_, bf16[128,2048]{1,0:T(8,128)(2,1)} %refs_2_.1, ...), custom_call_target="tpu_custom_call" | custom-call | tf_op jit(solution)/shard_map/gather_start/pallas_call | solution.py:664
  84.5 1.1 slice.89
  85.6 1.7 slice_convert_fusion
  87.2 1.6 copy.269
  89.9 1.4 copy-done.77
  91.3 2.9 fusion.64
  94.5 1.2 copy-done.9
  96.9 1.1 convert_reduce_fusion
  100.2 1.3 multiply_reduce_fusion.7
  102.0 4.1 fusion.63
  106.2 1.0 slice.177
  107.8 2.7 fusion.22
  110.5 1.2 copy.210
  111.8 1.0 copy-done.34
  112.8 4.6 convolution_convert_fusion.2
  117.4 86.9 %column_sum_gather.1 = (bf16[128,2048]{1,0:T(8,128)(2,1)S(1)}, bf16[16,256,2048]{2,1,0:T(8,128)(2,1)}) custom-call(bf16[2,2,128,2048]{3,2,1,0:T(8,128)(2,1)S(1)} %bitcast.210, bf16[128,2048]{1,0:T(8,128)(2,1)S(1)} %copy-done.2), custom_call_target="tpu_custom_call" | custom-call | tf_op jit(solution)/shard_map/column_sum_gather/pallas_call | solution.py:1383
  206.8 223.9 %experts.1 = (bf16[128,2048]{1,0:T(8,128)(2,1)}, bf16[16,256,2048]{2,1,0:T(8,128)(2,1)}, f32[32,8,128]{2,1,0:T(8,128)}, bf16[2,4,320,2048]{3,2,1,0:T(8,128)(2,1)...) custom-call(bf16[128,2048]{1,0:T(8,128)(2,1)} %copy-done.12, ...), custom_call_target="tpu_custom_call" | custom-call | tf_op jit(solution)/shard_map/experts/pallas_call | solution.py:1323
  430.8 11.7 %fusion.68 = f32[2,384,2048]{2,1,0:T(8,128)} fusion(bf16[2,1280,384]{2,1,0:T(8,128)(2,1)} %bitcast.215, bf16[2,1280,2048]{2,1,0:T(8,128)(2,1)} %bitcast.214), kind=kOutput, calls=%fused_computation.167 | convolution fusion | flops 4026531840 | bytes 18743296 | tf_op jit(solution)/shard_map/emf,emd->efd/dot_general | solution.py:1500
  443.2 7.7 %fusion.67 = f32[2,2048,384]{2,1,0:T(8,128)} fusion(bf16[2,1280,2048]{2,1,0:T(8,128)(2,1)S(1)} %bitcast.261, bf16[2,1280,384]{2,1,0:T(8,128)(2,1)S(1)} %bitcast.232), kind=kOutput, calls=%fused_computation.166 | convolution fusion | flops 4026531840 | bytes 18743296 | tf_op jit(solution)/shard_map/emd,emf->edf/dot_general | solution.py:1500
  450.8 7.9 %fusion.66 = f32[2,2048,384]{2,1,0:T(8,128)} fusion(bf16[2,1280,2048]{2,1,0:T(8,128)(2,1)S(1)} %bitcast.262, bf16[2,1280,384]{2,1,0:T(8,128)(2,1)S(1)} %bitcast.231), kind=kOutput, calls=%fused_computation.165 | convolution fusion | flops 4026531840 | bytes 18743296 | tf_op jit(solution)/shard_map/emd,emf->edf/dot_general | solution.py:1500
  458.8 1.0 bitcast_reduce_fusion
  460.2 1.2 reshape.436
  461.5 1.8 multiply_reduce_fusion.2
  463.3 1.3 fusion.59.x_ref
  464.6 93.3 %reduce_and_column.1 = (bf16[128,2048]{1,0:T(8,128)(2,1)}, bf16[2,2,128,2048]{3,2,1,0:T(8,128)(2,1)}) custom-call(bf16[16,256,2048]{2,1,0:T(8,128)(2,1)} %get-tuple-element.39.p_ref, bf16[128,2048]{1,0:T(8,128)(2,1)} %fusion.59.x_ref), custom_call_target="tpu_custom_call" | custom-call | tf_op jit(solution)/shard_map/reduce_and_column/pallas_call | solution.py:1443
  557.9 5.3 fusion.21
  564.2 1.3 fusion.8
  565.5 0.9 fusion.10
  566.5 1.0 multiply_bitcast_fusion
  567.5 1.0 multiply_add_fusion
  569.1 2.0 multiply_reduce_fusion
  572.0 3.0 mul.696
  575.0 2.6 copy.217
  578.4 1.7 mul.650.clone
  580.2 4.3 fusion.17
  584.5 0.9 fusion.23
  585.6 2.0 multiply_reduce_fusion.5
  587.7 1.3 multiply_convert_fusion.1
  590.6 4.7 fusion.7
  596.7 6.1 convolution_convert_fusion.1
  602.8 4.7 convolution_convert_fusion
  607.6 85.5 %reduce_end.1 = (bf16[128,2048]{1,0:T(8,128)(2,1)}, bf16[4,64,1280]{2,1,0:T(8,128)(2,1)}, bf16[128,2048]{1,0:T(8,128)(2,1)}, f32[32,24,128]{2,1,0:T(8,128)}) custom-call(bf16[2,2,128,2048]{3,2,1,0:T(8,128)(2,1)} %bitcast.230, bf16[4,4,2,64,1280]{4,3,2,1,0:T(8,128)(2,1)} %bitcast.222, bf16[4,2,128,2048]{3,2,1,0:T(8,128)(2,1)} %bitcast.223, ...), custom_call_target="tpu_custom_call" | custom-call | tf_op jit(solution)/shard_map/reduce_end/pallas_call | solution.py:828
  693.1 1.2 convert_element_type.271
  694.4 1.1 copy.259
  697.2 2.1 fusion.30
  699.3 1.1 convert_element_type.272
  (239 shorter events, 26.4 us)
Async XLA Ops:
  85.6 119.7 %copy-start.10 = (bf16[32,64,128]{2,1,0:T(8,128)(2,1)}, bf16[32,64,128]{2,1,0:T(8,128)(2,1)S(1)}, u32[]{:S(2)}) copy-start(bf16[32,64,128]{2,1,0:T(8,128)(2,1)S(1)} %slice.89) | copy-start | bytes 1572868
  85.6 3.2 copy-start.14
  88.8 2.5 copy-start.77
  96.2 2.6 copy-start.4
  99.4 2.4 copy-start.28
  99.4 2.4 copy-start.30
  100.2 5.9 copy-start.18
  100.2 5.9 copy-start.20
  101.5 4.6 copy-start.59
  101.7 4.5 copy-start.65
  102.0 4.1 copy-start.42
  102.0 4.1 copy-start.44
  106.2 4.4 copy-start.61
  112.8 4.6 copy-start.2
  117.3 87.0 %copy-start.6 = (bf16[128,2048]{1,0:T(8,128)(2,1)S(1)}, bf16[128,2048]{1,0:T(8,128)(2,1)}, u32[]{:S(2)}) copy-start(bf16[128,2048]{1,0:T(8,128)(2,1)} %refs_0_.1) | copy-start | bytes 1572868
  117.4 87.3 %copy-start.24 = (f32[2048,1]{1,0:T(8,128)S(1)}, f32[2048,1]{1,0:T(8,128)}, u32[]{:S(2)}) copy-start(f32[2048,1]{1,0:T(8,128)} %get-tuple-element.150) | copy-start | bytes 24580
  204.6 2.2 copy-start.73
  430.8 11.7 %copy-start.27 = (bf16[2,4,320,768]{3,2,1,0:T(8,128)(2,1)S(1)}, bf16[2,4,320,768]{3,2,1,0:T(8,128)(2,1)}, u32[]{:S(2)}) copy-start(bf16[2,4,320,768]{3,2,1,0:T(8,128)(2,1)} %get-tuple-element.49) | copy-start | bytes 11796484
  430.8 12.4 %copy-start.76 = (bf16[2,4,320,2048]{3,2,1,0:T(8,128)(2,1)S(1)}, bf16[2,4,320,2048]{3,2,1,0:T(8,128)(2,1)}, u32[]{:S(2)}) copy-start(bf16[2,4,320,2048]{3,2,1,0:T(8,128)(2,1)} %get-tuple-element.48) | copy-start | bytes 31457284
  450.8 9.0 %copy-start.47 = (f32[128,32]{0,1:T(8,128)S(1)}, f32[128,32]{0,1:T(8,128)}, u32[]{:S(2)}) copy-start(f32[128,32]{0,1:T(8,128)} %copy-done.46) | copy-start | bytes 49156
  450.8 9.0 %copy-start.52 = (pred[128,32]{0,1:T(8,128)(4,1)S(1)}, pred[128,32]{0,1:T(8,128)(4,1)}, u32[]{:S(2)}) copy-start(pred[128,32]{0,1:T(8,128)(4,1)} %copy-done.51) | copy-start | bytes 12292
  450.8 9.0 %copy-start.64 = (f32[128]{0:T(128)S(1)}, f32[128]{0:T(128)}, u32[]{:S(2)}) copy-start(f32[128]{0:T(128)} %copy-done.63) | copy-start | bytes 1540
  450.8 9.0 %copy-start.68 = (f32[128]{0:T(128)S(1)}, f32[128]{0:T(128)}, u32[]{:S(2)}) copy-start(f32[128]{0:T(128)} %copy-done.67) | copy-start | bytes 1540
  450.8 9.1 %copy-start.13 = (bf16[128,2048]{1,0:T(8,128)(2,1)S(1)}, bf16[128,2048]{1,0:T(8,128)(2,1)}, u32[]{:S(2)}) copy-start(bf16[128,2048]{1,0:T(8,128)(2,1)} %copy-done.12) | copy-start | bytes 1572868
  458.7 2.7 copy-start.1
  458.7 2.7 copy-start.7
  458.7 2.7 copy-start.11
  458.7 2.7 copy-start.56
  458.7 2.7 copy-start.74
  557.9 5.7 copy-start.25
  572.0 3.0 copy-start.17
  575.0 2.6 copy-start.50
  580.1 4.4 copy-start.19
  580.1 4.4 copy-start.21
  580.2 9.7 %slice-start = ((s8[5242880]{0:T(1024)(128)(4,1)}), s8[4194304]{0:T(1024)(128)(4,1)S(1)}, s32[]{:S(2)}) async-start(s8[5242880]{0:T(1024)(128)(4,1)} %bitcast.264), calls=%async_computation | async-start | bytes 8388608
  584.5 5.3 copy-start.38
  584.5 4.5 copy-start.26
  585.4 3.6 copy-start.37
  587.7 2.1 slice-start.1
  590.6 5.1 copy-start.33
  596.7 6.2 copy-start.39
  596.7 6.2 copy-start.78
  694.4 2.5 copy-start.8
  694.4 2.5 copy-start.32
  694.4 2.7 copy-start.23
  694.4 2.7 copy-start.40
  697.2 2.1 copy-start.41
  697.2 3.2 copy-start.48
  (33 other events, 40.3 us)

commit v3 on v2

--- a/solution.py
+++ b/solution.py
@@ -1447,6 +1447,294 @@
     )(part, x)
 
 
+def head_rotated(v, gain, cos, sin):
+    inv = lax.rsqrt(jnp.mean(v * v, axis=-1, keepdims=True) + epsilon)
+    n = v * inv * gain
+    return n * cos + pltpu.roll(n, HEAD_SIZE // 2, 1) * sin, inv
+
+
+def head_back(v, gain, cos, sin, grad):
+    inv = lax.rsqrt(jnp.mean(v * v, axis=-1, keepdims=True) + epsilon)
+    g = grad * cos - pltpu.roll(grad, HEAD_SIZE // 2, 1) * sin
+    s = g * gain
+    return inv * (s - v * (inv * inv * jnp.mean(s * v, axis=-1, keepdims=True))), g * v * inv
+
+
+def softmax_rows(q, k, allowed):
+    s = lax.dot_general(q, k, NT, preferred_element_type=F32) * (HEAD_SIZE ** -0.5)
+    s = jnp.where(allowed > 0.0, s, -1e30)
+    ex = jnp.exp(s - jnp.max(s, axis=-1, keepdims=True))
+    return ex * (1.0 / jnp.sum(ex, axis=-1, keepdims=True))
+
+
+def attention_forward(n_expert, X, W, O, gain, gq, gk, cos, sin, allowed, cot, cid):
+    T, D = cot.shape
+    L = 2 * T
+    rows = 2 * L
+    GQ = O.shape[0]
+    heads = GQ // HEAD_SIZE
+    C = W.shape[1]
+    HS = HEAD_SIZE
+
+    def kernel(X_ref, W_ref, O_ref, gain_ref, gq_ref, gk_ref, cos_ref, sin_ref, ok_ref, x_ref,
+               o_ref, N, first, raw, qs, ks, vs, att, part, acc, buf, fin, rsem, ssem, xr, xs, lsem):
+        net = Net(n_expert).enter()
+        z, e, c = net.at[0], net.e, net.c
+        own = lambda: pltpu.make_async_copy(x_ref, N.at[e, pl.ds(pl.multiple_of(c * T, T), T)], lsem)
+        own().start()
+        greet(net, (0, 1, 2))
+        own().wait()
+        ag = Gather22(net, N, T, xr, xs)
+        done = []
+
+        def gather():
+            ag.begin()
+            yield
+            for i in range(4):
+                if i < 3:
+                    ag.from_z(slot_plane(z, i + 1))
+                    yield
+                ag.from_two(slot_plane(z, i))
+                yield
+                if i:
+                    ag.from_three(slot_plane(z, i - 1))
+                    yield
+            ag.from_three(slot_plane(z, 3))
+            for i in range(4):
+                ag.from_partner(slot_plane(z, i))
+
+        def compute():
+            def norm(i, _):
+                r = pl.ds(pl.multiple_of(i * 32, 32), 32)
+                x = X_ref[r, :].astype(F32)
+                inv = lax.rsqrt(jnp.mean(x * x, axis=-1, keepdims=True) + epsilon)
+                first[r, :] = (x * inv * gain_ref[...]).astype(BF)
+                return 0
+
+            lax.fori_loop(0, rows // 32, norm, 0)
+
+            def project(j, _):
+                cols = pl.ds(pl.multiple_of(j * 256, 256), 256)
+                raw[:, cols] = jnp.dot(first[...], W_ref[:, cols], preferred_element_type=F32)
+                return 0
+
+            lax.fori_loop(0, 2, project, 0)
+            yield
+            lax.fori_loop(2, C // 256, project, 0)
+            yield
+            for s in range(2):
+                r = slice(s * L, (s + 1) * L)
+                k, _ = head_rotated(raw[r, GQ:GQ + HS], gk_ref[...], cos_ref[...], sin_ref[...])
+                ks[r, :] = k.astype(BF)
+                vs[r, :] = raw[r, GQ + HS:].astype(BF)
+            for s in range(2):
+                r = pl.ds(s * L, L)
+
+                def one_head(h, _):
+                    cols = pl.ds(pl.multiple_of(h * HS, HS), HS)
+                    q, _ = head_rotated(raw[r, cols], gq_ref[...], cos_ref[...], sin_ref[...])
+                    q = q.astype(BF)
+                    qs[r, cols] = q
+                    p = softmax_rows(q, ks[r, :], ok_ref[s]).astype(BF)
+                    att[r, cols] = jnp.dot(p, vs[r, :], preferred_element_type=F32).astype(BF)
+                    return 0
+
+                for g in range(2):
+                    lax.fori_loop(g * heads // 2, (g + 1) * heads // 2, one_head, 0)
+                    yield
+
+            def project_out(j, _):
+                cols = pl.ds(pl.multiple_of(j * 512, 512), 512)
+                part[:, cols] = jnp.dot(att[...], O_ref[:, cols], preferred_element_type=F32).astype(BF)
+                return 0
+
+            lax.fori_loop(0, D // 512, project_out, 0)
+            yield
+            yield from col_rs(
+                net, lambda s, h: part.at[pl.ds(s * L + h * T, T)], o_ref, lambda w, s, h: acc.at[w, s, h],
+                lambda w, s, h: buf.at[w, s, h], lambda i: fin.at[i], lambda w, s, h: rsem.at[w, s, h],
+                lambda w, s, h: ssem.at[w, s, h], T, done)
+
+        interleave(gather(), compute())
+        for f in done:
+            f()
+
+        def finish(i, _):
+            ag.drain(i)
+            return 0
+
+        lax.fori_loop(0, 4, finish, 0)
+
+    S = jax.ShapeDtypeStruct
+    V = pltpu.VMEM
+    return pl.pallas_call(
+        kernel,
+        out_shape=(S((T, D), BF), S((n_expert, 2 * T, D), BF), S((rows, D), BF), S((rows, C), F32), S((rows, GQ), BF),
+                   S((rows, HS), BF), S((rows, HS), BF), S((rows, GQ), BF)),
+        in_specs=[VM] * 10, out_specs=(VM, ANY, VM, VM, VM, VM, VM, VM),
+        scratch_shapes=[V((rows, D), BF), V((2, 2, 2, T, D), BF), V((2, 2, 2, T, D), BF), V((2, T, D), BF),
+                        DMA((3, 2, 2)), DMA((3, 2, 2)), DMA((2, n_expert, 2)), DMA((2, n_expert, 5)), DMA],
+        compiler_params=params(cid, 60 << 20), name="attention_forward",
+    )(X, W, O, gain, gq, gk, cos, sin, allowed, cot)
+
+
+def attention_backward(n_expert, out_part, gx, X, first, raw, qs, ks, vs, att, W, O, gain, gq, gk, cos, sin, allowed, cid):
+    T, D = gx.shape
+    L = 2 * T
+    rows = 2 * L
+    GQ = O.shape[0]
+    heads = GQ // HEAD_SIZE
+    C = W.shape[1]
+    HS = HEAD_SIZE
+    scale = HS ** -0.5
+
+    def kernel(p_ref, gx_ref, X_ref, first, raw, qs, ks, vs, att, W_ref, O_ref, gain_ref, gq_ref, gk_ref, cos_ref, sin_ref, ok_ref,
+               o_ref, dX, dW, dO, ga_out, gq_out, gk_out,
+               GA, gatt, graw, dk, dv, invc, Tb, acc, b1, b2, zb, r0, s0, r1, s1, r2, s2, r3, s3, xr, xs, lsem):
+        net = Net(n_expert).enter()
+        z = net.at[0]
+        far = lambda i: slot_plane(z, 3 - i)
+        load = lambda i: pltpu.make_async_copy(p_ref.at[pl.ds(far(i) * 4, 4)], Tb, lsem)
+        load(0).start()
+        greet(net, (0, 1, 2))
+        rs = Reduce22(net, T, acc, b1, b2, zb, (r0, s0, r1, s1, r2, s2, r3, s3))
+        lane = lax.broadcasted_iota(jnp.int32, (256, 256), 1)
+        sub = lax.broadcasted_iota(jnp.int32, (256, 256), 0)
+        eye = jnp.where(sub == lane, 1.0, 0.0).astype(BF)
+
+        def flip(v):
+            return lax.dot_general(eye[:v.shape[1], :v.shape[1]], v, NT, preferred_element_type=F32).astype(BF)
+
+        def reduce():
+            for i in range(4):
+                load(i).wait()
+                rs.p_send(Tb, far(i))
+                yield
+                rs.stage0(Tb, far(i))
+                rs.p_wait_send(Tb, far(i))
+                if i < 3:
+                    load(i + 1).start()
+                yield
+                if i:
+                    rs.stage1(far(i - 1))
+                    yield
+                if i > 1:
+                    rs.stage2(far(i - 2))
+                    yield
+            rs.stage1(far(3))
+            yield
+            rs.stage2(far(2))
+            yield
+            for i in (0, 1, 2):
+                rs.relay(far(i))
+                yield
+            rs.stage2(far(3))
+            yield
+            rs.last(o_ref)
+
+        def compute():
+            done = []
+            place = lambda s, h: GA.at[pl.ds(pl.multiple_of(s * L + h * T, T), T)]
+            yield from col_ag(net, gx_ref, place, lambda s, h: xr.at[s, h], lambda w, s, h: xs.at[w, s, h], done)
+            for f in done:
+                f()
+
+            def grad_att(j, _):
+                cols = pl.ds(pl.multiple_of(j * 256, 256), 256)
+                gatt[:, cols] = lax.dot_general(GA[...], O_ref[cols, :], NT, preferred_element_type=F32).astype(BF)
+                return 0
+
+            lax.fori_loop(0, GQ // 256, grad_att, 0)
+            yield
+            gq_out[...] = jnp.zeros_like(gq_out)
+            gk_out[...] = jnp.zeros_like(gk_out)
+
+            def inverse(i, _):
+                r = pl.ds(pl.multiple_of(i * 32, 32), 32)
+                x = X_ref[r, :].astype(F32)
+                inv = lax.rsqrt(jnp.mean(x * x, axis=-1, keepdims=True) + epsilon)
+                invc[r, :] = jnp.broadcast_to(inv, (32, 128))
+                return 0
+
+            lax.fori_loop(0, rows // 32, inverse, 0)
+            for s in range(2):
+                r = pl.ds(s * L, L)
+                dk[...] = jnp.zeros_like(dk)
+                dv[...] = jnp.zeros_like(dv)
+
+                def one_head(h, _):
+                    cols = pl.ds(pl.multiple_of(h * HS, HS), HS)
+                    q, k, v, g = qs[r, cols], ks[r, :], vs[r, :], gatt[r, cols]
+                    p = softmax_rows(q, k, ok_ref[s])
+                    dp = lax.dot_general(g, v, NT, preferred_element_type=F32)
+                    ds = (p * (dp - jnp.sum(p * dp, axis=-1, keepdims=True))).astype(BF)
+                    dv[...] += jnp.dot(flip(p.astype(BF)), g, preferred_element_type=F32)
+                    dk[...] += jnp.dot(flip(ds), q, preferred_element_type=F32)
+                    dq = jnp.dot(ds, k, preferred_element_type=F32) * scale
+                    gr, terms = head_back(raw[r, cols], gq_ref[...], cos_ref[...], sin_ref[...], dq)
+                    graw[r, cols] = gr.astype(BF)
+                    gq_out[...] += jnp.sum(terms, axis=0, keepdims=True)
+                    return 0
+
+                for g in range(2):
+                    lax.fori_loop(g * heads // 2, (g + 1) * heads // 2, one_head, 0)
+                    yield
+                gr, terms = head_back(raw[r, GQ:GQ + HS], gk_ref[...], cos_ref[...], sin_ref[...], dk[...] * scale)
+                graw[r, GQ:GQ + HS] = gr.astype(BF)
+                gk_out[...] += jnp.sum(terms, axis=0, keepdims=True)
+                graw[r, GQ + HS:] = dv[...].astype(BF)
+
+            def grad_o(h, _):
+                cols = pl.ds(pl.multiple_of(h * HS, HS), HS)
+                aT = flip(att[:, cols])
+                for j in range(2):
+                    w = slice(j * (D // 2), (j + 1) * (D // 2))
+                    dO[cols, w] = jnp.dot(aT, GA[:, w], preferred_element_type=F32).astype(BF)
+                return 0
+
+            lax.fori_loop(0, heads, grad_o, 0)
+            yield
+
+            def grad_x(j, _):
+                cols = pl.ds(pl.multiple_of(j * 256, 256), 256)
+                dx = lax.dot_general(graw[...], W_ref[cols, :], NT, preferred_element_type=F32)
+                dX[:, cols] = dx.astype(BF)
+                ga_out[:, cols] = jnp.sum(dx * X_ref[:, cols].astype(F32) * invc[:, 0:1], axis=0, keepdims=True)
+                return 0
+
+            for g in range(2):
+                lax.fori_loop(g * D // 512, (g + 1) * D // 512, grad_x, 0)
+                yield
+
+            def grad_w(j, _):
+                cols = pl.ds(pl.multiple_of(j * 256, 256), 256)
+                dW[cols, :] = jnp.dot(flip(first[:, cols]), graw[...], preferred_element_type=F32).astype(BF)
+                return 0
+
+            for g in range(2):
+                lax.fori_loop(g * D // 512, (g + 1) * D // 512, grad_w, 0)
+                yield
+
+        interleave(reduce(), compute())
+
+        def finish(i, _):
+            rs.drain(slot_plane(z, i))
+            return 0
+
+        lax.fori_loop(0, 4, finish, 0)
+
+    S = jax.ShapeDtypeStruct
+    V = pltpu.VMEM
+    return pl.pallas_call(
+        kernel,
+        out_shape=(S((T, D), BF), S((rows, D), BF), S((D, C), BF), S((GQ, D), BF), S((1, D), F32), S((1, HS), F32), S((1, HS), F32)),
+        in_specs=[ANY] + [VM] * 16, out_specs=(VM,) * 7,
+        scratch_shapes=[V((rows, D), BF), V((rows, GQ), BF), V((rows, C), BF), V((L, HS), F32), V((L, HS), F32), V((rows, 128), F32),
+                        V((4, 2 * T, D), BF)] + Reduce22.scratch(T, D) + [DMA((2, 2)), DMA((3, 2, 2)), DMA],
+        compiler_params=params(cid, 64 << 20), name="attention_backward",
+    )(out_part, gx, X, first, raw, qs, ks, vs, att, W, O, gain, gq, gk, cos, sin, allowed)
+
+
 MODEL_WIDTH = 2048
 QUERY_HEADS = 32
 KEY_VALUE_HEADS = 4
@@ -1541,16 +1829,14 @@
     dots_out = jnp.pad(dots, ((0, 0), (0, 8 - EXP_DEV), (0, 0)))
     dots_in = exchange(n_expert, dots_out, 3)
     parts = max(1, n_expert // 16)
+    cols = D // parts
 
     def summed(v, cid):
         v = v.reshape(n_expert, 2, T, D)
-        W_ = D // parts
-        return jnp.concatenate(
-            [reduce_scatter_all(n_expert, v[..., i * W_:(i + 1) * W_], cid + 2 * i) for i in range(parts)], axis=1).astype(F32)
-
-    back_sum = summed(back_part, 8)
-    out_sum = summed(out_part, 9)
-
+        part = lambda i: reduce_scatter_all(n_expert, lax.dynamic_slice_in_dim(v, i * cols, cols, axis=3), cid)
+        return lax.map(part, jnp.arange(parts)).transpose(1, 0, 2).reshape(T, D)
+
+    back_sum, out_sum = summed(back_part, 4), summed(out_part, 5)
     return back_sum, out_sum, dots_in, gate_grad, up_grad, down_grad
 
 
@@ -1596,32 +1882,36 @@
     docs = lax.dynamic_slice(docs, (2 * c, p, 0), (2, 1, 2 * T)).reshape(2, 2 * T)
 
     L = 2 * T
-    x = X.reshape(2 * L, D).astype(F32)
-    normed, inverse_attn = norm_parts(x, attn_gain)
-    first_in = normed.astype(BF)
-    raw = mm(first_in, W)
-    query_raw = raw[:, :GQ].reshape(2, L, GROUP, HEAD_SIZE)
-    key_raw = raw[:, GQ:GQ + KV].reshape(2, L, HEAD_SIZE)
-    value = raw[:, GQ + KV:].reshape(2, L, HEAD_SIZE).astype(BF)
-    cos, sin = rope_tables(jnp.arange(L, dtype=jnp.int32))
+    places = jnp.arange(L, dtype=jnp.int32)
+    cos, sin = rope_tables(places)
     qcos, qsin = cos[:, None, :], sin[:, None, :]
-    query_normed, query_inverse = norm_parts(query_raw, query_gain)
-    queries = rotate(query_normed, qcos, qsin).astype(BF)
-    key_normed, key_inverse = norm_parts(key_raw, key_gain)
-    keys = rotate(key_normed, cos, sin).astype(BF)
-    places = jnp.arange(L, dtype=jnp.int32)
     allowed = (places[:, None] >= places[None, :])[None] & (docs[:, :, None] == docs[:, None, :])
-    scores = ein("sqhd,skd->shqk", queries, keys) * score_scale
-    scores = jnp.where(allowed[:, None], scores, -1e30)
-    top = jnp.max(scores, axis=-1, keepdims=True)
-    ex = jnp.exp(scores - top)
-    probs = ex / jnp.sum(ex, axis=-1, keepdims=True)
-    probs_low = probs.astype(BF)
-    attended = ein("shqk,skd->sqhd", probs_low, value).reshape(2 * L, GQ).astype(BF)
-    part = mm(attended, O).astype(BF).reshape(2, 2, T, D)
     if small_plane:
-        attn_sum, G = column_sum_gather(n_expert, part, cotangent, 1)
+        cos2 = jnp.concatenate([cos, cos], axis=1)
+        sin2 = jnp.concatenate([-sin, sin], axis=1)
+        attn_sum, G, first_in, raw, queries, keys, value, attended = attention_forward(
+            n_expert, X.reshape(2 * L, D), W, O, attn_gain[None], query_gain[None], key_gain[None], cos2, sin2,
+            allowed.astype(F32), cotangent, 1)
     else:
+        x = X.reshape(2 * L, D).astype(F32)
+        normed, inverse_attn = norm_parts(x, attn_gain)
+        first_in = normed.astype(BF)
+        raw = mm(first_in, W)
+        query_raw = raw[:, :GQ].reshape(2, L, GROUP, HEAD_SIZE)
+        key_raw = raw[:, GQ:GQ + KV].reshape(2, L, HEAD_SIZE)
+        value = raw[:, GQ + KV:].reshape(2, L, HEAD_SIZE).astype(BF)
+        query_normed, query_inverse = norm_parts(query_raw, query_gain)
+        key_normed, key_inverse = norm_parts(key_raw, key_gain)
+        queries = rotate(query_normed, qcos, qsin).astype(BF)
+        keys = rotate(key_normed, cos, sin).astype(BF)
+        scores = ein("sqhd,skd->shqk", queries, keys) * score_scale
+        scores = jnp.where(allowed[:, None], scores, -1e30)
+        top = jnp.max(scores, axis=-1, keepdims=True)
+        ex = jnp.exp(scores - top)
+        probs = ex / jnp.sum(ex, axis=-1, keepdims=True)
+        probs_low = probs.astype(BF)
+        attended = ein("shqk,skd->sqhd", probs_low, value).reshape(2 * L, GQ).astype(BF)
+        part = mm(attended, O).astype(BF).reshape(2, 2, T, D)
         attn_sum, G = column_sum(n_expert, part, 1), G[0]
     middle = tokens.astype(F32) + attn_sum.astype(F32)
 
@@ -1660,28 +1950,31 @@
     grad_middle = grad_result + grad_middle_norm
 
     if small_plane:
-        out_sum, GA = reduce_and_column(n_expert, out_part, grad_middle.astype(BF), 6)
+        out_sum, grad_first, raw_grad, out_grad, attn_gain_grad, query_gain_grad, key_gain_grad = attention_backward(
+            n_expert, out_part, grad_middle.astype(BF), X.reshape(2 * L, D), first_in, raw, queries, keys, value, attended, W, O,
+            attn_gain[None], query_gain[None], key_gain[None], cos2, sin2, allowed.astype(F32), 6)
+        attn_gain_grad, query_gain_grad, key_gain_grad = attn_gain_grad[0], query_gain_grad[0], key_gain_grad[0]
     else:
         GA = column_gather(n_expert, grad_middle.astype(BF), 6)
+        GA = GA.reshape(2 * L, D)
+        out_grad = mm(attended.T, GA)
+        grad_attended = ein("td,fd->tf", GA, O).astype(BF).reshape(2, L, GROUP, HEAD_SIZE)
+        grad_probs = ein("sqhd,skd->shqk", grad_attended, value)
+        grad_scores = (probs * (grad_probs - jnp.sum(probs * grad_probs, axis=-1, keepdims=True))).astype(BF)
+        grad_queries = ein("shqk,skd->sqhd", grad_scores, keys) * score_scale
+        grad_keys = ein("shqk,sqhd->skd", grad_scores, queries) * score_scale
+        grad_values = ein("shqk,sqhd->skd", probs_low, grad_attended)
+        grad_query_raw, query_terms = norm_back(query_raw, query_inverse, query_gain, rotate_back(grad_queries, qcos, qsin))
+        grad_key_raw, key_terms = norm_back(key_raw, key_inverse, key_gain, rotate_back(grad_keys, cos, sin))
+        grad_raw = jnp.concatenate(
+            [grad_query_raw.reshape(2 * L, GQ).astype(BF), grad_key_raw.reshape(2 * L, KV).astype(BF),
+             grad_values.reshape(2 * L, KV).astype(BF)], axis=-1)
+        query_gain_grad = jnp.sum(query_terms, axis=(0, 1, 2))
+        key_gain_grad = jnp.sum(key_terms, axis=(0, 1))
+        grad_first = ein("tf,df->td", grad_raw, W)
+        raw_grad = mm(first_in.T, grad_raw)
+        attn_gain_grad = jnp.sum(grad_first * x * inverse_attn, axis=0)
     block_out = (middle + out_sum.astype(F32)).astype(BF)
-    GA = GA.reshape(2 * L, D)
-    out_grad = mm(attended.T, GA)
-    grad_attended = ein("td,fd->tf", GA, O).astype(BF).reshape(2, L, GROUP, HEAD_SIZE)
-    grad_probs = ein("sqhd,skd->shqk", grad_attended, value)
-    grad_scores = (probs * (grad_probs - jnp.sum(probs * grad_probs, axis=-1, keepdims=True))).astype(BF)
-    grad_queries = ein("shqk,skd->sqhd", grad_scores, keys) * score_scale
-    grad_keys = ein("shqk,sqhd->skd", grad_scores, queries) * score_scale
-    grad_values = ein("shqk,sqhd->skd", probs_low, grad_attended)
-    grad_query_raw, query_terms = norm_back(query_raw, query_inverse, query_gain, rotate_back(grad_queries, qcos, qsin))
-    grad_key_raw, key_terms = norm_back(key_raw, key_inverse, key_gain, rotate_back(grad_keys, cos, sin))
-    grad_raw = jnp.concatenate(
-        [grad_query_raw.reshape(2 * L, GQ).astype(BF), grad_key_raw.reshape(2 * L, KV).astype(BF),
-         grad_values.reshape(2 * L, KV).astype(BF)], axis=-1)
-    query_gain_grad = jnp.sum(query_terms, axis=(0, 1, 2))
-    key_gain_grad = jnp.sum(key_terms, axis=(0, 1))
-    grad_first = ein("tf,df->td", grad_raw, W)
-    raw_grad = mm(first_in.T, grad_raw)
-    attn_gain_grad = jnp.sum(grad_first * x * inverse_attn, axis=0)
 
     small = jnp.concatenate([
         router_grad.reshape(nd, R * E), attn_gain_grad.reshape(nd, R), ffn_gain_grad.reshape(nd, R),

time: 712 us -> 675 us (0.948)
  matrix products: 68.9 us -> 30.2 us
  Pallas kernels: 564 us -> 595 us
  local copies, waits for them, and re-layouts: 37.1 us -> 21.3 us
  other arithmetic: 30.2 us -> 20.2 us
    pallas_call x2, Pallas kernels: 180 us -> 221 us  [the longest x1 117 us: attention_forward(): pl.pallas_call(kernel, out_shape=(S((T, D), BF), S((n_expert, 2 * T, D),...]
    dot_general x7 -> x3, matrix products: 20.8 us -> 2.99 us  [mm(): return jnp.dot(a, b, preferred_element_type=F32)]
    dot_general x10 -> x3, matrix products: 44 us -> 27.2 us  [ein(): return jnp.einsum(spec, *args, preferred_element_type=F32)]
    pallas_call x1, Pallas kernels: 224 us -> 213 us  [experts_fused(): pl.pallas_call(kernel, out_shape=(S((T, D), BF), S((chips, 2 * T, D), BF)...]
    unnamed x175 -> x85, local copies, waits for them, and re-layouts: 13.3 us -> 4.86 us
where the time goes in v3:
time: 675 us; the launch traced here: 668 us
  Pallas kernels  595 us (88%)
  matrix products  30.2 us (4%)
  local copies, waits for them, and re-layouts  21.3 us (3%)
  other arithmetic  20.2 us (3%)
    pallas_call x1, Pallas kernels, experts_fused(): pl.pallas_call(kernel, out_shape=(S((T, D), BF), S((chips, 2 * T, D), BF)...  213 us
    pallas_call x1, Pallas kernels, attention_forward(): pl.pallas_call(kernel, out_shape=(S((T, D), BF), S((n_expert, 2 * T, D),...  117 us
    pallas_call x1, Pallas kernels, attention_backward(): pl.pallas_call(kernel, out_shape=(S((T, D), BF), S((rows, D), BF), S((D,...  104 us
    pallas_call x1, Pallas kernels, reduce_end(): pl.pallas_call(kernel, out_shape=(S((T, D), BF), S((Z, R, C), BF), S((HR,...  85.8 us
    pallas_call x1, Pallas kernels, gather_start(): pl.pallas_call(kernel, out_shape=(S((2, 2, T, D), BF), S((Z, plane, 2, R,...  74.5 us
    dot_general x3, matrix products, ein(): return jnp.einsum(spec, *args, preferred_element_type=F32)  27.2 us

profile of v3, /device:TPU:13, one launch (start us, length us, event | category | flops | bytes accessed | tf_op | source)
XLA Modules:
  0.0 667.7 jit_solution(18119890268191646715)
XLA Ops:
  0.7 0.7 dynamic-slice_convert_fusion
  1.3 0.7 pad_bitcast_fusion.2
  2.1 0.7 pad_bitcast_fusion.1
  2.9 0.8 copy.61
  3.7 0.8 copy.62
  4.4 0.8 copy.63
  5.3 0.6 fusion.13.refs_3_
  5.9 0.9 copy_bitcast_fusion.3
  6.8 1.1 copy.98
  7.9 0.9 maximum_bitcast_fusion.refs_1_
  8.8 74.5 %gather_start.1 = (bf16[2,2,128,2048]{3,2,1,0:T(8,128)(2,1)}, bf16[4,4,2,64,1280]{4,3,2,1,0:T(8,128)(2,1)}, bf16[4,2,128,2048]{3,2,1,0:T(8,128)(2,1)}, bf16[32,80,128]{2,1,0:T(8,128)(2,1)}) custom-call(bf16[128,2048]{1,0:T(8,128)(2,1)} %refs_0_.1, bf16[4,64,1280]{2,1,0:T(8,128)(2,1)} %maximum_bitcast_fusion.refs_1_, bf16[128,2048]{1,0:T(8,128)(2,1)} %refs_2_.1, ...), custom_call_target="tpu_custom_call" | custom-call | tf_op jit(solution)/shard_map/gather_start/pallas_call | solution.py:664
  83.3 0.9 slice_reduce_fusion
  84.3 0.9 and_convert_fusion.ok_ref
  85.2 1.1 slice.55
  86.7 0.9 copy.90
  87.6 1.1 convert_reduce_fusion
  88.7 0.6 reshape.230.gq_ref
  89.4 0.6 reshape.231.gk_ref
  90.5 0.8 pad_maximum_fusion
  91.4 116.9 %attention_forward.1 = (bf16[128,2048]{1,0:T(8,128)(2,1)}, bf16[16,256,2048]{2,1,0:T(8,128)(2,1)}, bf16[512,2048]{1,0:T(8,128)(2,1)}, f32[512,1280]{1,0:T(8,128)...) custom-call(bf16[512,2048]{1,0:T(8,128)(2,1)} %bitcast.92, ...), custom_call_target="tpu_custom_call" | custom-call | tf_op jit(solution)/shard_map/attention_forward/pallas_call | solution.py:1570
  208.3 1.3 multiply_reduce_fusion.2
  210.0 1.3 multiply_convert_fusion.x_ref
  212.7 0.6 fusion.15.a_ref
  213.3 213.2 %experts.1 = (bf16[128,2048]{1,0:T(8,128)(2,1)}, bf16[16,256,2048]{2,1,0:T(8,128)(2,1)}, f32[32,8,128]{2,1,0:T(8,128)}, bf16[2,4,320,2048]{3,2,1,0:T(8,128)(2,1)...) custom-call(bf16[128,2048]{1,0:T(8,128)(2,1)} %copy-done.5, ...), custom_call_target="tpu_custom_call" | custom-call | tf_op jit(solution)/shard_map/experts/pallas_call | solution.py:1323
  426.5 11.7 %fusion.26 = f32[2,384,2048]{2,1,0:T(8,128)} fusion(bf16[2,1280,384]{2,1,0:T(8,128)(2,1)} %bitcast.88, bf16[2,1280,2048]{2,1,0:T(8,128)(2,1)} %bitcast.87), kind=kOutput, calls=%fused_computation.78 | convolution fusion | flops 4026531840 | bytes 18743296 | tf_op jit(solution)/shard_map/emf,emd->efd/dot_general | solution.py:1788
  438.2 0.6 fusion.20
  438.9 7.5 %fusion.25 = f32[2,2048,384]{2,1,0:T(8,128)} fusion(bf16[2,1280,2048]{2,1,0:T(8,128)(2,1)S(1)} %bitcast.120, bf16[2,1280,384]{2,1,0:T(8,128)(2,1)S(1)} %bitcast.99), kind=kOutput, calls=%fused_computation.77 | convolution fusion | flops 4026531840 | bytes 18743296 | tf_op jit(solution)/shard_map/emd,emf->edf/dot_general | solution.py:1788
  446.5 7.9 %fusion.24 = f32[2,2048,384]{2,1,0:T(8,128)} fusion(bf16[2,1280,2048]{2,1,0:T(8,128)(2,1)S(1)} %bitcast.121, bf16[2,1280,384]{2,1,0:T(8,128)(2,1)S(1)} %bitcast.98), kind=kOutput, calls=%fused_computation.76 | convolution fusion | flops 4026531840 | bytes 18743296 | tf_op jit(solution)/shard_map/emd,emf->edf/dot_general | solution.py:1788
  454.4 0.9 bitcast_reduce_fusion
  455.8 1.2 reshape.216
  457.0 2.3 multiply_reduce_fusion
  459.4 1.3 fusion.19.gx_ref
  460.7 104.2 %attention_backward.1 = (bf16[128,2048]{1,0:T(8,128)(2,1)}, bf16[512,2048]{1,0:T(8,128)(2,1)}, bf16[2048,1280]{1,0:T(8,128)(2,1)}, bf16[1024,2048]{1,0:T(8,128)(...) custom-call(bf16[16,256,2048]{2,1,0:T(8,128)(2,1)} %get-tuple-element.50.p_ref, ...), custom_call_target="tpu_custom_call" | custom-call | tf_op jit(solution)/shard_map/attention_backward/pallas_call | solution.py:1728
  565.4 1.4 reduce.15
  566.8 1.3 reduce.16
  568.2 1.3 reduce.17
  569.6 0.8 reshape.217
  570.4 1.0 concatenate.23
  571.5 0.8 copy.89
  572.3 85.8 %reduce_end.1 = (bf16[128,2048]{1,0:T(8,128)(2,1)}, bf16[4,64,1280]{2,1,0:T(8,128)(2,1)}, bf16[128,2048]{1,0:T(8,128)(2,1)}, f32[32,24,128]{2,1,0:T(8,128)}) custom-call(bf16[2,2,128,2048]{3,2,1,0:T(8,128)(2,1)} %bitcast.97, bf16[4,4,2,64,1280]{4,3,2,1,0:T(8,128)(2,1)} %bitcast.94, bf16[4,2,128,2048]{3,2,1,0:T(8,128)(2,1)} %bitcast.95, f32[32,24,128]{2,1,0:T(8,128)} %bitcast.100), custom_call_target="tpu_custom_call" | custom-call | tf_op jit(solution)/shard_map/reduce_end/pallas_call | solution.py:828
  658.1 1.3 convert_element_type.157
  659.6 1.1 copy.86
  660.7 0.7 copy.99
  661.4 0.7 copy.100
  662.4 2.1 fusion.5
  664.5 1.1 convert_element_type.158
  665.7 0.7 copy.75
  667.0 0.6 fusion.22
  (111 shorter events, 5.4 us)
Async XLA Ops:
  86.3 125.0 %copy-start.3 = (bf16[32,64,128]{2,1,0:T(8,128)(2,1)}, bf16[32,64,128]{2,1,0:T(8,128)(2,1)S(1)}, u32[]{:S(2)}) copy-start(bf16[32,64,128]{2,1,0:T(8,128)(2,1)S(1)} %slice.55) | copy-start | bytes 1572868
  91.4 116.9 %copy-start = (bf16[128,2048]{1,0:T(8,128)(2,1)S(1)}, bf16[128,2048]{1,0:T(8,128)(2,1)}, u32[]{:S(2)}) copy-start(bf16[128,2048]{1,0:T(8,128)(2,1)} %refs_0_.1) | copy-start | bytes 1572868
  208.3 3.0 copy-start.33
  209.6 3.7 copy-start.30
  210.0 3.3 copy-start.23
  211.3 0.8 copy-start.5
  211.3 2.0 copy-start.21
  212.1 0.6 copy-start.17
  212.1 1.2 copy-start.26
  212.7 0.6 copy-start.28
  426.5 11.7 %copy-start.13 = (bf16[2,4,320,768]{3,2,1,0:T(8,128)(2,1)S(1)}, bf16[2,4,320,768]{3,2,1,0:T(8,128)(2,1)}, u32[]{:S(2)}) copy-start(bf16[2,4,320,768]{3,2,1,0:T(8,128)(2,1)} %get-tuple-element.71) | copy-start | bytes 11796484
  426.5 12.4 %copy-start.36 = (bf16[2,4,320,2048]{3,2,1,0:T(8,128)(2,1)S(1)}, bf16[2,4,320,2048]{3,2,1,0:T(8,128)(2,1)}, u32[]{:S(2)}) copy-start(bf16[2,4,320,2048]{3,2,1,0:T(8,128)(2,1)} %get-tuple-element.70) | copy-start | bytes 31457284
  446.4 8.9 %copy-start.18 = (f32[128,32]{0,1:T(8,128)S(1)}, f32[128,32]{0,1:T(8,128)}, u32[]{:S(2)}) copy-start(f32[128,32]{0,1:T(8,128)} %copy-done.17) | copy-start | bytes 49156
  446.4 9.0 %copy-start.22 = (pred[128,32]{0,1:T(8,128)(4,1)S(1)}, pred[128,32]{0,1:T(8,128)(4,1)}, u32[]{:S(2)}) copy-start(pred[128,32]{0,1:T(8,128)(4,1)} %copy-done.21) | copy-start | bytes 12292
  446.4 9.0 %copy-start.27 = (f32[128]{0:T(128)S(1)}, f32[128]{0:T(128)}, u32[]{:S(2)}) copy-start(f32[128]{0:T(128)} %copy-done.26) | copy-start | bytes 1540
  446.4 9.0 %copy-start.29 = (f32[128]{0:T(128)S(1)}, f32[128]{0:T(128)}, u32[]{:S(2)}) copy-start(f32[128]{0:T(128)} %copy-done.28) | copy-start | bytes 1540
  446.4 9.0 %copy-start.6 = (bf16[128,2048]{1,0:T(8,128)(2,1)S(1)}, bf16[128,2048]{1,0:T(8,128)(2,1)}, u32[]{:S(2)}) copy-start(bf16[128,2048]{1,0:T(8,128)(2,1)} %copy-done.5) | copy-start | bytes 1572868
  446.4 10.6 %copy-start.1 = (bf16[128,2048]{1,0:T(8,128)(2,1)S(1)}, bf16[128,2048]{1,0:T(8,128)(2,1)}, u32[]{:S(2)}) copy-start(bf16[128,2048]{1,0:T(8,128)(2,1)} %refs_0_.1) | copy-start | bytes 1572868
  446.5 10.6 %copy-start.4 = (bf16[32,64,128]{2,1,0:T(8,128)(2,1)S(1)}, bf16[32,64,128]{2,1,0:T(8,128)(2,1)}, u32[]{:S(2)}) copy-start(bf16[32,64,128]{2,1,0:T(8,128)(2,1)} %copy-done.3) | copy-start | bytes 1572868
  446.5 10.6 %copy-start.7 = (bf16[128,2048]{1,0:T(8,128)(2,1)S(1)}, bf16[128,2048]{1,0:T(8,128)(2,1)}, u32[]{:S(2)}) copy-start(bf16[128,2048]{1,0:T(8,128)(2,1)} %get-tuple-element.48) | copy-start | bytes 1572868
  446.5 10.5 %copy-start.24 = (f32[2048,1]{0,1:T(1,128)S(1)}, f32[2048,1]{0,1:T(1,128)}, u32[]{:S(2)}) copy-start(f32[2048,1]{0,1:T(1,128)} %copy-done.23) | copy-start | bytes 24580
  446.5 10.5 %copy-start.31 = (f32[128]{0:T(128)S(1)}, f32[128]{0:T(128)}, u32[]{:S(2)}) copy-start(f32[128]{0:T(128)} %copy-done.30) | copy-start | bytes 1540
  455.5 3.9 copy-start.9
  459.4 1.3 copy-start.11
  459.4 1.3 copy-start.34
  658.1 4.0 copy-start.2
  658.1 4.0 copy-start.14
  658.1 4.0 copy-start.20
  659.4 2.9 copy-start.37
  659.4 2.9 copy-start.8
  659.4 2.9 copy-start.10
  659.4 2.9 copy-start.12
  659.4 2.9 copy-start.15
  659.4 2.9 copy-start.25
  659.5 2.9 copy-start.32
  659.5 2.9 copy-start.35
  662.1 2.4 copy-start.16
  662.4 3.2 copy-start.19

commit v4 on v3

--- a/solution.py
+++ b/solution.py
@@ -70,6 +70,22 @@
     pl.semaphore_wait(bar, count)
 
 
+def greet_column(net):
+    bar = pltpu.get_barrier_semaphore()
+    n, z = net.dims[0], net.at[0]
+    for k in range(1, n):
+        dev = (net.chip(net.moved(0, (z + k) % n)), net.c)
+        pl.semaphore_signal(bar, inc=1, device_id=dev, device_id_type=MESH_ID)
+    count = n - 1
+    for axis in (1, 2):
+        for cond, to in net.near(axis):
+            dev = (net.chip(net.moved(axis, to)), net.c)
+            when(cond, lambda dev=dev: pl.semaphore_signal(bar, inc=1, device_id=dev, device_id_type=MESH_ID))
+            count = count + (1 if cond is None else jnp.where(cond, 1, 0))
+    pl.semaphore_signal(bar, inc=1, device_id=(net.e, 1 - net.c), device_id_type=MESH_ID)
+    pl.semaphore_wait(bar, count + 1)
+
+
 def greet_all(net):
     bar = pltpu.get_barrier_semaphore()
     total = net.chips * 2
@@ -84,14 +100,15 @@
     pl.semaphore_wait(bar, total - 1)
 
 
-def interleave(*gens):
-    gens = list(gens)
-    while gens:
-        for g in list(gens):
+def interleave(*gens, steps=None):
+    left = [(g, steps[i] if steps else 1) for i, g in enumerate(gens)]
+    while left:
+        for item in list(left):
             try:
-                next(g)
+                for _ in range(item[1]):
+                    next(item[0])
             except StopIteration:
-                gens.remove(g)
+                left.remove(item)
 
 
 def ag_piece(net, order, block, rs, ss, done, partner=True):
@@ -173,12 +190,11 @@
 
 
 def add_into(dst, src, rows):
-    step = 16
-    assert rows % step == 0
+    step = 16 if rows % 16 == 0 else 8
 
     def body(i, _):
         r = pl.ds(pl.multiple_of(i * step, step), step)
-        dst[r, :] = (dst[r, :].astype(F32) + src[r, :].astype(F32)).astype(BF)
+        dst[r, :] = (dst[r, :].astype(F32) + src[r, :].astype(F32)).astype(dst.dtype)
         return 0
 
     lax.fori_loop(0, rows // step, body, 0)
@@ -336,36 +352,6 @@
 ORDER_B = (0, 2, 1)
 
 
-def all_gather_all(n_expert, x, cid):
-    rows, cols = x.shape
-    half = rows // 2
-
-    def kernel(x_ref, o_ref, rsem, ssem, lsem):
-        net = Net(n_expert).enter()
-        cp = pltpu.make_async_copy(x_ref, o_ref.at[net.e, net.c], lsem)
-        cp.start()
-        greet(net, (0, 1, 2))
-        cp.wait()
-        done = []
-        gens = []
-        for i, order in enumerate((ORDER_A, ORDER_B)):
-            gens.append(ag_piece(
-                net, order,
-                lambda ch, co, i=i: o_ref.at[ch, co, pl.ds(i * half, half)],
-                lambda ch, co, i=i: rsem.at[i, ch, co],
-                lambda ch, kind, i=i: ssem.at[i, ch, kind], done))
-        interleave(*gens)
-        for f in done:
-            f()
-
-    return pl.pallas_call(
-        kernel, out_shape=jax.ShapeDtypeStruct((n_expert, 2, rows, cols), x.dtype),
-        in_specs=[VM], out_specs=ANY,
-        scratch_shapes=[DMA((2, n_expert, 2)), DMA((2, n_expert, 7)), DMA],
-        compiler_params=params(cid), name="gather_all",
-    )(x)
-
-
 def reduce_scatter_all(n_expert, t, cid):
     _, _, rows, cols = t.shape
     half = rows // 2
@@ -606,10 +592,10 @@
         done = []
         local_copy(w_ref.at[z], W.at[z, p, c], loc.at[0], [])
         local_copy(o_ref, O.at[p, c], loc.at[1], [])
-        local_copy(a_ref, A.at[me], loc.at[2], done)
+        local_copy(a_ref, A.at[me], loc.at[2], [])
         if with_g:
             local_copy(g_ref, G.at[net.e, c], loc.at[3], [])
-        greet_all(net)
+        greet_column(net)
 
         def wgen():
             for k in range(1, Z):
@@ -636,6 +622,11 @@
                     except StopIteration:
                         gens.remove(g)
 
+        def agen():
+            pltpu.make_async_copy(a_ref, A.at[me], loc.at[2]).wait()
+            yield from ag_piece(
+                net, ORDER_A, lambda ch, co: A.at[ch * 2 + co], lambda ch, co: ar.at[ch, co], lambda ch, kind: as_.at[ch, kind], done)
+
         def ogen(i, order):
             if i == 0:
                 pltpu.make_async_copy(o_ref, O.at[p, c], loc.at[1]).wait()
@@ -654,7 +645,7 @@
 
         interleave(
             wgen(),
-            to_all(net, lambda t: a_ref, lambda s: A.at[s], lambda s: ar.at[s], lambda k: as_.at[k], done),
+            agen(),
             col_ag(net, t_ref, lambda s, h: X.at[s, h], lambda s, h: xr.at[s, h], lambda w, s, h: xs.at[w, s, h], done),
             ogen(0, (1, 2)), ogen(1, (2, 1)), *([ggen(0, ORDER_A), ggen(1, ORDER_B)] if with_g else []))
         for f in done:
@@ -667,7 +658,7 @@
         + ((S((n_expert, 2, T, D), BF),) if with_g else ()),
         in_specs=[VM] * (5 if with_g else 4), out_specs=(ANY,) * (5 if with_g else 4),
         scratch_shapes=[DMA((2, 2)), DMA((3, 2, 2)), DMA((Z,)), DMA((Z,)), DMA((2, plane, 2)), DMA((2, plane, 7)),
-                        DMA((2, plane, 2)), DMA((2, plane, 7)), DMA((nd,)), DMA((nd,)),
+                        DMA((2, plane, 2)), DMA((2, plane, 7)), DMA((n_expert, 2)), DMA((n_expert, 7)),
                         DMA((2, n_expert, 2)), DMA((2, n_expert, 7)), DMA((4,))],
         compiler_params=params(cid), name="gather_start",
     )(tokens, wqkv, w_out, aux, *((cot,) if with_g else ()))
@@ -784,7 +775,9 @@
         z, p, c = net.at[0], net.e % plane, net.c
         me = net.e * 2 + c
         done = []
-        local_copy(s_ref.at[me], s_out.at[me], loc.at[0], done)
+        own = lambda: pltpu.make_async_copy(s_ref.at[me], s_out.at[me], loc)
+        own().start()
+        done.append(lambda: own().wait())
         greet_all(net)
 
         def wgen(q):
@@ -810,11 +803,11 @@
                 lambda st, k: ous.at[i, st, k if st else k % plane], hr, done)
 
         interleave(
-            to_all(net, lambda t: s_ref.at[t], lambda s: s_out.at[s], lambda s: sr.at[s], lambda k: s_s.at[k], done),
             *[wgen(q) for q in range(Z)],
+            ogen(0), ogen(1),
             col_rs(net, lambda s, h: p_ref.at[s, h], x_out, lambda w, s, h: acc.at[w, s, h], lambda w, s, h: buf.at[w, s, h],
                    lambda i: fin.at[i], lambda w, s, h: xr.at[w, s, h], lambda w, s, h: xs.at[w, s, h], T, done),
-            ogen(0), ogen(1))
+            to_all(net, lambda t: s_ref.at[t], lambda s: s_out.at[s], lambda s: sr.at[s], lambda k: s_s.at[k], done))
         o_out[...] = oacc[p]
         for k in range(1, Z):
             o = (z + k) % Z
@@ -832,7 +825,7 @@
                         V((Z, plane, R, C), BF), V((Z, sizes[0], R, C), BF), V((Z, sizes[1], R, C), BF),
                         V((plane, HR, D), BF), V((sizes[0], HR, D), BF), V((sizes[1], HR, D), BF), V((Z, R, C), BF),
                         DMA((3, 2, 2)), DMA((3, 2, 2)), DMA((Z, 3, ns)), DMA((Z, 3, ns)), DMA((2, 3, ns)), DMA((2, 3, ns)),
-                        DMA((nd,)), DMA((nd,)), DMA((Z,)), DMA((Z,)), DMA((1,))],
+                        DMA((nd,)), DMA((nd,)), DMA((Z,)), DMA((Z,)), DMA],
         compiler_params=params(cid, 60 << 20), name="reduce_end",
     )(part, dw, do, small)
 
@@ -844,11 +837,14 @@
 
 
 class Gather22:
-    def __init__(self, net, N, T, rsem, ssem):
-        self.net, self.N, self.T, self.rsem, self.ssem = net, N, T, rsem, ssem
-        self.axes = ((1, 2), (2, 1))
+    def __init__(self, net, N, T, rsem, ssem, A=None):
+        self.net, self.N, self.T, self.rsem, self.ssem, self.A = net, N, T, rsem, ssem, A
+        self.axes = ((1, 2), (2, 1), (1, 2))
+        self.pieces = (0, 1) if A is None else (2, 0, 1)
 
     def blk(self, piece, chip, core):
+        if piece == 2:
+            return self.A.at[chip * 2 + core]
         h = self.T // 2
         return self.N.at[chip, pl.ds(pl.multiple_of(core * self.T + piece * h, h), h)]
 
@@ -896,7 +892,7 @@
 
     def begin(self):
         z = self.net.at[0]
-        for piece in (0, 1):
+        for piece in self.pieces:
             pl.when(z < 3)(lambda piece=piece: self.copy(piece, self.net.at, 0, self.dev(0, z + 1)).start())
             pl.when(z > 0)(lambda piece=piece: self.copy(piece, self.net.at, 1, self.dev(0, z - 1)).start())
             self.push(piece, z, False, False)
@@ -908,25 +904,25 @@
 
     def from_z(self, zt):
         to, more = self.onward(zt)
-        for piece in (0, 1):
+        for piece in self.pieces:
             at = self.level(piece, zt, False, False)
             self.wait(piece, at, self.net.c)
             pl.when(more)(lambda piece=piece, at=at: self.copy(piece, at, 0, self.dev(0, to)).start())
             self.push(piece, zt, False, False)
 
     def from_two(self, zt):
-        for piece in (0, 1):
+        for piece in self.pieces:
             self.wait(piece, self.level(piece, zt, True, False), self.net.c)
             self.push(piece, zt, True, False)
 
     def from_three(self, zt):
         for two in (False, True):
-            for piece in (0, 1):
+            for piece in self.pieces:
                 self.wait(piece, self.level(piece, zt, two, True), self.net.c)
                 self.push(piece, zt, two, True)
 
     def from_partner(self, zt):
-        for piece in (0, 1):
+        for piece in self.pieces:
             for a in (0, 1):
                 for b in (0, 1):
                     self.wait(piece, (zt, a, b), 1 - self.net.c)
@@ -935,7 +931,7 @@
         z = self.net.at[0]
         zt = slot_plane(z, i)
         to, more = self.onward(zt)
-        for piece in (0, 1):
+        for piece in self.pieces:
             def own(piece=piece):
                 pl.when(z < 3)(lambda: self.copy(piece, self.net.at, 0, self.dev(0, z + 1)).wait_send())
                 pl.when(z > 0)(lambda: self.copy(piece, self.net.at, 1, self.dev(0, z - 1)).wait_send())
@@ -1128,7 +1124,7 @@
 
     def kernel(x_ref, a_ref, g_ref, wg_ref, wu_ref, wd_ref, o_sum, o_part, o_dots, o_rows, o_grows, o_act, o_ggu, N,
                A, wgu, wdn, Nst, Gst, H, pk, pkt, sw, rowsb, growsb, h1, h2, actw, ggu, yb, To, Tb, dsend,
-               acc, b1, b2, zb, r0, s0, r1, s1, r2, s2, r3, s3, ar, asd, xr, xs, dr, ds_, lsem):
+               acc, b1, b2, zb, r0, s0, r1, s1, r2, s2, r3, s3, xr, xs, dr, ds_, lsem):
         net = Net(chips).enter()
         z, c, e = net.at[0], net.c, net.e
         me = e * 2 + c
@@ -1143,11 +1139,9 @@
         greet_all(net)
         own().wait()
         acopy().wait()
-        ag = Gather22(net, N, T, xr, xs)
+        ag = Gather22(net, N, T, xr, xs, A)
         rs = Reduce22(net, T, acc, b1, b2, zb, (r0, s0, r1, s1, r2, s2, r3, s3))
-        done = []
         ag.begin()
-        interleave(to_all(net, lambda t: a_ref, lambda s: A.at[s], lambda s: ar.at[s], lambda k: asd.at[k], done))
         for f in loads:
             f().start()
         lane = lax.broadcasted_iota(jnp.int32, (256, 256), 1)
@@ -1157,10 +1151,11 @@
         place = ((lax.broadcasted_iota(jnp.int32, (8, 256), 1) // 128) * cap).astype(F32)
         ag.from_z(slot_plane(z, 1))
         ag.from_two(z)
-        for f in done:
-            f()
         for f in loads:
             f().wait()
+
+        def dots_to(t, act):
+            pl.when(t != me)(lambda: act(rcopy(dsend.at[t], o_dots.at[me], ds_.at[t], dr.at[me], (t // 2, t % 2))))
 
         saves = lambda i: [
             (rowsb, o_rows.at[:, i], 8), (growsb, o_grows.at[:, i], 9), (actw, o_act.at[:, i], 10), (ggu, o_ggu.at[:, i], 11)]
@@ -1242,6 +1237,8 @@
                         dsend[(zt * 4 + ch) * 2 + co, ei:ei + 1, :] = dd[:, co * 128:(co + 1) * 128]
                 if ei == 0:
                     pl.when(i < 3)(lambda: ag.from_two(zn))
+            for k in range(8):
+                dots_to(zt * 8 + k, lambda cp: cp.start())
             pltpu.make_async_copy(actw, o_act.at[:, i], lsem.at[10]).start()
             pltpu.make_async_copy(ggu, o_ggu.at[:, i], lsem.at[11]).start()
             pl.when(i > 0)(lambda: rs.stage2(zp))
@@ -1295,10 +1292,8 @@
 
         lax.fori_loop(0, 4, body, 0)
         z3 = slot_plane(z, 3)
-        last_done = []
         own_dots = pltpu.make_async_copy(dsend.at[me], o_dots.at[me], lsem.at[5])
         own_dots.start()
-        interleave(to_all(net, lambda t: dsend.at[t], lambda s: o_dots.at[s], lambda s: dr.at[s], lambda k: ds_.at[k], last_done))
         rs.stage1(z3)
         rs.relay(slot_plane(z, 2))
         rs.stage2(z3)
@@ -1306,8 +1301,14 @@
         rs.relay(slot_plane(z, 1))
         rs.last(o_sum)
         own_dots.wait()
-        for f in last_done:
-            f()
+
+        def dots_from(k, _):
+            t = (me + k) % nd
+            rcopy(o_dots.at[t], o_dots.at[t], ds_.at[t], dr.at[t], (e, c)).wait_recv()
+            dots_to(t, lambda cp: cp.wait_send())
+            return 0
+
+        lax.fori_loop(1, nd, dots_from, 0)
         for src, dst, s in saves(3):
             pltpu.make_async_copy(src, dst, lsem.at[s]).wait()
 
@@ -1331,15 +1332,42 @@
             V((M, 2 * Fh), F32), V((M, Fh), F32), V((2, M, Fh), BF), V((2, M, 2 * Fh), BF), V((4, 2 * S2, D), BF),
             V((2, 2 * T, D), BF), V((4, 2 * T, D), BF), V((nd, 8, 128), F32)]
         + Reduce22.scratch(T, D)
-        + [DMA((nd,)), DMA((nd,)), DMA((2, chips, 2)), DMA((2, chips, 5)), DMA((nd,)), DMA((nd,)), DMA((16,))],
+        + [DMA((3, chips, 2)), DMA((3, chips, 5)), DMA((nd,)), DMA((nd,)), DMA((16,))],
         compiler_params=params(cid, 64 << 20), name="experts",
     )(x, marked, G, w_gate, w_up, w_down)[:7]
 
 
-def column_sum_gather(n_expert, part, x, cid):
-    _, _, T, D = part.shape
-
-    def kernel(p_ref, x_ref, o_ref, N, acc, buf, fin, rsem, ssem, xr, xs, lsem):
+def head_rotated(v, gain, cos, sin):
+    inv = lax.rsqrt(jnp.mean(v * v, axis=-1, keepdims=True) + epsilon)
+    n = v * inv * gain
+    return n * cos + pltpu.roll(n, HEAD_SIZE // 2, 1) * sin, inv
+
+
+def head_back(v, gain, cos, sin, grad):
+    inv = lax.rsqrt(jnp.mean(v * v, axis=-1, keepdims=True) + epsilon)
+    g = grad * cos - pltpu.roll(grad, HEAD_SIZE // 2, 1) * sin
+    s = g * gain
+    return inv * (s - v * (inv * inv * jnp.mean(s * v, axis=-1, keepdims=True))), g * v * inv
+
+
+def softmax_rows(q, k, allowed):
+    s = lax.dot_general(q, k, NT, preferred_element_type=F32) * (HEAD_SIZE ** -0.5)
+    s = jnp.where(allowed > 0.0, s, -1e30)
+    ex = jnp.exp(s - jnp.max(s, axis=-1, keepdims=True))
+    return ex * (1.0 / jnp.sum(ex, axis=-1, keepdims=True))
+
+
+def attention_forward(n_expert, X, W, O, gain, gq, gk, cos, sin, allowed, cot, cid):
+    T, D = cot.shape
+    L = 2 * T
+    rows = 2 * L
+    GQ = O.shape[0]
+    heads = GQ // HEAD_SIZE
+    C = W.shape[1]
+    HS = HEAD_SIZE
+
+    def kernel(X_ref, W_ref, O_ref, gain_ref, gq_ref, gk_ref, cos_ref, sin_ref, ok_ref, x_ref,
+               o_ref, N, first, raw, qs, ks, vs, att, part, acc, buf, fin, rsem, ssem, xr, xs, lsem):
         net = Net(n_expert).enter()
         z, e, c = net.at[0], net.e, net.c
         own = lambda: pltpu.make_async_copy(x_ref, N.at[e, pl.ds(pl.multiple_of(c * T, T), T)], lsem)
@@ -1365,144 +1393,6 @@
             for i in range(4):
                 ag.from_partner(slot_plane(z, i))
 
-        interleave(
-            col_rs(net, lambda s, h: p_ref.at[s, h], o_ref, lambda w, s, h: acc.at[w, s, h], lambda w, s, h: buf.at[w, s, h],
-                   lambda i: fin.at[i], lambda w, s, h: rsem.at[w, s, h], lambda w, s, h: ssem.at[w, s, h], T, done),
-            gather())
-        for f in done:
-            f()
-
-        def finish(i, _):
-            ag.drain(i)
-            return 0
-
-        lax.fori_loop(0, 4, finish, 0)
-
-    S = jax.ShapeDtypeStruct
-    V = pltpu.VMEM
-    return pl.pallas_call(
-        kernel, out_shape=(S((T, D), BF), S((n_expert, 2 * T, D), BF)), in_specs=[VM, VM], out_specs=(VM, ANY),
-        scratch_shapes=[V((2, 2, 2, T, D), BF), V((2, 2, 2, T, D), BF), V((2, T, D), BF),
-                        DMA((3, 2, 2)), DMA((3, 2, 2)), DMA((2, n_expert, 2)), DMA((2, n_expert, 5)), DMA],
-        compiler_params=params(cid, 40 << 20), name="column_sum_gather",
-    )(part, x)
-
-
-def reduce_and_column(n_expert, part, x, cid):
-    T, D = x.shape
-
-    def kernel(p_ref, x_ref, o_ref, X, Tb, acc, b1, b2, zb, r0, s0, r1, s1, r2, s2, r3, s3, xr, xs, lsem):
-        net = Net(n_expert).enter()
-        z = net.at[0]
-        load = lambda i: pltpu.make_async_copy(p_ref.at[pl.ds(slot_plane(z, 3 - i) * 4, 4)], Tb.at[i % 2], lsem.at[i % 2])
-        load(0).start()
-        greet(net, (0, 1, 2))
-        rs = Reduce22(net, T, acc, b1, b2, zb, (r0, s0, r1, s1, r2, s2, r3, s3))
-        done = []
-        far = lambda i: slot_plane(z, 3 - i)
-
-        def reduce():
-            for i in range(4):
-                if i:
-                    rs.p_wait_send(Tb.at[(i - 1) % 2], far(i - 1))
-                if i < 3:
-                    load(i + 1).start()
-                load(i).wait()
-                rs.p_send(Tb.at[i % 2], far(i))
-                yield
-                rs.stage0(Tb.at[i % 2], far(i))
-                yield
-                if i:
-                    rs.stage1(far(i - 1))
-                    yield
-                if i > 1:
-                    rs.stage2(far(i - 2))
-                    yield
-            rs.p_wait_send(Tb.at[1], far(3))
-            rs.stage1(far(3))
-            rs.stage2(far(2))
-            yield
-            for i in (0, 1, 2):
-                rs.relay(far(i))
-            rs.stage2(far(3))
-            rs.last(o_ref)
-
-        interleave(
-            reduce(),
-            col_ag(net, x_ref, lambda s, h: X.at[s, h], lambda s, h: xr.at[s, h], lambda w, s, h: xs.at[w, s, h], done))
-        for f in done:
-            f()
-
-        def finish(i, _):
-            rs.drain(slot_plane(z, i))
-            return 0
-
-        lax.fori_loop(0, 4, finish, 0)
-
-    S = jax.ShapeDtypeStruct
-    return pl.pallas_call(
-        kernel, out_shape=(S((T, D), BF), S((2, 2, T, D), BF)), in_specs=[ANY, VM], out_specs=(VM, ANY),
-        scratch_shapes=[pltpu.VMEM((2, 4, 2 * T, D), BF)] + Reduce22.scratch(T, D) + [DMA((2, 2)), DMA((3, 2, 2)), DMA((2,))],
-        compiler_params=params(cid, 60 << 20), name="reduce_and_column",
-    )(part, x)
-
-
-def head_rotated(v, gain, cos, sin):
-    inv = lax.rsqrt(jnp.mean(v * v, axis=-1, keepdims=True) + epsilon)
-    n = v * inv * gain
-    return n * cos + pltpu.roll(n, HEAD_SIZE // 2, 1) * sin, inv
-
-
-def head_back(v, gain, cos, sin, grad):
-    inv = lax.rsqrt(jnp.mean(v * v, axis=-1, keepdims=True) + epsilon)
-    g = grad * cos - pltpu.roll(grad, HEAD_SIZE // 2, 1) * sin
-    s = g * gain
-    return inv * (s - v * (inv * inv * jnp.mean(s * v, axis=-1, keepdims=True))), g * v * inv
-
-
-def softmax_rows(q, k, allowed):
-    s = lax.dot_general(q, k, NT, preferred_element_type=F32) * (HEAD_SIZE ** -0.5)
-    s = jnp.where(allowed > 0.0, s, -1e30)
-    ex = jnp.exp(s - jnp.max(s, axis=-1, keepdims=True))
-    return ex * (1.0 / jnp.sum(ex, axis=-1, keepdims=True))
-
-
-def attention_forward(n_expert, X, W, O, gain, gq, gk, cos, sin, allowed, cot, cid):
-    T, D = cot.shape
-    L = 2 * T
-    rows = 2 * L
-    GQ = O.shape[0]
-    heads = GQ // HEAD_SIZE
-    C = W.shape[1]
-    HS = HEAD_SIZE
-
-    def kernel(X_ref, W_ref, O_ref, gain_ref, gq_ref, gk_ref, cos_ref, sin_ref, ok_ref, x_ref,
-               o_ref, N, first, raw, qs, ks, vs, att, part, acc, buf, fin, rsem, ssem, xr, xs, lsem):
-        net = Net(n_expert).enter()
-        z, e, c = net.at[0], net.e, net.c
-        own = lambda: pltpu.make_async_copy(x_ref, N.at[e, pl.ds(pl.multiple_of(c * T, T), T)], lsem)
-        own().start()
-        greet(net, (0, 1, 2))
-        own().wait()
-        ag = Gather22(net, N, T, xr, xs)
-        done = []
-
-        def gather():
-            ag.begin()
-            yield
-            for i in range(4):
-                if i < 3:
-                    ag.from_z(slot_plane(z, i + 1))
-                    yield
-                ag.from_two(slot_plane(z, i))
-                yield
-                if i:
-                    ag.from_three(slot_plane(z, i - 1))
-                    yield
-            ag.from_three(slot_plane(z, 3))
-            for i in range(4):
-                ag.from_partner(slot_plane(z, i))
-
         def compute():
             def norm(i, _):
                 r = pl.ds(pl.multiple_of(i * 32, 32), 32)
@@ -1555,7 +1445,7 @@
                 lambda w, s, h: buf.at[w, s, h], lambda i: fin.at[i], lambda w, s, h: rsem.at[w, s, h],
                 lambda w, s, h: ssem.at[w, s, h], T, done)
 
-        interleave(gather(), compute())
+        interleave(gather(), compute(), steps=(1, 3))
         for f in done:
             f()
 
@@ -1980,11 +1870,11 @@
         router_grad.reshape(nd, R * E), attn_gain_grad.reshape(nd, R), ffn_gain_grad.reshape(nd, R),
         query_gain_grad.reshape(nd, Q), key_gain_grad.reshape(nd, Q)], axis=1)
     n_small = small.shape[1]
-    small = jnp.pad(small, ((0, 0), (0, -n_small % 1024))).reshape(nd, -1, 128)
+    small = jnp.pad(small, ((0, 0), (0, -n_small % 2048))).reshape(nd, -1, 128).astype(BF)
     grad_first_sum, raw_sum, out_sum2, small_in = reduce_end(
         n_expert, grad_first.astype(BF).reshape(2, 2, T, D), raw_grad.astype(BF).reshape(Z, plane, 2, R, GQ + 2 * KV),
         out_grad.astype(BF).reshape(plane, 2, HR, D), small, 7)
-    small_sum = jnp.sum(small_in, axis=0).reshape(-1)
+    small_sum = jnp.sum(small_in.astype(F32), axis=0).reshape(-1)
     router_grad = small_sum[:R * E].reshape(R, E)
     attn_gain_grad = small_sum[R * E:R * E + R]
     ffn_gain_grad = small_sum[R * E + R:R * E + 2 * R]

time: 675 us -> 655 us (0.970)
  Pallas kernels: 595 us -> 571 us
    pallas_call x1, Pallas kernels: 117 us -> 103 us  [attention_forward(): pl.pallas_call(kernel, out_shape=(S((T, D), BF), S((n_expert, 2 * T, D),...]
    pallas_call x1, Pallas kernels: 74.5 us -> 60.6 us  [gather_start(): pl.pallas_call(kernel, out_shape=(S((2, 2, T, D), BF), S((Z, plane, 2, R,...]
where the time goes in v4:
time: 655 us; the launch traced here: 645 us
  Pallas kernels  571 us (87%)
  matrix products  28.9 us (4%)
  other arithmetic  22 us (3%)
  local copies, waits for them, and re-layouts  21.5 us (3%)
    pallas_call x1, Pallas kernels, experts_fused(): pl.pallas_call(kernel, out_shape=(S((T, D), BF), S((chips, 2 * T, D), BF)...  219 us
    pallas_call x1, Pallas kernels, attention_backward(): pl.pallas_call(kernel, out_shape=(S((T, D), BF), S((rows, D), BF), S((D,...  105 us
    pallas_call x1, Pallas kernels, attention_forward(): pl.pallas_call(kernel, out_shape=(S((T, D), BF), S((n_expert, 2 * T, D),...  103 us
    pallas_call x1, Pallas kernels, reduce_end(): pl.pallas_call(kernel, out_shape=(S((T, D), BF), S((Z, R, C), BF), S((HR,...  84.8 us
    pallas_call x1, Pallas kernels, gather_start(): pl.pallas_call(kernel, out_shape=(S((2, 2, T, D), BF), S((Z, plane, 2, R,...  60.6 us
    dot_general x3, matrix products, ein(): return jnp.einsum(spec, *args, preferred_element_type=F32)  25.1 us

profile of v4, /device:TPU:13, one launch (start us, length us, event | category | flops | bytes accessed | tf_op | source)
XLA Modules:
  0.0 645.2 jit_solution(8291332124471926449)
XLA Ops:
  0.7 0.7 dynamic-slice_convert_fusion
  1.3 0.7 pad_bitcast_fusion.2
  2.0 0.7 pad_bitcast_fusion.1
  2.7 0.7 fusion.10
  3.6 0.8 copy.61
  4.4 0.8 copy.62
  5.2 0.8 copy.63
  6.7 0.9 copy_bitcast_fusion.3
  8.1 0.8 pad_maximum_fusion
  9.0 1.1 copy.97
  10.1 0.9 maximum_bitcast_fusion.refs_1_
  10.9 60.6 %gather_start.1 = (bf16[2,2,128,2048]{3,2,1,0:T(8,128)(2,1)}, bf16[4,4,2,64,1280]{4,3,2,1,0:T(8,128)(2,1)}, bf16[4,2,128,2048]{3,2,1,0:T(8,128)(2,1)}, bf16[32,80,128]{2,1,0:T(8,128)(2,1)}) custom-call(bf16[128,2048]{1,0:T(8,128)(2,1)} %refs_0_.1, bf16[4,64,1280]{2,1,0:T(8,128)(2,1)} %maximum_bitcast_fusion.refs_1_, bf16[128,2048]{1,0:T(8,128)(2,1)} %refs_2_.1, ...), custom_call_target="tpu_custom_call" | custom-call | tf_op jit(solution)/shard_map/gather_start/pallas_call | solution.py:655
  71.6 0.9 slice_reduce_fusion
  72.5 1.1 convert_reduce_fusion.1
  73.6 1.1 slice.55
  74.7 0.7 reshape.231.gk_ref
  76.0 0.9 and_convert_fusion.ok_ref
  77.6 0.9 copy.89
  78.6 102.5 %attention_forward.1 = (bf16[128,2048]{1,0:T(8,128)(2,1)}, bf16[16,256,2048]{2,1,0:T(8,128)(2,1)}, bf16[512,2048]{1,0:T(8,128)(2,1)}, f32[512,1280]{1,0:T(8,128)...) custom-call(bf16[512,2048]{1,0:T(8,128)(2,1)} %bitcast.94, ...), custom_call_target="tpu_custom_call" | custom-call | tf_op jit(solution)/shard_map/attention_forward/pallas_call | solution.py:1460
  181.1 1.3 multiply_reduce_fusion.2
  182.5 1.3 multiply_convert_fusion.x_ref
  185.7 0.6 fusion.15.a_ref
  186.3 218.5 %experts.1 = (bf16[128,2048]{1,0:T(8,128)(2,1)}, bf16[16,256,2048]{2,1,0:T(8,128)(2,1)}, f32[32,8,128]{2,1,0:T(8,128)}, bf16[2,4,320,2048]{3,2,1,0:T(8,128)(2,1)...) custom-call(bf16[128,2048]{1,0:T(8,128)(2,1)} %copy-done.5, ...), custom_call_target="tpu_custom_call" | custom-call | tf_op jit(solution)/shard_map/experts/pallas_call | solution.py:1324
  404.8 1.0 bitcast_reduce_fusion
  405.9 0.8 multiply_reduce_fusion.3
  406.7 0.8 select_convert_fusion
  407.4 1.2 convolution_convert_fusion
  408.7 2.2 multiply_reduce_fusion
  411.5 0.7 reshape.218
  412.5 1.2 reshape.217
  413.7 1.3 fusion.19.gx_ref
  415.0 104.6 %attention_backward.1 = (bf16[128,2048]{1,0:T(8,128)(2,1)}, bf16[512,2048]{1,0:T(8,128)(2,1)}, bf16[2048,1280]{1,0:T(8,128)(2,1)}, bf16[1024,2048]{1,0:T(8,128)(...) custom-call(bf16[16,256,2048]{2,1,0:T(8,128)(2,1)} %get-tuple-element.50.p_ref, ...), custom_call_target="tpu_custom_call" | custom-call | tf_op jit(solution)/shard_map/attention_backward/pallas_call | solution.py:1618
  519.6 0.6 convert_reduce_fusion.5
  520.2 0.6 convert_reduce_fusion.4
  520.8 0.7 convert_reduce_fusion.3
  521.9 1.0 concatenate.24
  522.9 0.7 copy.88
  523.7 84.8 %reduce_end.1 = (bf16[128,2048]{1,0:T(8,128)(2,1)}, bf16[4,64,1280]{2,1,0:T(8,128)(2,1)}, bf16[128,2048]{1,0:T(8,128)(2,1)}, bf16[32,32,128]{2,1,0:T(8,128)(2,1)}) custom-call(bf16[2,2,128,2048]{3,2,1,0:T(8,128)(2,1)} %bitcast.99, bf16[4,4,2,64,1280]{4,3,2,1,0:T(8,128)(2,1)} %bitcast.96, bf16[4,2,128,2048]{3,2,1,0:T(8,128)(2,1)} %bitcast.97, ...), custom_call_target="tpu_custom_call" | custom-call | tf_op jit(solution)/shard_map/reduce_end/pallas_call | solution.py:821
  608.6 1.4 fusion.6
  610.0 3.1 fusion.5
  614.4 0.7 copy.75
  615.4 1.1 copy.85
  616.5 0.7 copy.98
  617.1 0.7 copy.99
  617.8 1.1 convert_element_type.165
  619.6 11.4 %fusion.23 = f32[2,2048,384]{2,1,0:T(8,128)} fusion(bf16[2,1280,2048]{2,1,0:T(8,128)(2,1)} %bitcast.122, bf16[2,1280,384]{2,1,0:T(8,128)(2,1)S(1)} %bitcast.101), kind=kOutput, calls=%fused_computation.80 | convolution fusion | flops 4026531840 | bytes 18743296 | tf_op jit(solution)/shard_map/emd,emf->edf/dot_general | solution.py:1678
  631.0 7.5 %fusion.24 = f32[2,2048,384]{2,1,0:T(8,128)} fusion(bf16[2,1280,2048]{2,1,0:T(8,128)(2,1)S(1)} %bitcast.125, bf16[2,1280,384]{2,1,0:T(8,128)(2,1)S(1)} %bitcast.100), kind=kOutput, calls=%fused_computation.81 | convolution fusion | flops 4026531840 | bytes 18743296 | tf_op jit(solution)/shard_map/emd,emf->edf/dot_general | solution.py:1678
  638.6 6.2 fusion.25
  (111 shorter events, 8.2 us)
Async XLA Ops:
  3.4 181.2 %copy-start.19 = (pred[128,32]{0,1:T(8,128)(4,1)}, pred[128,32]{0,1:T(8,128)(4,1)S(1)}, u32[]{:S(2)}) copy-start(pred[128,32]{0,1:T(8,128)(4,1)S(1)} %fusion.10) | copy-start | bytes 12292
  74.7 109.0 %copy-start.4 = (bf16[32,64,128]{2,1,0:T(8,128)(2,1)}, bf16[32,64,128]{2,1,0:T(8,128)(2,1)S(1)}, u32[]{:S(2)}) copy-start(bf16[32,64,128]{2,1,0:T(8,128)(2,1)S(1)} %slice.55) | copy-start | bytes 1572868
  77.6 104.8 %copy-start.20 = (f32[2048,1]{0,1:T(1,128)}, f32[2048,1]{0,1:T(1,128)S(1)}, u32[]{:S(2)}) copy-start(f32[2048,1]{0,1:T(1,128)S(1)} %copy.90) | copy-start | bytes 24580
  78.6 102.5 %copy-start = (bf16[128,2048]{1,0:T(8,128)(2,1)S(1)}, bf16[128,2048]{1,0:T(8,128)(2,1)}, u32[]{:S(2)}) copy-start(bf16[128,2048]{1,0:T(8,128)(2,1)} %refs_0_.1) | copy-start | bytes 1572868
  182.4 2.1 copy-start.25
  183.7 0.8 copy-start.5
  184.5 0.6 copy-start.16
  184.5 0.6 copy-start.23
  185.1 0.5 copy-start.24
  404.8 8.9 %copy-start.1 = (bf16[128,2048]{1,0:T(8,128)(2,1)S(1)}, bf16[128,2048]{1,0:T(8,128)(2,1)}, u32[]{:S(2)}) copy-start(bf16[128,2048]{1,0:T(8,128)(2,1)} %refs_0_.1) | copy-start | bytes 1572868
  404.8 8.9 %copy-start.6 = (bf16[128,2048]{1,0:T(8,128)(2,1)S(1)}, bf16[128,2048]{1,0:T(8,128)(2,1)}, u32[]{:S(2)}) copy-start(bf16[128,2048]{1,0:T(8,128)(2,1)} %get-tuple-element.48) | copy-start | bytes 1572868
  404.8 8.9 %copy-start.8 = (bf16[128,2048]{1,0:T(8,128)(2,1)S(1)}, bf16[128,2048]{1,0:T(8,128)(2,1)}, u32[]{:S(2)}) copy-start(bf16[128,2048]{1,0:T(8,128)(2,1)} %x_ref.1) | copy-start | bytes 1572868
  404.8 8.9 %copy-start.21 = (f32[2048,1]{0,1:T(1,128)S(1)}, f32[2048,1]{0,1:T(1,128)}, u32[]{:S(2)}) copy-start(f32[2048,1]{0,1:T(1,128)} %copy-done.20) | copy-start | bytes 24580
  404.8 8.9 %copy-start.26 = (f32[128]{0:T(128)S(1)}, f32[128]{0:T(128)}, u32[]{:S(2)}) copy-start(f32[128]{0:T(128)} %copy-done.25) | copy-start | bytes 1540
  410.9 2.8 copy-start.10
  410.9 2.8 copy-start.28
  523.7 84.9 %copy-start.2 = (bf16[128,2048]{1,0:T(8,128)(2,1)S(1)}, bf16[128,2048]{1,0:T(8,128)(2,1)}, u32[]{:S(2)}) copy-start(bf16[128,2048]{1,0:T(8,128)(2,1)} %refs_0_.1) | copy-start | bytes 1572868
  523.7 84.9 %copy-start.18 = (f32[2048,1]{0,1:T(1,128)S(1)}, f32[2048,1]{0,1:T(1,128)}, u32[]{:S(2)}) copy-start(f32[2048,1]{0,1:T(1,128)} %copy.89) | copy-start | bytes 24580
  523.7 86.3 %copy-start.7 = (bf16[128,2048]{1,0:T(8,128)(2,1)S(1)}, bf16[128,2048]{1,0:T(8,128)(2,1)}, u32[]{:S(2)}) copy-start(bf16[128,2048]{1,0:T(8,128)(2,1)} %get-tuple-element.48) | copy-start | bytes 1572868
  523.7 86.3 %copy-start.9 = (bf16[128,2048]{1,0:T(8,128)(2,1)S(1)}, bf16[128,2048]{1,0:T(8,128)(2,1)}, u32[]{:S(2)}) copy-start(bf16[128,2048]{1,0:T(8,128)(2,1)} %x_ref.1) | copy-start | bytes 1572868
  523.7 86.3 %copy-start.11 = (f32[128,2048]{1,0:T(8,128)S(1)}, f32[128,2048]{1,0:T(8,128)}, u32[]{:S(2)}) copy-start(f32[128,2048]{1,0:T(8,128)} %copy-done.10) | copy-start | bytes 3145732
  523.7 86.3 %copy-start.14 = (bf16[128,2048]{1,0:T(8,128)(2,1)S(1)}, bf16[128,2048]{1,0:T(8,128)(2,1)}, u32[]{:S(2)}) copy-start(bf16[128,2048]{1,0:T(8,128)(2,1)} %get-tuple-element.59) | copy-start | bytes 1572868
  523.7 86.3 %copy-start.22 = (f32[2048,1]{0,1:T(1,128)S(1)}, f32[2048,1]{0,1:T(1,128)}, u32[]{:S(2)}) copy-start(f32[2048,1]{0,1:T(1,128)} %copy-done.20) | copy-start | bytes 24580
  523.7 86.3 %copy-start.27 = (f32[128]{0:T(128)S(1)}, f32[128]{0:T(128)}, u32[]{:S(2)}) copy-start(f32[128]{0:T(128)} %copy-done.25) | copy-start | bytes 1540
  523.7 86.3 %copy-start.29 = (f32[128]{0:T(128)S(1)}, f32[128]{0:T(128)}, u32[]{:S(2)}) copy-start(f32[128]{0:T(128)} %copy-done.28) | copy-start | bytes 1540
  523.7 86.3 %copy-start.30 = (f32[128]{0:T(128)S(1)}, f32[128]{0:T(128)}, u32[]{:S(2)}) copy-start(f32[128]{0:T(128)} %add_rsqrt_fusion) | copy-start | bytes 1540
  608.5 4.6 copy-start.17
  608.6 6.5 %copy-start.13 = (bf16[4,64,1280]{2,1,0:T(8,128)(2,1)S(1)}, bf16[4,64,1280]{2,1,0:T(8,128)(2,1)}, u32[]{:S(2)}) copy-start(bf16[4,64,1280]{2,1,0:T(8,128)(2,1)} %get-tuple-element.67) | copy-start | bytes 1966084
  615.1 2.7 copy-start.15
  615.2 3.6 copy-start.12
  618.9 12.1 %slice-start.3 = ((s8[10485760]{0:T(1024)(128)(4,1)}), s8[4194304]{0:T(1024)(128)(4,1)S(1)}, s32[]{:S(2)}) async-start(s8[10485760]{0:T(1024)(128)(4,1)} %bitcast.123), calls=%async_computation.3 | async-start | bytes 8388608
  619.5 11.4 %slice-start.4 = ((s8[10485760]{0:T(1024)(128)(4,1)}), s8[4194304]{0:T(1024)(128)(4,1)S(1)}, s32[]{:S(2)}) async-start(s8[10485760]{0:T(1024)(128)(4,1)} %bitcast.123), calls=%async_computation.4 | async-start | bytes 8388608
  619.5 11.4 %slice-start.5 = ((s8[10485760]{0:T(1024)(128)(4,1)}), s8[2097152]{0:T(1024)(128)(4,1)S(1)}, s32[]{:S(2)}) async-start(s8[10485760]{0:T(1024)(128)(4,1)} %bitcast.123), calls=%async_computation.5 | async-start | bytes 4194304
  619.5 19.0 %slice-start = ((s8[10485760]{0:T(1024)(128)(4,1)}), s8[4194304]{0:T(1024)(128)(4,1)S(1)}, s32[]{:S(2)}) async-start(s8[10485760]{0:T(1024)(128)(4,1)} %bitcast.87), calls=%async_computation | async-start | bytes 8388608
  619.5 19.0 %slice-start.1 = ((s8[10485760]{0:T(1024)(128)(4,1)}), s8[4194304]{0:T(1024)(128)(4,1)S(1)}, s32[]{:S(2)}) async-start(s8[10485760]{0:T(1024)(128)(4,1)} %bitcast.87), calls=%async_computation.1 | async-start | bytes 8388608
  631.0 7.6 %slice-start.2 = ((s8[10485760]{0:T(1024)(128)(4,1)}), s8[2097152]{0:T(1024)(128)(4,1)S(1)}, s32[]{:S(2)}) async-start(s8[10485760]{0:T(1024)(128)(4,1)} %bitcast.87), calls=%async_computation.2 | async-start | bytes 4194304
  631.0 7.6 %copy-start.3 = (bf16[2,4,320,384]{3,2,1,0:T(8,128)(2,1)S(1)}, bf16[2,4,320,384]{3,2,1,0:T(8,128)(2,1)}, u32[]{:S(2)}) copy-start(bf16[2,4,320,384]{3,2,1,0:T(8,128)(2,1)} %get-tuple-element.72) | copy-start | bytes 5898244
